TPU v7x, 256 devices: a whole 4x4x8 slice. The times are simulated.
256 devices in a mesh: orb: 32 (over y_lo, z, core), slab: 8 (over y_hi, x).
Axes of the slice: x: 4, y: 4 (y_hi: 2, y_lo: 2; y = y_hi * 2 + y_lo), z: 8, core: 2. Of those that a mesh axis runs over, the one named last changes fastest.
Arguments:
- orbitals: bfloat16 [512, 32768], P('orb', 'slab'), may hold values from -6 to 6
- eigenpotentials: bfloat16 [1024, 32768], P(None, 'slab'), may hold values from -0.03125 to 0.03125
- screening: float32 [1024], replicated, may hold values from 0.02 to 2
- trial_vectors: bfloat16 [16, 32768], P(None, 'orb'), may hold values from -0.001953125 to 0.001953125
- pair_index: int32 [2, 32768], P(None, 'orb'), may hold values from -1 to 511, as said below
Outputs:
- direct: float32 [16, 32768], P(None, 'orb')
Inputs may be any that keep to these rules, and one draw needn't show every extreme that they name: `pair_index`: each column is a pair (i, j) of two different orbitals, or holds -1 in both rows for an empty slot. The 1024 slots of one pair owner (one device of orb) hold its pairs; in every draw some owner has all of its slots used.
All inputs are finite; a program needn't handle non-finite values.
Results may differ from a plain program's by a relative error of at most 0.0091.
Values may be sent and summed in bfloat16 or wider, within the bound.
No kernel may reach another device: no remote copies, remote signals or barrier semaphores. Data moves between devices by JAX's collectives and lax.ppermute only.
A program may use at most 128 MiB of HBM per device.

v0:
```python
import jax
import jax.numpy as jnp
from jax import lax
from jax.sharding import PartitionSpec as P


def in_blocks(shard, dim, length):
    before, after = (shard.shape[:dim], shard.shape[dim + 1 :])
    return jnp.moveaxis(shard.reshape(*before, length, -1, *after), dim, 0)


def summed_on_arrival(shard, axis, dim):
    length = lax.axis_size(axis)
    pieces = lax.all_to_all(in_blocks(shard, dim, length), axis, 0, 0, tiled=True)
    return jnp.sum(pieces.astype(jnp.float32), axis=0)


def copy_for_each(shard, axis):
    copies = jnp.broadcast_to(shard, (lax.axis_size(axis), *shard.shape))
    return lax.all_to_all(copies, axis, split_axis=0, concat_axis=0, tiled=True)


def taken_together(shard, axis):
    everything = copy_for_each(shard, axis)
    return jnp.sum(everything, axis=0)


def split_pair(matrix_in):
    upper_part = matrix_in.astype(jnp.bfloat16)
    lower_part = (matrix_in - upper_part.astype(jnp.float32)).astype(jnp.bfloat16)
    return jnp.concatenate([upper_part, lower_part], 0)


def fold_halves(stacked):
    half_rows = stacked.shape[0] // 2
    return stacked[:half_rows] + stacked[half_rows:]


def contract_last(left_side, right_side):
    return lax.dot_general(
        left_side, right_side, (((1,), (1,)), ((), ())), preferred_element_type=jnp.float32
    )


def project_trials(trial_vectors, coef_split):
    return fold_halves(contract_last(coef_split, trial_vectors)).T


def apply_screened(scaled, coef_split):
    half_rows = coef_split.shape[0] // 2
    upper_coef = coef_split[:half_rows]
    lower_coef = coef_split[half_rows:]
    scaled_split = split_pair(scaled)
    main_part = fold_halves(jnp.dot(scaled_split, upper_coef, preferred_element_type=jnp.float32))
    scaled_rows = scaled_split[: scaled.shape[0]]
    return main_part + jnp.dot(scaled_rows, lower_coef, preferred_element_type=jnp.float32)


def shards(orbitals, eigenpotentials, screening, trial_vectors, pair_index):
    gathered = lax.all_gather(orbitals, "orb", axis=0, tiled=True)
    is_live = pair_index[0] >= 0
    first_rows = jnp.take(gathered, jnp.maximum(pair_index[0], 0), axis=0)
    second_rows = jnp.take(gathered, jnp.maximum(pair_index[1], 0), axis=0)
    density = jnp.where(is_live[:, None], first_rows * second_rows, jnp.zeros((), jnp.bfloat16))
    share_rows = eigenpotentials.shape[0] // lax.axis_size("slab")
    shares = summed_on_arrival(
        contract_last(eigenpotentials, density).astype(jnp.bfloat16), "slab", 0
    )
    share_scale = lax.dynamic_slice_in_dim(
        screening, lax.axis_index("slab") * share_rows, share_rows, 0
    )
    share_split = split_pair(shares)
    owner_terms = project_trials(trial_vectors, share_split)
    projected = taken_together(owner_terms, "orb")
    slab_terms = apply_screened(projected * share_scale[None, :], share_split)
    direct = taken_together(slab_terms, "slab")
    return direct


def solution(mesh):
    return jax.shard_map(
        shards,
        mesh=mesh,
        in_specs=(P("orb", "slab"), P(None, "slab"), P(), P(None, "orb"), P(None, "orb")),
        out_specs=P(None, "orb"),
        check_vma=False,
    )
```

profile of v0, /device:TPU:2, one launch (start us, length us, event | category | flops | bytes accessed | tf_op | source)
XLA Modules:
  0.0 206.6 jit_solution(8717730145189990898)
XLA Ops:
  6.5 0.0 copy-start
  6.5 0.0 all-gather.2.cloned.1.call-start
  6.5 0.7 all-gather.2.cloned.1.call-update
  7.3 0.7 compare_reduce_fusion
  8.0 0.8 slice_maximum_fusion.1
  8.8 69.7 %all-gather.2.cloned.1.call-done = bf16[512,4096]{1,0:T(8,128)(2,1)} async-done(((bf16[16,4096]{1,0:T(8,128)(2,1)}), bf16[512,4096]{1,0:T(8,128)(2,1)}) %all-gather.2.cloned.1.call-update) | async-done | bytes 4194320 | tf_op jit(solution)/shard_map/all_gather | solution.py:60
  78.5 17.8 %gather_fusion = bf16[1024,4096]{1,0:T(8,128)(2,1)} fusion(bf16[512,4096]{1,0:T(8,128)(2,1)} %all-gather.2.cloned.1.call-done, s32[1024]{0:T(1024)S(1)} %fusion.21), kind=kCustom, calls=%fused_computation.clone | custom fusion | bytes 16781312 | tf_op jit(solution)/shard_map/jit(_take)/gather | solution.py:62
  96.3 17.8 %gather_fusion.1 = bf16[1024,4096]{1,0:T(8,128)(2,1)} fusion(bf16[512,4096]{1,0:T(8,128)(2,1)} %all-gather.2.cloned.1.call-done, s32[1024]{0:T(1024)S(1)} %fusion.22), kind=kCustom, calls=%fused_computation.1.clone | custom fusion | bytes 16781312 | tf_op jit(solution)/shard_map/jit(_take)/gather | solution.py:63
  114.1 15.8 %fusion.9 = bf16[1024,1024]{0,1:T(8,128)(2,1)S(1)} fusion(bf16[1024,4096]{1,0:T(8,128)(2,1)} %param.8, bf16[1024,4096]{1,0:T(8,128)(2,1)} %gather_fusion.1, bf16[1024,4096]{1,0:T(8,128)(2,1)} %gather_fusion, pred[1024]{0:T(1024)(128)(4,1)S(1)} %get-tuple-element.12, pred[1024]{0:T(1024)(128)(4,1)S(1)} %get-tuple-element.13, ...), kind=kOutput, calls=%fused_computation.12 | convolution fusion | flops 8607760384 | bytes 27266048 | tf_op jit(solution)/shard_map/dot_general | solution.py:40
  129.9 34.6 %all_to_all.15 = bf16[8,128,1024]{2,1,0:T(8,128)(2,1)S(1)} all-to-all(bf16[8,128,1024]{2,1,0:T(8,128)(2,1)S(1)} %bitcast.12), channel_id=1, replica_groups=mesh['orb'=32,'slab'=8] {'slab'}, dimensions={0} | all-to-all | bytes 4194304 | tf_op jit(solution)/shard_map/all_to_all | solution.py:14
  164.5 0.4 convert_reduce_fusion
  164.9 0.1 subtract_convert_fusion
  165.0 0.0 copy-done
  165.0 0.2 fusion.12
  165.2 0.7 broadcast_in_dim.31
  166.0 6.3 %all-to-all-start.1 = ((f32[32,16,128]{2,1,0:T(8,128)}), f32[32,16,128]{2,1,0:T(8,128)S(1)}, u32[]{:S(2)}, u32[]{:S(2)}) async-start(f32[32,16,128]{2,1,0:T(8,128)} %broadcast_in_dim.31), calls=%async_computation.1 | async-start | bytes 524288 | tf_op jit(solution)/shard_map/all_to_all | solution.py:20
  172.3 0.8 dynamic_slice.3
  173.1 12.4 %all-to-all-done.1 = f32[32,16,128]{2,1,0:T(8,128)S(1)} async-done(((f32[32,16,128]{2,1,0:T(8,128)}), f32[32,16,128]{2,1,0:T(8,128)S(1)}, u32[]{:S(2)}, u32[]{:S(2)}) %all-to-all-start.1) | async-done | bytes 262176 | tf_op jit(solution)/shard_map/all_to_all | solution.py:20
  185.5 0.2 fusion.17
  185.7 0.2 convolution_add_fusion
  185.9 13.2 %all_to_all.16 = f32[8,16,1024]{2,1,0:T(8,128)S(1)} all-to-all(f32[8,16,1024]{2,1,0:T(8,128)S(1)} %broadcast_in_dim.32), channel_id=1, replica_groups=mesh['orb'=32,'slab'=8] {'slab'}, dimensions={0} | all-to-all | bytes 1048576 | tf_op jit(solution)/shard_map/all_to_all | solution.py:20
  199.1 0.7 reduce_sum.29
  (7 shorter events, 0.1 us)
Async XLA Ops:
  6.5 158.4 %copy-start = (bf16[16,1024]{1,0:T(8,128)(2,1)S(1)}, bf16[16,1024]{1,0:T(8,128)(2,1)}, u32[]{:S(2)}) copy-start(bf16[16,1024]{1,0:T(8,128)(2,1)} %param.10) | copy-start | bytes 98308
  6.5 72.0 %all-gather.2.cloned.1.call-start = ((), (), s32[]{:S(2)}) async-start(), calls=%async_computation.3 | async-start | bytes 4325376 | tf_op jit(solution)/shard_map/all_gather | solution.py:60
  166.0 19.5 %all-to-all-start.1 = ((f32[32,16,128]{2,1,0:T(8,128)}), f32[32,16,128]{2,1,0:T(8,128)S(1)}, u32[]{:S(2)}, u32[]{:S(2)}) async-start(f32[32,16,128]{2,1,0:T(8,128)} %broadcast_in_dim.31), calls=%async_computation.1 | async-start | bytes 524288 | tf_op jit(solution)/shard_map/all_to_all | solution.py:20
Sparse Core Ops, SparseCore 0:
  9.2 69.2 all-gather.1
where the time goes:
time: 207 us
  waiting for transfers between devices  82.8 us (40%)
  blocking collectives  47.8 us (23%)
  local copies, waits for them, and re-layouts  37.2 us (18%)
  matrix products  16.4 us (8%)
  between operations  13.5 us (7%)
  starting transfers between devices  6.33 us (3%)
  other arithmetic  2.65 us (1%)
    all_gather x1, waiting for transfers between devices, shards(): gathered = lax.all_gather(orbitals, 'orb', axis=0, tiled=True)  69.7 us
    all_to_all x1, blocking collectives, summed_on_arrival(): lax.all_to_all(in_blocks(shard, dim, length), axis, 0, 0, tiled=True)  34.6 us
    gather x1, local copies, waits for them, and re-layouts, shards(): first_rows = jnp.take(gathered, jnp.maximum(pair_index[0], 0), axis=0)  17.8 us
    gather x1, local copies, waits for them, and re-layouts, shards(): second_rows = jnp.take(gathered, jnp.maximum(pair_index[1], 0), axis=0)  17.8 us
    dot_general x2, matrix products, contract_last(): lax.dot_general(left_side, right_side, (((1,), (1,)), ((), ())), preferre...  16 us
    all_to_all x1, blocking collectives, copy_for_each(): return lax.all_to_all(copies, axis, split_axis=0, concat_axis=0, tiled=True)  13.2 us
    all_to_all x1, waiting for transfers between devices, copy_for_each(): return lax.all_to_all(copies, axis, split_axis=0, concat_axis=0, tiled=True)  12.4 us
    all_to_all x1, starting transfers between devices, copy_for_each(): return lax.all_to_all(copies, axis, split_axis=0, concat_axis=0, tiled=True)  6.33 us
  transfers between devices with their start and end apart: 2, of which 2 were waited for; matrix products, arithmetic and copies ran while one was open for 1% of the time, Pallas kernels for 0%

commit v1 on v0

v1 whole, which is shorter than its diff:
```python
import jax
import jax.numpy as jnp
from jax import lax
from jax.experimental import pallas as pl
from jax.experimental.pallas import tpu as pltpu
from jax.sharding import Mesh, PartitionSpec as P

AXES = ("yl", "zh", "zl", "c", "yh", "x")
SIZES = (2, 4, 2, 2, 2, 4)
ORB = ("yl", "zh", "zl", "c")
SLAB = ("yh", "x")
GROUP = ("yl", "zl", "c")
COLUMN = ("zh", "zl", "c")
PLANE = ("yl", "yh", "x")

f32 = jnp.float32
bf16 = jnp.bfloat16


def exchange(blocks, axes):
    return lax.all_to_all(blocks, axes, 0, 0, tiled=True)


def summed(blocks):
    return jnp.sum(blocks.astype(f32), axis=0)


def copies(value, count):
    return jnp.broadcast_to(value[None], (count, *value.shape))


def in_two(value):
    upper = value.astype(bf16)
    lower = (value - upper.astype(f32)).astype(bf16)
    return jnp.concatenate([upper, lower], axis=0)


def dot(left, right, dims=(((1,), (0,)), ((), ()))):
    return lax.dot_general(left, right, dims, preferred_element_type=f32)


NT = (((1,), (1,)), ((), ()))


def density_body(where_ref, phi_ref, slots_ref, pot_ref, dens_ref, proj_ref, phit_ref, fieldt_ref):
    step = pl.program_id(0)

    @pl.when(step == 0)
    def _():
        phit_ref[...] = phi_ref[...].T
        fieldt_ref[...] = jnp.zeros_like(fieldt_ref)

    slots = slots_ref[0]
    width = slots.shape[1]
    rows = lax.broadcasted_iota(jnp.int32, (256, width), 0).astype(f32)

    def picked(first):
        low = (rows == slots[first : first + 1].astype(f32)).astype(bf16)
        high = (rows == slots[first + 1 : first + 2].astype(f32)).astype(bf16)
        return dot(phit_ref[:, :256], low) + dot(phit_ref[:, 256:], high)

    dens = (picked(16) * picked(18)).astype(bf16)
    dens_ref[0] = dens
    fieldt_ref[...] += dot(dens, slots[:16], NT)

    @pl.when(step == pl.num_programs(0) - 1)
    def _():
        split = in_two(fieldt_ref[...].T)
        both = dot(split, pot_ref[...], NT)
        proj_ref[...] = (both[:16] + both[16:]).astype(bf16)


def density(where, phi, slots, eigenpotentials):
    owners, rows, width = slots.shape
    orbs, points = phi.shape
    neig = eigenpotentials.shape[0]
    return pl.pallas_call(
        density_body,
        grid_spec=pltpu.PrefetchScalarGridSpec(
            num_scalar_prefetch=1,
            grid=(owners,),
            in_specs=[
                pl.BlockSpec((orbs, points), lambda i, w: (0, 0)),
                pl.BlockSpec((1, rows, width), lambda i, w: (i, 0, 0)),
                pl.BlockSpec((neig, points), lambda i, w: (0, w[0])),
            ],
            out_specs=[
                pl.BlockSpec((1, points, width), lambda i, w: (i, 0, 0)),
                pl.BlockSpec((16, neig), lambda i, w: (0, 0)),
            ],
            scratch_shapes=[pltpu.VMEM((points, orbs), bf16), pltpu.VMEM((points, 16), f32)],
        ),
        out_shape=[
            jax.ShapeDtypeStruct((owners, points, width), bf16),
            jax.ShapeDtypeStruct((16, neig), bf16),
        ],
        name="density",
    )(where, phi, slots, eigenpotentials)


def direct_body(where_ref, screened_ref, pot_ref, dens_ref, out_ref, field_ref):
    @pl.when(pl.program_id(0) == 0)
    def _():
        half = screened_ref.shape[2]
        total = jnp.zeros(field_ref.shape, f32)
        for core in range(2):
            total += dot(in_two(screened_ref[core]), pot_ref[core * half : (core + 1) * half, :])
        field_ref[...] = total

    split = in_two(field_ref[:16] + field_ref[16:])
    both = dot(split, dens_ref[0])
    out_ref[0] = (both[:16] + both[16:]).astype(bf16)


def direct_terms(where, screened, eigenpotentials, dens):
    owners, points, width = dens.shape
    neig = eigenpotentials.shape[0]
    return pl.pallas_call(
        direct_body,
        grid_spec=pltpu.PrefetchScalarGridSpec(
            num_scalar_prefetch=1,
            grid=(owners,),
            in_specs=[
                pl.BlockSpec(screened.shape, lambda i, w: (0, 0, 0)),
                pl.BlockSpec((neig, points), lambda i, w: (0, w[0])),
                pl.BlockSpec((1, points, width), lambda i, w: (i, 0, 0)),
            ],
            out_specs=pl.BlockSpec((1, 16, width), lambda i, w: (i, 0, 0)),
            scratch_shapes=[pltpu.VMEM((32, points), f32)],
        ),
        out_shape=jax.ShapeDtypeStruct((owners, 16, width), bf16),
        name="direct_terms",
    )(where, screened, eigenpotentials, dens)


def slot_rows(trial_vectors, pair_index):
    low = jnp.where(pair_index < 256, pair_index, -1).astype(bf16)
    high = jnp.where(pair_index >= 256, pair_index - 256, -1).astype(bf16)
    rows = [trial_vectors, low[:1], high[:1], low[1:], high[1:], jnp.zeros((4, trial_vectors.shape[1]), bf16)]
    return jnp.concatenate(rows, axis=0)


def shards(orbitals, eigenpotentials, screening, trial_vectors, pair_index):
    rows, points = orbitals.shape
    part = points // 8
    slots = exchange(copies(slot_rows(trial_vectors, pair_index), 8), GROUP)
    cut = orbitals.reshape(rows, 8, part).transpose(1, 0, 2)
    cut = cut.reshape(2, 1, 2, 2, rows, part)
    sent = jnp.broadcast_to(cut, (2, 4, 2, 2, rows, part)).reshape(32, rows, part)
    phi = exchange(sent, ORB).reshape(32 * rows, part)
    where = lax.axis_index(GROUP).astype(jnp.int32).reshape(1)
    dens, projected = density(where, phi, slots, eigenpotentials)
    neig = projected.shape[1]
    halves = projected.reshape(16, 2, neig // 2).transpose(1, 0, 2)
    halves = copies(halves, 8).reshape(16, 16, neig // 2)
    column = summed(exchange(halves, COLUMN)).astype(bf16)
    half = summed(exchange(copies(column, 16), PLANE))
    scale = lax.dynamic_slice_in_dim(screening, lax.axis_index("c") * (neig // 2), neig // 2, 0)
    screened = lax.all_gather(half * scale[None, :], "c", axis=0)
    terms = direct_terms(where, screened, eigenpotentials, dens)
    owner = summed(exchange(terms, GROUP)).astype(bf16)
    return summed(exchange(copies(owner, 8), SLAB))


def solution(mesh):
    fine = Mesh(mesh.devices.reshape(SIZES), AXES)
    return jax.shard_map(
        shards,
        mesh=fine,
        in_specs=(P(ORB, SLAB), P(None, SLAB), P(), P(None, ORB), P(None, ORB)),
        out_specs=P(None, ORB),
        check_vma=False,
    )
```

time: 207 us -> 124 us (0.60)
  waiting for transfers between devices: 82.8 us -> 34.2 us
  local copies, waits for them, and re-layouts: 37.2 us -> 6.06 us
  Pallas kernels: 0 us -> 23.7 us
  matrix products: 16.4 us -> 0 us
  between operations: 13.5 us -> 0.1 us
  starting transfers between devices: 6.33 us -> 19.7 us
  blocking collectives: 47.8 us -> 37.6 us
    all_gather x1 -> x0, waiting for transfers between devices: 69.7 us -> none  [shards(): gathered = lax.all_gather(orbitals, 'orb', axis=0, tiled=True)]
    gather x2 -> x0, local copies, waits for them, and re-layouts: 35.6 us -> none  [the longest x1 17.8 us: shards(): first_rows = jnp.take(gathered, jnp.maximum(pair_index[0], 0), axis=0)]
    pallas_call x0 -> x2, Pallas kernels: none -> 23.7 us  [the longest x1 15.5 us: density(): pl.pallas_call(density_body, grid_spec=pltpu.PrefetchScalarGridSpec(num_s...]
    all_to_all x1 -> x3, waiting for transfers between devices: 12.4 us -> 34.2 us  [exchange(): return lax.all_to_all(blocks, axes, 0, 0, tiled=True)]
    dot_general x4 -> x0, matrix products: 16.4 us -> none  [the longest x2 16 us: contract_last(): lax.dot_general(left_side, right_side, (((1,), (1,)), ((), ())), preferre...]
    all_to_all x1 -> x3, starting transfers between devices: 6.33 us -> 19.7 us  [exchange(): return lax.all_to_all(blocks, axes, 0, 0, tiled=True)]
    all_to_all x2 -> x3, blocking collectives: 47.8 us -> 35.6 us  [exchange(): return lax.all_to_all(blocks, axes, 0, 0, tiled=True)]
  transfers between devices with their start and end apart: 2 -> 3, of which waited for: 2 -> 3; matrix products, arithmetic and copies ran while one was open for 1% -> 1% of each run, Pallas kernels for 0% -> 0%
where the time goes in v1:
time: 124 us; the launch traced here: 123 us
  blocking collectives  37.6 us (30%)
  waiting for transfers between devices  34.2 us (28%)
  Pallas kernels  23.7 us (19%)
  starting transfers between devices  19.7 us (16%)
  local copies, waits for them, and re-layouts  6.06 us (5%)
  other arithmetic  1.52 us (1%)
    all_to_all x3, blocking collectives, exchange(): return lax.all_to_all(blocks, axes, 0, 0, tiled=True)  35.6 us
    all_to_all x3, waiting for transfers between devices, exchange(): return lax.all_to_all(blocks, axes, 0, 0, tiled=True)  34.2 us
    all_to_all x3, starting transfers between devices, exchange(): return lax.all_to_all(blocks, axes, 0, 0, tiled=True)  19.7 us
    pallas_call x1, Pallas kernels, density(): pl.pallas_call(density_body, grid_spec=pltpu.PrefetchScalarGridSpec(num_s...  15.5 us
    pallas_call x1, Pallas kernels, direct_terms(): pl.pallas_call(direct_body, grid_spec=pltpu.PrefetchScalarGridSpec(num_sc...  8.16 us
  transfers between devices with their start and end apart: 3, of which 3 were waited for; matrix products, arithmetic and copies ran while one was open for 1% of the time, Pallas kernels for 0%

profile of v1, /device:TPU:2, one launch (start us, length us, event | category | flops | bytes accessed | tf_op | source)
XLA Modules:
  0.0 122.8 jit_solution(3034191110030214884)
XLA Ops:
  0.0 0.0 copy-start.2
  0.0 0.7 fusion
  0.8 0.8 concatenate.3
  1.6 0.8 broadcast_in_dim.44
  2.3 4.2 %all-to-all-start.1 = ((bf16[8,24,1024]{2,1,0:T(8,128)(2,1)}), bf16[8,24,1024]{2,1,0:T(8,128)(2,1)S(1)}, u32[]{:S(2)}, u32[]{:S(2)}) async-start(bf16[8,24,1024]{2,1,0:T(8,128)(2,1)} %broadcast_in_dim.44), calls=%async_computation.1 | async-start | bytes 786432 | tf_op jit(solution)/shard_map/all_to_all | solution.py:21
  6.6 0.9 copy.13
  7.6 7.3 %all-to-all-done.1.slots_ref = bf16[8,24,1024]{2,1,0:T(8,128)(2,1)S(1)} async-done(((bf16[8,24,1024]{2,1,0:T(8,128)(2,1)}), bf16[8,24,1024]{2,1,0:T(8,128)(2,1)S(1)}, u32[]{:S(2)}, u32[]{:S(2)}) %all-to-all-start.1) | async-done | bytes 393248 | tf_op jit(solution)/shard_map/all_to_all | solution.py:21
  14.9 0.0 copy-start.1
  14.9 1.0 broadcast_in_dim.20
  15.8 8.0 %all-to-all-start = ((bf16[32,16,512]{2,1,0:T(8,128)(2,1)}), bf16[32,16,512]{2,1,0:T(8,128)(2,1)S(1)}, u32[]{:S(2)}, u32[]{:S(2)}) async-start(bf16[32,16,512]{2,1,0:T(8,128)(2,1)} %bitcast.3), calls=%async_computation | async-start | bytes 1048576 | tf_op jit(solution)/shard_map/all_to_all | solution.py:21
  23.9 18.4 %all-to-all-done = bf16[32,16,512]{2,1,0:T(8,128)(2,1)S(1)} async-done(((bf16[32,16,512]{2,1,0:T(8,128)(2,1)}), bf16[32,16,512]{2,1,0:T(8,128)(2,1)S(1)}, u32[]{:S(2)}, u32[]{:S(2)}) %all-to-all-start) | async-done | bytes 524320 | tf_op jit(solution)/shard_map/all_to_all | solution.py:21
  42.3 0.0 copy-start
  42.3 0.0 copy-done.1
  42.3 0.8 copy-done
  43.1 15.5 %density.1 = (bf16[8,512,1024]{2,1,0:T(8,128)(2,1)}, bf16[16,1024]{1,0:T(8,128)(2,1)}) custom-call(s32[1]{0:T(128)} %bitcast.where_ref, bf16[512,512]{1,0:T(8,128)(2,1)} %bitcast.12, bf16[8,24,1024]{2,1,0:T(8,128)(2,1)} %copy-done.1, bf16[1024,4096]{1,0:T(8,128)(2,1)} %pot_ref.3), custom_call_target="tpu_custom_call" | custom-call | tf_op jit(solution)/shard_map/density/pallas_call | solution.py:77
  58.6 0.8 reshape.57
  59.5 13.6 %all_to_all.30 = bf16[16,16,512]{2,1,0:T(8,128)(2,1)S(1)} all-to-all(bf16[16,16,512]{2,1,0:T(8,128)(2,1)S(1)} %bitcast.13), channel_id=1, replica_groups=mesh['yl'=2,'zh'=4,'zl'=2,'c'=2,'yh'=2,'x'=4] {'zh','zl','c'}, dimensions={0} | all-to-all | bytes 524288 | tf_op jit(solution)/shard_map/all_to_all | solution.py:21
  73.1 0.8 broadcast_in_dim.46
  73.9 7.5 %all-to-all-start.3 = ((bf16[16,16,512]{2,1,0:T(8,128)(2,1)}), bf16[16,16,512]{2,1,0:T(8,128)(2,1)S(1)}, u32[]{:S(2)}, u32[]{:S(2)}) async-start(bf16[16,16,512]{2,1,0:T(8,128)(2,1)} %broadcast_in_dim.46), calls=%async_computation.3 | async-start | bytes 524288 | tf_op jit(solution)/shard_map/all_to_all | solution.py:21
  81.4 0.0 copy-done.2
  81.4 0.1 dynamic_slice.3
  81.4 8.5 %all-to-all-done.3 = bf16[16,16,512]{2,1,0:T(8,128)(2,1)S(1)} async-done(((bf16[16,16,512]{2,1,0:T(8,128)(2,1)}), bf16[16,16,512]{2,1,0:T(8,128)(2,1)S(1)}, u32[]{:S(2)}, u32[]{:S(2)}) %all-to-all-start.3) | async-done | bytes 262176 | tf_op jit(solution)/shard_map/all_to_all | solution.py:21
  90.0 2.0 %all_gather.4.screened_ref = f32[2,16,512]{2,1,0:T(8,128)} all-gather(f32[1,16,512]{2,1,0:T(8,128)S(1)} %bitcast_multiply_fusion), channel_id=1, replica_groups=mesh['yl'=2,'zh'=4,'zl'=2,'c'=2,'yh'=2,'x'=4] {'c'}, dimensions={0}, use_global_device_ids=true | all-gather | bytes 98304 | tf_op jit(solution)/shard_map/all_gather | solution.py:159
  92.0 8.2 %direct_terms.1 = bf16[8,16,1024]{2,1,0:T(8,128)(2,1)} custom-call(s32[1]{0:T(128)} %bitcast.where_ref, f32[2,16,512]{2,1,0:T(8,128)} %all_gather.4.screened_ref, bf16[1024,4096]{1,0:T(8,128)(2,1)} %pot_ref.3, bf16[8,512,1024]{2,1,0:T(8,128)(2,1)} %get-tuple-element.8.dens_ref), custom_call_target="tpu_custom_call" | custom-call | tf_op jit(solution)/shard_map/direct_terms/pallas_call | solution.py:118
  100.1 10.2 %all_to_all.31 = bf16[8,16,1024]{2,1,0:T(8,128)(2,1)S(1)} all-to-all(bf16[8,16,1024]{2,1,0:T(8,128)(2,1)} %direct_terms.1), channel_id=1, replica_groups=mesh['yl'=2,'zh'=4,'zl'=2,'c'=2,'yh'=2,'x'=4] {'yl','zl','c'}, dimensions={0} | all-to-all | bytes 524288 | tf_op jit(solution)/shard_map/all_to_all | solution.py:21
  110.4 11.7 %all_to_all.32 = bf16[8,16,1024]{2,1,0:T(8,128)(2,1)S(1)} all-to-all(bf16[8,16,1024]{2,1,0:T(8,128)(2,1)S(1)} %broadcast_in_dim.47), channel_id=1, replica_groups=mesh['yl'=2,'zh'=4,'zl'=2,'c'=2,'yh'=2,'x'=4] {'yh','x'}, dimensions={0} | all-to-all | bytes 524288 | tf_op jit(solution)/shard_map/all_to_all | solution.py:21
  122.2 0.7 convert_reduce_fusion
  (10 shorter events, 0.2 us)
Async XLA Ops:
  0.0 81.4 %copy-start.2 = (f32[1024]{0:T(1024)S(1)}, f32[1024]{0:T(1024)}, u32[]{:S(2)}) copy-start(f32[1024]{0:T(1024)} %param.7) | copy-start | bytes 12292
  2.3 12.5 %all-to-all-start.1 = ((bf16[8,24,1024]{2,1,0:T(8,128)(2,1)}), bf16[8,24,1024]{2,1,0:T(8,128)(2,1)S(1)}, u32[]{:S(2)}, u32[]{:S(2)}) async-start(bf16[8,24,1024]{2,1,0:T(8,128)(2,1)} %broadcast_in_dim.44), calls=%async_computation.1 | async-start | bytes 786432 | tf_op jit(solution)/shard_map/all_to_all | solution.py:21
  14.9 27.4 %copy-start.1 = (bf16[8,24,1024]{2,1,0:T(8,128)(2,1)}, bf16[8,24,1024]{2,1,0:T(8,128)(2,1)S(1)}, u32[]{:S(2)}) copy-start(bf16[8,24,1024]{2,1,0:T(8,128)(2,1)S(1)} %all-to-all-done.1.slots_ref) | copy-start | bytes 1179652
  15.8 26.5 %all-to-all-start = ((bf16[32,16,512]{2,1,0:T(8,128)(2,1)}), bf16[32,16,512]{2,1,0:T(8,128)(2,1)S(1)}, u32[]{:S(2)}, u32[]{:S(2)}) async-start(bf16[32,16,512]{2,1,0:T(8,128)(2,1)} %bitcast.3), calls=%async_computation | async-start | bytes 1048576 | tf_op jit(solution)/shard_map/all_to_all | solution.py:21
  42.3 0.8 copy-start
  73.9 16.0 %all-to-all-start.3 = ((bf16[16,16,512]{2,1,0:T(8,128)(2,1)}), bf16[16,16,512]{2,1,0:T(8,128)(2,1)S(1)}, u32[]{:S(2)}, u32[]{:S(2)}) async-start(bf16[16,16,512]{2,1,0:T(8,128)(2,1)} %broadcast_in_dim.46), calls=%async_computation.3 | async-start | bytes 524288 | tf_op jit(solution)/shard_map/all_to_all | solution.py:21

commit v2 on v1

v2 whole, which is shorter than its diff:
```python
import jax
import jax.numpy as jnp
from jax import lax
from jax.experimental import pallas as pl
from jax.experimental.pallas import tpu as pltpu
from jax.sharding import Mesh, PartitionSpec as P

AXES = ("yl", "zh", "zl", "c", "yh", "x")
SIZES = (2, 4, 2, 2, 2, 4)
ORB = ("yl", "zh", "zl", "c")
SLAB = ("yh", "x")
GROUP = ("yl", "zl", "c")
COLUMN = ("zh", "zl", "c")
PLANE = ("yl", "yh", "x")

NB = 16
BLOCK = 128
ROWS = 24
TAKE = 4

f32 = jnp.float32
bf16 = jnp.bfloat16
NT = (((1,), (1,)), ((), ()))
LIMIT = 30 * 1024 * 1024


def exchange(blocks, axes):
    return lax.all_to_all(blocks, axes, 0, 0, tiled=True)


def summed(blocks):
    return jnp.sum(blocks.astype(f32), axis=0)


def copies(value, count):
    return jnp.broadcast_to(value[None], (count, *value.shape))


def in_two(value):
    upper = value.astype(bf16)
    lower = (value - upper.astype(f32)).astype(bf16)
    return jnp.concatenate([upper, lower], axis=0)


def folded(both):
    return both[:NB] + both[NB:]


def dot(left, right, dims=(((1,), (0,)), ((), ()))):
    return lax.dot_general(left, right, dims, preferred_element_type=f32)


def vmem(*values):
    return [pltpu.with_memory_space_constraint(v, pltpu.VMEM) for v in values]


def hbm(*values):
    return [pltpu.with_memory_space_constraint(v, pltpu.HBM) for v in values]


IN_VMEM = pl.BlockSpec(memory_space=pltpu.VMEM)
IN_SMEM = pl.BlockSpec(memory_space=pltpu.SMEM)
IN_HBM = pl.BlockSpec(memory_space=pltpu.HBM)


def prepare_body(orbitals_ref, trial_ref, pair_ref, sent_ref, slots_ref, trials_ref, pairs_ref, sems, in_sems):
    part = sent_ref.shape[2]
    trials = pltpu.make_async_copy(trial_ref, trials_ref, in_sems.at[0])
    pairs = pltpu.make_async_copy(pair_ref, pairs_ref, in_sems.at[1])
    trials.start()
    pairs.start()
    cuts = []
    for group in range(8):
        piece = orbitals_ref.at[:, group * part : (group + 1) * part]
        for layer in range(4):
            to = (group // 4) * 16 + layer * 4 + group % 4
            cuts.append(pltpu.make_async_copy(piece, sent_ref.at[to], sems.at[to]))
    for cut in cuts:
        cut.start()
    pairs.wait()
    index = pairs_ref[...]
    low = jnp.where(index < 256, index, -1)
    high = jnp.where(index >= 256, index - 256, -1)
    where = jnp.concatenate([low, high, low, high], axis=0).astype(f32).astype(bf16)
    trials.wait()
    for block in range(slots_ref.shape[1]):
        lanes = slice(block * BLOCK, (block + 1) * BLOCK)
        for group in range(8):
            slots_ref[group, block, :NB, :] = trials_ref[:, lanes]
            slots_ref[group, block, NB:ROWS, :] = where[:, lanes]
    for cut in cuts:
        cut.wait()


def prepare(orbitals, trial_vectors, pair_index):
    rows, points = orbitals.shape
    blocks = trial_vectors.shape[1] // BLOCK
    return pl.pallas_call(
        prepare_body,
        in_specs=[IN_HBM] * 3,
        out_specs=[IN_VMEM] * 2,
        out_shape=[
            pltpu.VMEM((32, rows, points // 8), bf16),
            pltpu.VMEM((8, blocks, ROWS, BLOCK), bf16),
        ],
        scratch_shapes=[
            pltpu.VMEM(trial_vectors.shape, bf16),
            pltpu.VMEM(pair_index.shape, jnp.int32),
            pltpu.SemaphoreType.DMA((32,)),
            pltpu.SemaphoreType.DMA((2,)),
        ],
        compiler_params=pltpu.CompilerParams(vmem_limit_bytes=LIMIT),
        name="prepare",
    )(*hbm(orbitals, trial_vectors, pair_index))


def density_body(
    group_ref,
    phi_ref,
    slots_ref,
    all_pot_ref,
    kept_ref,
    pot_ref,
    halves_ref,
    list_ref,
    phit_ref,
    fieldt_ref,
    dens_ref,
    sem,
    sems,
):
    points = phit_ref.shape[0]
    fetch = pltpu.make_async_copy(all_pot_ref.at[:, pl.ds(group_ref[0] * points, points)], pot_ref, sem)
    fetch.start()
    phit_ref[...] = phi_ref[...].T
    fieldt_ref[...] = jnp.zeros_like(fieldt_ref)
    blocks = slots_ref.shape[0]
    count = jnp.int32(0)
    for block in range(blocks):
        most = jnp.max(slots_ref[block, NB:ROWS, :].astype(f32))
        list_ref[1 + count] = jnp.int32(block)
        count += (most >= 0.0).astype(jnp.int32)
    list_ref[0] = count
    for extra in range(TAKE):
        list_ref[1 + count + extra] = jnp.int32(0)

    rows = lax.broadcasted_iota(jnp.int32, (256, TAKE * BLOCK), 0).astype(f32)

    def step(turn, unused):
        pieces, trials = [], []
        for k in range(TAKE):
            at = turn * TAKE + k
            block = list_ref[1 + at]
            where = slots_ref[block, NB:ROWS, :].astype(f32)
            pieces.append(jnp.where(at < count, where, -1.0))
            trials.append(slots_ref[block, :NB, :])
        where = jnp.concatenate(pieces, axis=1)
        trial = jnp.concatenate(trials, axis=1)

        def picked(row):
            low = (rows == where[row : row + 1]).astype(bf16)
            high = (rows == where[row + 2 : row + 3]).astype(bf16)
            return dot(phit_ref[...], jnp.concatenate([low, high], axis=0))

        dens = (picked(0) * picked(1)).astype(bf16)
        dens_ref[turn] = dens
        pltpu.make_async_copy(dens_ref.at[turn], kept_ref.at[turn], sems.at[turn]).start()
        fieldt_ref[...] += dot(dens, trial, NT)
        return unused

    turns = (count + TAKE - 1) // TAKE
    lax.fori_loop(0, turns, step, 0)
    fetch.wait()
    proj = folded(dot(in_two(fieldt_ref[...].T), pot_ref[...], NT)).astype(bf16)
    half = halves_ref.shape[2]
    for core in range(2):
        for layer in range(8):
            halves_ref[layer * 2 + core] = proj[:, core * half : (core + 1) * half]

    def kept(turn, unused):
        pltpu.make_async_copy(dens_ref.at[turn], kept_ref.at[turn], sems.at[turn]).wait()
        return unused

    lax.fori_loop(0, turns, kept, 0)


def density(group, phi, slots, eigenpotentials):
    blocks = slots.shape[0]
    orbs, points = phi.shape
    neig = eigenpotentials.shape[0]
    return pl.pallas_call(
        density_body,
        in_specs=[IN_SMEM, IN_VMEM, IN_VMEM, IN_HBM],
        out_specs=[IN_HBM, IN_VMEM, IN_VMEM, IN_SMEM],
        out_shape=[
            pltpu.HBM((blocks // TAKE, points, TAKE * BLOCK), bf16),
            pltpu.VMEM((neig, points), bf16),
            pltpu.VMEM((16, NB, neig // 2), bf16),
            jax.ShapeDtypeStruct((1 + blocks + TAKE,), jnp.int32),
        ],
        scratch_shapes=[
            pltpu.VMEM((points, orbs), bf16),
            pltpu.VMEM((points, NB), f32),
            pltpu.VMEM((blocks // TAKE, points, TAKE * BLOCK), bf16),
            pltpu.SemaphoreType.DMA(()),
            pltpu.SemaphoreType.DMA((blocks // TAKE,)),
        ],
        compiler_params=pltpu.CompilerParams(vmem_limit_bytes=LIMIT),
        name="density",
    )(group, *vmem(phi, slots), *hbm(eigenpotentials))


def direct_body(core_ref, list_ref, mine_ref, other_ref, screening_ref, pot_ref, kept_ref, out_ref, split_ref, dens_ref, sems):
    count = list_ref[0]
    turns = (count + TAKE - 1) // TAKE

    def fetch(turn, unused):
        pltpu.make_async_copy(kept_ref.at[turn], dens_ref.at[turn], sems.at[turn]).start()
        return unused

    lax.fori_loop(0, turns, fetch, 0)
    half = mine_ref.shape[1]
    total = jnp.zeros((NB, pot_ref.shape[1]), f32)
    for ref, core in ((mine_ref, core_ref[0]), (other_ref, 1 - core_ref[0])):
        screened = ref[...] * screening_ref[pl.ds(core, 1), :]
        rows = pot_ref[pl.ds(pl.multiple_of(core * half, half), half), :]
        total += folded(dot(in_two(screened), rows))
    split_ref[...] = in_two(total)
    out_ref[...] = jnp.zeros_like(out_ref)

    def step(turn, unused):
        pltpu.make_async_copy(kept_ref.at[turn], dens_ref.at[turn], sems.at[turn]).wait()
        terms = folded(dot(split_ref[...], dens_ref[turn])).astype(bf16)
        for k in range(TAKE):
            at = turn * TAKE + k

            @pl.when(at < count)
            def _():
                out_ref[list_ref[1 + at]] = terms[:, k * BLOCK : (k + 1) * BLOCK]

        return unused

    lax.fori_loop(0, turns, step, 0)


def direct_terms(core, live, mine, other, screening, pot, dens):
    blocks = dens.shape[0] * TAKE
    return pl.pallas_call(
        direct_body,
        in_specs=[IN_SMEM, IN_SMEM] + [IN_VMEM] * 4 + [IN_HBM],
        out_specs=IN_VMEM,
        out_shape=pltpu.VMEM((blocks, NB, BLOCK), bf16),
        scratch_shapes=[
            pltpu.VMEM((2 * NB, pot.shape[1]), bf16),
            pltpu.VMEM(dens.shape, bf16),
            pltpu.SemaphoreType.DMA((dens.shape[0],)),
        ],
        compiler_params=pltpu.CompilerParams(vmem_limit_bytes=LIMIT),
        name="direct_terms",
    )(core, live, *vmem(mine, other, screening, pot), *hbm(dens))


def shards(orbitals, eigenpotentials, screening, trial_vectors, pair_index):
    neig = eigenpotentials.shape[0]
    group = lax.axis_index(GROUP).astype(jnp.int32).reshape(1)
    core = lax.axis_index("c").astype(jnp.int32).reshape(1)
    scales = screening.reshape(2, neig // 2)
    sent, slots = prepare(orbitals, trial_vectors, pair_index)
    sent, slots, group, core, scales = lax.optimization_barrier((sent, slots, group, core, scales))
    slots = exchange(slots, GROUP)
    slots, sent = lax.optimization_barrier((slots, sent))
    phi = exchange(sent, ORB)
    phi = phi.reshape(32 * phi.shape[1], phi.shape[2])
    slots = slots.reshape(-1, ROWS, BLOCK)
    dens, pot, halves, live = density(group, phi, slots, eigenpotentials)
    column = summed(exchange(halves, COLUMN)).astype(bf16)
    mine = summed(exchange(copies(column, 16), PLANE))
    other = lax.ppermute(mine, "c", [(0, 1), (1, 0)])
    terms = direct_terms(core, live, mine, other, scales, pot, dens)
    terms = exchange(terms.reshape(8, -1, NB, BLOCK), GROUP)
    owner = summed(terms).astype(bf16)
    direct = summed(exchange(copies(owner, 8), SLAB))
    return direct.transpose(1, 0, 2).reshape(NB, -1)


def solution(mesh):
    fine = Mesh(mesh.devices.reshape(SIZES), AXES)
    return jax.shard_map(
        shards,
        mesh=fine,
        in_specs=(P(ORB, SLAB), P(None, SLAB), P(), P(None, ORB), P(None, ORB)),
        out_specs=P(None, ORB),
        check_vma=False,
    )
```

time: 124 us -> 105 us (0.85)
  blocking collectives: 37.6 us -> 89.2 us
  waiting for transfers between devices: 34.2 us -> 1.19 us
  starting transfers between devices: 19.7 us -> 0.09 us
  Pallas kernels: 23.7 us -> 12.3 us
  local copies, waits for them, and re-layouts: 6.06 us -> 1.39 us
  other arithmetic: 1.52 us -> 0.16 us
    all_to_all x3 -> x6, blocking collectives: 35.6 us -> 89.2 us  [exchange(): return lax.all_to_all(blocks, axes, 0, 0, tiled=True)]
    all_to_all x3 -> x0, waiting for transfers between devices: 34.2 us -> none  [exchange(): return lax.all_to_all(blocks, axes, 0, 0, tiled=True)]
    all_to_all x3 -> x0, starting transfers between devices: 19.7 us -> none  [exchange(): return lax.all_to_all(blocks, axes, 0, 0, tiled=True)]
    pallas_call x2 -> x3, Pallas kernels: 23.7 us -> 12.3 us  [the longest x1 7.72 us: density(): pl.pallas_call(density_body, in_specs=[IN_SMEM, IN_VMEM, IN_VMEM, IN_HBM]...]
    all_gather x1 -> x0, blocking collectives: 1.99 us -> none  [shards(): screened = lax.all_gather(half * scale[None, :], 'c', axis=0)]
    unnamed x7 -> x0, local copies, waits for them, and re-layouts: 1.79 us -> none
    broadcast_in_dim x4 -> x2, local copies, waits for them, and re-layouts: 1.58 us -> 0.06 us  [copies(): return jnp.broadcast_to(value[None], (count, *value.shape))]
  transfers between devices with their start and end apart: 3 -> 1, of which waited for: 3 -> 1; matrix products, arithmetic and copies ran while one was open for 1% -> 0% of each run, Pallas kernels for 0% -> 0%
where the time goes in v2:
time: 105 us; the launch traced here: 104 us
  blocking collectives  89.2 us (85%)
  Pallas kernels  12.3 us (12%)
  local copies, waits for them, and re-layouts  1.39 us (1%)
  waiting for transfers between devices  1.19 us (1%)
    all_to_all x6, blocking collectives, exchange(): return lax.all_to_all(blocks, axes, 0, 0, tiled=True)  89.2 us
    pallas_call x1, Pallas kernels, density(): pl.pallas_call(density_body, in_specs=[IN_SMEM, IN_VMEM, IN_VMEM, IN_HBM]...  7.72 us
    pallas_call x1, Pallas kernels, direct_terms(): pl.pallas_call(direct_body, in_specs=[IN_SMEM, IN_SMEM] + [IN_VMEM] * 4 +...  3.15 us
  transfers between devices with their start and end apart: 1, of which 1 were waited for; matrix products, arithmetic and copies ran while one was open for 0% of the time, Pallas kernels for 0%

profile of v2, /device:TPU:2, one launch (start us, length us, event | category | flops | bytes accessed | tf_op | source)
XLA Modules:
  0.0 104.5 jit_solution(3028060287189061930)
XLA Ops:
  0.0 0.7 reshape.25.screening_ref
  0.7 1.5 %prepare.1 = (bf16[32,16,512]{2,1,0:T(8,128)(2,1)S(1)}, bf16[8,8,24,128]{3,2,1,0:T(8,128)(2,1)S(1)}) custom-call(bf16[16,4096]{1,0:T(8,128)(2,1)} %orbitals_ref.1, bf16[16,1024]{1,0:T(8,128)(2,1)} %trial_ref.1, s32[2,1024]{1,0:T(2,128)} %pair_ref.1), custom_call_target="tpu_custom_call" | custom-call | tf_op jit(solution)/shard_map/prepare/pallas_call | solution.py:98
  2.2 12.3 %all_to_all.30 = bf16[8,8,24,128]{3,2,1,0:T(8,128)(2,1)S(1)} all-to-all(bf16[8,8,24,128]{3,2,1,0:T(8,128)(2,1)S(1)} %get-tuple-element.22), channel_id=1, replica_groups=mesh['yl'=2,'zh'=4,'zl'=2,'c'=2,'yh'=2,'x'=4] {'yl','zl','c'}, dimensions={0} | all-to-all | bytes 786432 | tf_op jit(solution)/shard_map/all_to_all | solution.py:28
  14.5 26.2 %all_to_all.31 = bf16[32,16,512]{2,1,0:T(8,128)(2,1)S(1)} all-to-all(bf16[32,16,512]{2,1,0:T(8,128)(2,1)S(1)} %get-tuple-element.24), channel_id=1, replica_groups=mesh['yl'=2,'zh'=4,'zl'=2,'c'=2,'yh'=2,'x'=4] {'yl','zh','zl','c'}, dimensions={0} | all-to-all | bytes 1048576 | tf_op jit(solution)/shard_map/all_to_all | solution.py:28
  40.6 7.7 %density.1 = (bf16[16,512,512]{2,1,0:T(8,128)(2,1)}, bf16[1024,512]{1,0:T(8,128)(2,1)S(1)}, bf16[16,16,512]{2,1,0:T(8,128)(2,1)S(1)}, s32[69]{0:T(128)S(1)}) custom-call(s32[1]{0:T(128)} %bitcast.group_ref, bf16[512,512]{1,0:T(8,128)(2,1)S(1)} %bitcast.11, bf16[64,24,128]{2,1,0:T(8,128)(2,1)S(1)} %bitcast.12, bf16[1024,4096]{1,0:T(8,128)(2,1)} %all_pot_ref.1), custom_call_target="tpu_custom_call" | custom-call | tf_op jit(solution)/shard_map/density/pallas_call | solution.py:191
  48.4 14.4 %all_to_all.32 = bf16[16,16,512]{2,1,0:T(8,128)(2,1)S(1)} all-to-all(bf16[16,16,512]{2,1,0:T(8,128)(2,1)S(1)} %get-tuple-element.27), channel_id=1, replica_groups=mesh['yl'=2,'zh'=4,'zl'=2,'c'=2,'yh'=2,'x'=4] {'zh','zl','c'}, dimensions={0} | all-to-all | bytes 524288 | tf_op jit(solution)/shard_map/all_to_all | solution.py:28
  62.9 15.3 %all_to_all.33 = bf16[16,16,512]{2,1,0:T(8,128)(2,1)S(1)} all-to-all(bf16[16,16,512]{2,1,0:T(8,128)(2,1)S(1)} %broadcast_in_dim.4), channel_id=1, replica_groups=mesh['yl'=2,'zh'=4,'zl'=2,'c'=2,'yh'=2,'x'=4] {'yl','yh','x'}, dimensions={0} | all-to-all | bytes 524288 | tf_op jit(solution)/shard_map/all_to_all | solution.py:28
  78.2 0.1 collective-permute-start
  78.3 1.2 %collective-permute-done.other_ref = f32[16,512]{1,0:T(8,128)S(1)} collective-permute-done((f32[16,512]{1,0:T(8,128)S(1)}, f32[16,512]{1,0:T(8,128)S(1)}, u32[]{:S(2)}, u32[]{:S(2)}) %collective-permute-start) | collective-permute-done | bytes 32800 | tf_op jit(solution)/shard_map/ppermute | solution.py:278
  79.5 3.2 %direct_terms.1 = bf16[64,16,128]{2,1,0:T(8,128)(2,1)S(1)} custom-call(s32[1]{0:T(128)} %bitcast.1.core_ref, s32[69]{0:T(128)S(1)} %get-tuple-element.26.list_ref, f32[16,512]{1,0:T(8,128)S(1)} %convert_reduce_fusion.1.mine_ref, f32[16,512]{1,0:T(8,128)S(1)} %collective-permute-done.other_ref, f32[2,512]{1,0:T(2,128)S(1)} %reshape.25.screening_ref, ...), custom_call_target="tpu_custom_call" | custom-call | tf_op jit(solution)/shard_map/direct_terms/pallas_call | solution.py:248
  82.6 9.3 %all_to_all.34 = bf16[8,8,16,128]{3,2,1,0:T(8,128)(2,1)S(1)} all-to-all(bf16[8,8,16,128]{3,2,1,0:T(8,128)(2,1)S(1)} %bitcast.13), channel_id=1, replica_groups=mesh['yl'=2,'zh'=4,'zl'=2,'c'=2,'yh'=2,'x'=4] {'yl','zl','c'}, dimensions={0} | all-to-all | bytes 524288 | tf_op jit(solution)/shard_map/all_to_all | solution.py:28
  92.0 11.7 %all_to_all.35 = bf16[8,8,16,128]{3,2,1,0:T(8,128)(2,1)S(1)} all-to-all(bf16[8,8,16,128]{3,2,1,0:T(8,128)(2,1)S(1)} %broadcast_in_dim.5), channel_id=1, replica_groups=mesh['yl'=2,'zh'=4,'zl'=2,'c'=2,'yh'=2,'x'=4] {'yh','x'}, dimensions={0} | all-to-all | bytes 524288 | tf_op jit(solution)/shard_map/all_to_all | solution.py:28
  103.8 0.6 copy_bitcast_fusion
  (6 shorter events, 0.2 us)
Async XLA Ops:
  78.2 1.3 %collective-permute-start = (f32[16,512]{1,0:T(8,128)S(1)}, f32[16,512]{1,0:T(8,128)S(1)}, u32[]{:S(2)}, u32[]{:S(2)}) collective-permute-start(f32[16,512]{1,0:T(8,128)S(1)} %convert_reduce_fusion.1.mine_ref), channel_id=1, source_target_pairs={{0,8},{8,0},{1,9},{9,1},{2,10},{10,2},{3,11},{11,3},{4,12},{12,4},... | collective-permute-start | bytes 98312 | tf_op jit(solution)/shard_map/ppermute | solution.py:278

commit v3 on v2

--- a/solution.py
+++ b/solution.py
@@ -5,11 +5,13 @@
 from jax.experimental.pallas import tpu as pltpu
 from jax.sharding import Mesh, PartitionSpec as P
 
+
 AXES = ("yl", "zh", "zl", "c", "yh", "x")
 SIZES = (2, 4, 2, 2, 2, 4)
 ORB = ("yl", "zh", "zl", "c")
 SLAB = ("yh", "x")
-GROUP = ("yl", "zl", "c")
+GROUP = ("yl", "zl")
+SOURCES = ("yl", "zh", "zl")
 COLUMN = ("zh", "zl", "c")
 PLANE = ("yl", "yh", "x")
 
@@ -67,27 +69,27 @@
     part = sent_ref.shape[2]
     trials = pltpu.make_async_copy(trial_ref, trials_ref, in_sems.at[0])
     pairs = pltpu.make_async_copy(pair_ref, pairs_ref, in_sems.at[1])
+    pairs.start()
     trials.start()
-    pairs.start()
     cuts = []
-    for group in range(8):
+    for to in range(sent_ref.shape[0]):
+        group = (to // 8) * 2 + to % 2
         piece = orbitals_ref.at[:, group * part : (group + 1) * part]
-        for layer in range(4):
-            to = (group // 4) * 16 + layer * 4 + group % 4
-            cuts.append(pltpu.make_async_copy(piece, sent_ref.at[to], sems.at[to]))
+        cuts.append(pltpu.make_async_copy(piece, sent_ref.at[to], sems.at[to]))
     for cut in cuts:
         cut.start()
     pairs.wait()
     index = pairs_ref[...]
-    low = jnp.where(index < 256, index, -1)
-    high = jnp.where(index >= 256, index - 256, -1)
-    where = jnp.concatenate([low, high, low, high], axis=0).astype(f32).astype(bf16)
+    place = lax.shift_right_logical(index, 5) * 16 + (index & 15)
+    odd = (index & 16) > 0
+    even_core = jnp.where((index >= 0) & ~odd, place, -1)
+    odd_core = jnp.where((index >= 0) & odd, place, -1)
+    where = jnp.concatenate([even_core, odd_core, even_core, odd_core], axis=0).astype(f32).astype(bf16)
     trials.wait()
-    for block in range(slots_ref.shape[1]):
+    for block in range(slots_ref.shape[0]):
         lanes = slice(block * BLOCK, (block + 1) * BLOCK)
-        for group in range(8):
-            slots_ref[group, block, :NB, :] = trials_ref[:, lanes]
-            slots_ref[group, block, NB:ROWS, :] = where[:, lanes]
+        slots_ref[block, :NB, :] = trials_ref[:, lanes]
+        slots_ref[block, NB:ROWS, :] = where[:, lanes]
     for cut in cuts:
         cut.wait()
 
@@ -100,13 +102,13 @@
         in_specs=[IN_HBM] * 3,
         out_specs=[IN_VMEM] * 2,
         out_shape=[
-            pltpu.VMEM((32, rows, points // 8), bf16),
-            pltpu.VMEM((8, blocks, ROWS, BLOCK), bf16),
+            pltpu.VMEM((16, rows, points // 4), bf16),
+            pltpu.VMEM((blocks, ROWS, BLOCK), bf16),
         ],
         scratch_shapes=[
             pltpu.VMEM(trial_vectors.shape, bf16),
             pltpu.VMEM(pair_index.shape, jnp.int32),
-            pltpu.SemaphoreType.DMA((32,)),
+            pltpu.SemaphoreType.DMA((16,)),
             pltpu.SemaphoreType.DMA((2,)),
         ],
         compiler_params=pltpu.CompilerParams(vmem_limit_bytes=LIMIT),
@@ -116,13 +118,19 @@
 
 def density_body(
     group_ref,
-    phi_ref,
-    slots_ref,
+    core_ref,
+    mine_ref,
+    other_ref,
+    slots0_ref,
+    slots1_ref,
+    slots2_ref,
+    slots3_ref,
     all_pot_ref,
     kept_ref,
     pot_ref,
     halves_ref,
     list_ref,
+    slots_ref,
     phit_ref,
     fieldt_ref,
     dens_ref,
@@ -130,9 +138,20 @@
     sems,
 ):
     points = phit_ref.shape[0]
-    fetch = pltpu.make_async_copy(all_pot_ref.at[:, pl.ds(group_ref[0] * points, points)], pot_ref, sem)
+    group = group_ref[0]
+    fetch = pltpu.make_async_copy(all_pot_ref.at[:, pl.ds(group * points, points)], pot_ref, sem)
     fetch.start()
-    phit_ref[...] = phi_ref[...].T
+    each = slots0_ref.shape[0]
+    for k, ref in enumerate((slots0_ref, slots1_ref, slots2_ref, slots3_ref)):
+        slots_ref[pl.ds((group ^ k) * each, each)] = ref[...]
+    half = mine_ref.shape[0]
+    for core in range(2):
+
+        @pl.when(core_ref[0] == core)
+        def _():
+            phit_ref[:, core * half : (core + 1) * half] = mine_ref[...].T
+            phit_ref[:, (1 - core) * half : (2 - core) * half] = other_ref[...].T
+
     fieldt_ref[...] = jnp.zeros_like(fieldt_ref)
     blocks = slots_ref.shape[0]
     count = jnp.int32(0)
@@ -144,7 +163,7 @@
     for extra in range(TAKE):
         list_ref[1 + count + extra] = jnp.int32(0)
 
-    rows = lax.broadcasted_iota(jnp.int32, (256, TAKE * BLOCK), 0).astype(f32)
+    rows = lax.broadcasted_iota(jnp.int32, (half, TAKE * BLOCK), 0).astype(f32)
 
     def step(turn, unused):
         pieces, trials = [], []
@@ -158,9 +177,9 @@
         trial = jnp.concatenate(trials, axis=1)
 
         def picked(row):
-            low = (rows == where[row : row + 1]).astype(bf16)
-            high = (rows == where[row + 2 : row + 3]).astype(bf16)
-            return dot(phit_ref[...], jnp.concatenate([low, high], axis=0))
+            even_core = (rows == where[row : row + 1]).astype(bf16)
+            odd_core = (rows == where[row + 2 : row + 3]).astype(bf16)
+            return dot(phit_ref[...], jnp.concatenate([even_core, odd_core], axis=0))
 
         dens = (picked(0) * picked(1)).astype(bf16)
         dens_ref[turn] = dens
@@ -171,11 +190,15 @@
     turns = (count + TAKE - 1) // TAKE
     lax.fori_loop(0, turns, step, 0)
     fetch.wait()
-    proj = folded(dot(in_two(fieldt_ref[...].T), pot_ref[...], NT)).astype(bf16)
-    half = halves_ref.shape[2]
+    fieldt = fieldt_ref[...]
+    upper = fieldt.astype(bf16)
+    lower = (fieldt - upper.astype(f32)).astype(bf16)
+    projt = dot(pot_ref[...], upper) + dot(pot_ref[...], lower)
+    proj = projt.T.astype(bf16)
+    width = halves_ref.shape[2]
     for core in range(2):
         for layer in range(8):
-            halves_ref[layer * 2 + core] = proj[:, core * half : (core + 1) * half]
+            halves_ref[layer * 2 + core] = proj[:, core * width : (core + 1) * width]
 
     def kept(turn, unused):
         pltpu.make_async_copy(dens_ref.at[turn], kept_ref.at[turn], sems.at[turn]).wait()
@@ -184,30 +207,32 @@
     lax.fori_loop(0, turns, kept, 0)
 
 
-def density(group, phi, slots, eigenpotentials):
-    blocks = slots.shape[0]
-    orbs, points = phi.shape
+def density(group, core, mine, other, slots, eigenpotentials):
+    blocks = slots[0].shape[0] * len(slots)
+    half, points = mine.shape
     neig = eigenpotentials.shape[0]
+    turns = blocks // TAKE
     return pl.pallas_call(
         density_body,
-        in_specs=[IN_SMEM, IN_VMEM, IN_VMEM, IN_HBM],
+        in_specs=[IN_SMEM] * 2 + [IN_VMEM] * 6 + [IN_HBM],
         out_specs=[IN_HBM, IN_VMEM, IN_VMEM, IN_SMEM],
         out_shape=[
-            pltpu.HBM((blocks // TAKE, points, TAKE * BLOCK), bf16),
+            pltpu.HBM((turns, points, TAKE * BLOCK), bf16),
             pltpu.VMEM((neig, points), bf16),
             pltpu.VMEM((16, NB, neig // 2), bf16),
             jax.ShapeDtypeStruct((1 + blocks + TAKE,), jnp.int32),
         ],
         scratch_shapes=[
-            pltpu.VMEM((points, orbs), bf16),
+            pltpu.VMEM((blocks, ROWS, BLOCK), bf16),
+            pltpu.VMEM((points, 2 * half), bf16),
             pltpu.VMEM((points, NB), f32),
-            pltpu.VMEM((blocks // TAKE, points, TAKE * BLOCK), bf16),
+            pltpu.VMEM((turns, points, TAKE * BLOCK), bf16),
             pltpu.SemaphoreType.DMA(()),
-            pltpu.SemaphoreType.DMA((blocks // TAKE,)),
+            pltpu.SemaphoreType.DMA((turns,)),
         ],
         compiler_params=pltpu.CompilerParams(vmem_limit_bytes=LIMIT),
         name="density",
-    )(group, *vmem(phi, slots), *hbm(eigenpotentials))
+    )(group, core, *vmem(mine, other, *slots), *hbm(eigenpotentials))
 
 
 def direct_body(core_ref, list_ref, mine_ref, other_ref, screening_ref, pot_ref, kept_ref, out_ref, split_ref, dens_ref, sems):
@@ -222,7 +247,8 @@
     half = mine_ref.shape[1]
     total = jnp.zeros((NB, pot_ref.shape[1]), f32)
     for ref, core in ((mine_ref, core_ref[0]), (other_ref, 1 - core_ref[0])):
-        screened = ref[...] * screening_ref[pl.ds(core, 1), :]
+        scales = jnp.where(core == 0, screening_ref[:, :half], screening_ref[:, half:])
+        screened = ref[...] * scales
         rows = pot_ref[pl.ds(pl.multiple_of(core * half, half), half), :]
         total += folded(dot(in_two(screened), rows))
     split_ref[...] = in_two(total)
@@ -261,23 +287,22 @@
 
 
 def shards(orbitals, eigenpotentials, screening, trial_vectors, pair_index):
-    neig = eigenpotentials.shape[0]
     group = lax.axis_index(GROUP).astype(jnp.int32).reshape(1)
     core = lax.axis_index("c").astype(jnp.int32).reshape(1)
-    scales = screening.reshape(2, neig // 2)
-    sent, slots = prepare(orbitals, trial_vectors, pair_index)
-    sent, slots, group, core, scales = lax.optimization_barrier((sent, slots, group, core, scales))
-    slots = exchange(slots, GROUP)
-    slots, sent = lax.optimization_barrier((slots, sent))
-    phi = exchange(sent, ORB)
-    phi = phi.reshape(32 * phi.shape[1], phi.shape[2])
-    slots = slots.reshape(-1, ROWS, BLOCK)
-    dens, pot, halves, live = density(group, phi, slots, eigenpotentials)
+    scales = screening.reshape(1, -1)
+    sent, own_slots = prepare(orbitals, trial_vectors, pair_index)
+    slots = [own_slots]
+    for k in range(1, 4):
+        slots.append(lax.ppermute(own_slots, GROUP, [(i, i ^ k) for i in range(4)]))
+    mine = exchange(sent, SOURCES)
+    mine = mine.reshape(-1, mine.shape[2])
+    other = lax.ppermute(mine, "c", [(0, 1), (1, 0)])
+    dens, pot, halves, live = density(group, core, mine, other, slots, eigenpotentials)
     column = summed(exchange(halves, COLUMN)).astype(bf16)
-    mine = summed(exchange(copies(column, 16), PLANE))
-    other = lax.ppermute(mine, "c", [(0, 1), (1, 0)])
-    terms = direct_terms(core, live, mine, other, scales, pot, dens)
-    terms = exchange(terms.reshape(8, -1, NB, BLOCK), GROUP)
+    part = summed(exchange(copies(column, 16), PLANE))
+    apart = lax.ppermute(part, "c", [(0, 1), (1, 0)])
+    terms = direct_terms(core, live, part, apart, scales, pot, dens)
+    terms = exchange(terms.reshape(4, -1, NB, BLOCK), GROUP)
     owner = summed(terms).astype(bf16)
     direct = summed(exchange(copies(owner, 8), SLAB))
     return direct.transpose(1, 0, 2).reshape(NB, -1)

time: 105 us -> 97.4 us (0.928)
  blocking collectives: 89.2 us -> 75.1 us
  starting transfers between devices: 0.09 us -> 3.58 us
  waiting for transfers between devices: 1.19 us -> 4.5 us
    all_to_all x6 -> x5, blocking collectives: 89.2 us -> 75.1 us  [exchange(): return lax.all_to_all(blocks, axes, 0, 0, tiled=True)]
    ppermute x0 -> x4, waiting for transfers between devices: none -> 4.5 us  [the longest x3 3.3 us: shards(): slots.append(lax.ppermute(own_slots, GROUP, [(i, i ^ k) for i in range(4)]))]
    ppermute x0 -> x4, starting transfers between devices: none -> 3.58 us  [the longest x3 3.49 us: shards(): slots.append(lax.ppermute(own_slots, GROUP, [(i, i ^ k) for i in range(4)]))]
    ppermute x1, waiting for transfers between devices: 1.19 us -> 0.01 us  [shards(): other = lax.ppermute(mine, 'c', [(0, 1), (1, 0)])]
  transfers between devices with their start and end apart: 1 -> 5, of which waited for: 1 -> 4; matrix products, arithmetic and copies ran while one was open for 0% -> 0% of each run, Pallas kernels for 0% -> 0%
where the time goes in v3:
time: 97.4 us; the launch traced here: 97 us
  blocking collectives  75.1 us (77%)
  Pallas kernels  13 us (13%)
  waiting for transfers between devices  4.5 us (5%)
  starting transfers between devices  3.58 us (4%)
    all_to_all x5, blocking collectives, exchange(): return lax.all_to_all(blocks, axes, 0, 0, tiled=True)  75.1 us
    pallas_call x1, Pallas kernels, density(): pl.pallas_call(density_body, in_specs=[IN_SMEM] * 2 + [IN_VMEM] * 6 + [IN...  8.69 us
    ppermute x3, starting transfers between devices, shards(): slots.append(lax.ppermute(own_slots, GROUP, [(i, i ^ k) for i in range(4)]))  3.49 us
    ppermute x3, waiting for transfers between devices, shards(): slots.append(lax.ppermute(own_slots, GROUP, [(i, i ^ k) for i in range(4)]))  3.3 us
    pallas_call x1, Pallas kernels, direct_terms(): pl.pallas_call(direct_body, in_specs=[IN_SMEM, IN_SMEM] + [IN_VMEM] * 4 +...  3.08 us
  transfers between devices with their start and end apart: 5, of which 4 were waited for; matrix products, arithmetic and copies ran while one was open for 0% of the time, Pallas kernels for 0%

profile of v3, /device:TPU:2, one launch (start us, length us, event | category | flops | bytes accessed | tf_op | source)
XLA Modules:
  0.0 97.0 jit_solution(15397629658608904556)
XLA Ops:
  0.0 0.0 copy-start
  0.0 1.2 %prepare.1 = (bf16[16,16,1024]{2,1,0:T(8,128)(2,1)S(1)}, bf16[8,24,128]{2,1,0:T(8,128)(2,1)S(1)}) custom-call(bf16[16,4096]{1,0:T(8,128)(2,1)} %orbitals_ref.1, bf16[16,1024]{1,0:T(8,128)(2,1)} %trial_ref.1, s32[2,1024]{1,0:T(2,128)} %pair_ref.1), custom_call_target="tpu_custom_call" | custom-call | tf_op jit(solution)/shard_map/prepare/pallas_call | solution.py:100
  1.2 25.1 %all_to_all.25 = bf16[16,16,1024]{2,1,0:T(8,128)(2,1)S(1)} all-to-all(bf16[16,16,1024]{2,1,0:T(8,128)(2,1)S(1)} %get-tuple-element.11), channel_id=1, replica_groups=mesh['yl'=2,'zh'=4,'zl'=2,'c'=2,'yh'=2,'x'=4] {'yl','zh','zl'}, dimensions={0} | all-to-all | bytes 1048576 | tf_op jit(solution)/shard_map/all_to_all | solution.py:30
  26.3 0.0 collective-permute-start
  26.3 2.3 %collective-permute-start.3 = (bf16[8,24,128]{2,1,0:T(8,128)(2,1)S(1)}, bf16[8,24,128]{2,1,0:T(8,128)(2,1)S(1)}, u32[]{:S(2)}, u32[]{:S(2)}) collective-permute-start(bf16[8,24,128]{2,1,0:T(8,128)(2,1)S(1)} %get-tuple-element.12.slots0_ref), channel_id=1, source_target_pairs={{0,144},{16,128},{128,16},{144,0},{1,145},{17,129},{129,17},{145,1... | collective-permute-start | bytes 147464 | tf_op jit(solution)/shard_map/ppermute | solution.py:296
  28.6 0.4 collective-permute-start.2
  29.0 0.8 collective-permute-start.1
  29.8 1.6 %collective-permute-done.3.slots3_ref = bf16[8,24,128]{2,1,0:T(8,128)(2,1)S(1)} collective-permute-done((bf16[8,24,128]{2,1,0:T(8,128)(2,1)S(1)}, bf16[8,24,128]{2,1,0:T(8,128)(2,1)S(1)}, u32[]{:S(2)}, u32[]{:S(2)}) %collective-permute-start.3) | collective-permute-done | bytes 49184 | tf_op jit(solution)/shard_map/ppermute | solution.py:296
  31.3 1.4 %collective-permute-done.2.slots2_ref = bf16[8,24,128]{2,1,0:T(8,128)(2,1)S(1)} collective-permute-done((bf16[8,24,128]{2,1,0:T(8,128)(2,1)S(1)}, bf16[8,24,128]{2,1,0:T(8,128)(2,1)S(1)}, u32[]{:S(2)}, u32[]{:S(2)}) %collective-permute-start.2) | collective-permute-done | bytes 49184 | tf_op jit(solution)/shard_map/ppermute | solution.py:296
  32.7 0.4 collective-permute-done.1.slots1_ref
  33.1 0.0 collective-permute-done.other_ref
  33.1 8.7 %density.1 = (bf16[8,1024,512]{2,1,0:T(8,128)(2,1)}, bf16[1024,1024]{1,0:T(8,128)(2,1)S(1)}, bf16[16,16,512]{2,1,0:T(8,128)(2,1)S(1)}, s32[37]{0:T(128)S(1)}) custom-call(s32[1]{0:T(128)} %bitcast.1.group_ref, s32[1]{0:T(128)} %bitcast.core_ref, bf16[256,1024]{1,0:T(8,128)(2,1)S(1)} %bitcast.12, bf16[256,1024]{1,0:T(8,128)(2,1)S(1)} %collective-permute-done.other_ref, ...), custom_call_target="tpu_custom_call" | custom-call | tf_op jit(solution)/shard_map/density/pallas_call | solution.py:215
  41.8 15.4 %all_to_all.26 = bf16[16,16,512]{2,1,0:T(8,128)(2,1)S(1)} all-to-all(bf16[16,16,512]{2,1,0:T(8,128)(2,1)S(1)} %get-tuple-element.14), channel_id=1, replica_groups=mesh['yl'=2,'zh'=4,'zl'=2,'c'=2,'yh'=2,'x'=4] {'zh','zl','c'}, dimensions={0} | all-to-all | bytes 524288 | tf_op jit(solution)/shard_map/all_to_all | solution.py:30
  57.2 15.3 %all_to_all.27 = bf16[16,16,512]{2,1,0:T(8,128)(2,1)S(1)} all-to-all(bf16[16,16,512]{2,1,0:T(8,128)(2,1)S(1)} %broadcast_in_dim.4), channel_id=1, replica_groups=mesh['yl'=2,'zh'=4,'zl'=2,'c'=2,'yh'=2,'x'=4] {'yl','yh','x'}, dimensions={0} | all-to-all | bytes 524288 | tf_op jit(solution)/shard_map/all_to_all | solution.py:30
  72.6 0.1 collective-permute-start.4
  72.7 1.2 %collective-permute-done.4.other_ref = f32[16,512]{1,0:T(8,128)S(1)} collective-permute-done((f32[16,512]{1,0:T(8,128)S(1)}, f32[16,512]{1,0:T(8,128)S(1)}, u32[]{:S(2)}, u32[]{:S(2)}) %collective-permute-start.4) | collective-permute-done | bytes 32800 | tf_op jit(solution)/shard_map/ppermute | solution.py:303
  73.9 0.0 copy-done
  73.9 3.1 %direct_terms.1 = bf16[32,16,128]{2,1,0:T(8,128)(2,1)S(1)} custom-call(s32[1]{0:T(128)} %bitcast.core_ref, s32[37]{0:T(128)S(1)} %get-tuple-element.13.list_ref, f32[16,512]{1,0:T(8,128)S(1)} %convert_reduce_fusion.1.mine_ref, f32[16,512]{1,0:T(8,128)S(1)} %collective-permute-done.4.other_ref, f32[1,1024]{1,0:T(1,128)S(1)} %bitcast.14, ...), custom_call_target="tpu_custom_call" | custom-call | tf_op jit(solution)/shard_map/direct_terms/pallas_call | solution.py:274
  77.0 7.6 %all_to_all.28 = bf16[4,8,16,128]{3,2,1,0:T(8,128)(2,1)S(1)} all-to-all(bf16[4,8,16,128]{3,2,1,0:T(8,128)(2,1)S(1)} %bitcast.13), channel_id=1, replica_groups=mesh['yl'=2,'zh'=4,'zl'=2,'c'=2,'yh'=2,'x'=4] {'yl','zl'}, dimensions={0} | all-to-all | bytes 262144 | tf_op jit(solution)/shard_map/all_to_all | solution.py:30
  84.7 11.7 %all_to_all.29 = bf16[8,8,16,128]{3,2,1,0:T(8,128)(2,1)S(1)} all-to-all(bf16[8,8,16,128]{3,2,1,0:T(8,128)(2,1)S(1)} %broadcast_in_dim.5), channel_id=1, replica_groups=mesh['yl'=2,'zh'=4,'zl'=2,'c'=2,'yh'=2,'x'=4] {'yh','x'}, dimensions={0} | all-to-all | bytes 524288 | tf_op jit(solution)/shard_map/all_to_all | solution.py:30
  96.4 0.6 copy_bitcast_fusion
  (6 shorter events, 0.2 us)
Async XLA Ops:
  0.0 73.9 %copy-start = (f32[1024]{0:T(1024)S(1)}, f32[1024]{0:T(1024)}, u32[]{:S(2)}) copy-start(f32[1024]{0:T(1024)} %param.7) | copy-start | bytes 12292
  26.3 6.8 %collective-permute-start = (bf16[256,1024]{1,0:T(8,128)(2,1)S(1)}, bf16[256,1024]{1,0:T(8,128)(2,1)S(1)}, u32[]{:S(2)}, u32[]{:S(2)}) collective-permute-start(bf16[256,1024]{1,0:T(8,128)(2,1)S(1)} %bitcast.11), channel_id=1, source_target_pairs={{0,8},{8,0},{1,9},{9,1},{2,10},{10,2},{3,11},{11,3},{4,12},{12,4},... | collective-permute-start | bytes 1572872 | tf_op jit(solution)/shard_map/ppermute | solution.py:299
  26.3 5.1 %collective-permute-start.3 = (bf16[8,24,128]{2,1,0:T(8,128)(2,1)S(1)}, bf16[8,24,128]{2,1,0:T(8,128)(2,1)S(1)}, u32[]{:S(2)}, u32[]{:S(2)}) collective-permute-start(bf16[8,24,128]{2,1,0:T(8,128)(2,1)S(1)} %get-tuple-element.12.slots0_ref), channel_id=1, source_target_pairs={{0,144},{16,128},{128,16},{144,0},{1,145},{17,129},{129,17},{145,1... | collective-permute-start | bytes 147464 | tf_op jit(solution)/shard_map/ppermute | solution.py:296
  28.6 4.1 %collective-permute-start.2 = (bf16[8,24,128]{2,1,0:T(8,128)(2,1)S(1)}, bf16[8,24,128]{2,1,0:T(8,128)(2,1)S(1)}, u32[]{:S(2)}, u32[]{:S(2)}) collective-permute-start(bf16[8,24,128]{2,1,0:T(8,128)(2,1)S(1)} %get-tuple-element.12.slots0_ref), channel_id=1, source_target_pairs={{0,128},{16,144},{128,0},{144,16},{1,129},{17,145},{129,1},{145,17... | collective-permute-start | bytes 147464 | tf_op jit(solution)/shard_map/ppermute | solution.py:296
  29.0 4.1 %collective-permute-start.1 = (bf16[8,24,128]{2,1,0:T(8,128)(2,1)S(1)}, bf16[8,24,128]{2,1,0:T(8,128)(2,1)S(1)}, u32[]{:S(2)}, u32[]{:S(2)}) collective-permute-start(bf16[8,24,128]{2,1,0:T(8,128)(2,1)S(1)} %get-tuple-element.12.slots0_ref), channel_id=1, source_target_pairs={{0,16},{16,0},{128,144},{144,128},{1,17},{17,1},{129,145},{145,129... | collective-permute-start | bytes 147464 | tf_op jit(solution)/shard_map/ppermute | solution.py:296
  72.6 1.3 %collective-permute-start.4 = (f32[16,512]{1,0:T(8,128)S(1)}, f32[16,512]{1,0:T(8,128)S(1)}, u32[]{:S(2)}, u32[]{:S(2)}) collective-permute-start(f32[16,512]{1,0:T(8,128)S(1)} %convert_reduce_fusion.1.mine_ref), channel_id=1, source_target_pairs={{0,8},{8,0},{1,9},{9,1},{2,10},{10,2},{3,11},{11,3},{4,12},{12,4},... | collective-permute-start | bytes 98312 | tf_op jit(solution)/shard_map/ppermute | solution.py:303

commit v4 on v3

--- a/solution.py
+++ b/solution.py
@@ -13,7 +13,7 @@
 GROUP = ("yl", "zl")
 SOURCES = ("yl", "zh", "zl")
 COLUMN = ("zh", "zl", "c")
-PLANE = ("yl", "yh", "x")
+WIDE = ("yl", "zl", "yh", "x")
 
 NB = 16
 BLOCK = 128
@@ -128,7 +128,7 @@
     all_pot_ref,
     kept_ref,
     pot_ref,
-    halves_ref,
+    quarters_ref,
     list_ref,
     slots_ref,
     phit_ref,
@@ -195,10 +195,10 @@
     lower = (fieldt - upper.astype(f32)).astype(bf16)
     projt = dot(pot_ref[...], upper) + dot(pot_ref[...], lower)
     proj = projt.T.astype(bf16)
-    width = halves_ref.shape[2]
-    for core in range(2):
-        for layer in range(8):
-            halves_ref[layer * 2 + core] = proj[:, core * width : (core + 1) * width]
+    width = quarters_ref.shape[2]
+    for to in range(16):
+        quarter = (to % 2) * 2 + (to // 2) % 2
+        quarters_ref[to] = proj[:, quarter * width : (quarter + 1) * width]
 
     def kept(turn, unused):
         pltpu.make_async_copy(dens_ref.at[turn], kept_ref.at[turn], sems.at[turn]).wait()
@@ -219,7 +219,7 @@
         out_shape=[
             pltpu.HBM((turns, points, TAKE * BLOCK), bf16),
             pltpu.VMEM((neig, points), bf16),
-            pltpu.VMEM((16, NB, neig // 2), bf16),
+            pltpu.VMEM((16, NB, neig // 4), bf16),
             jax.ShapeDtypeStruct((1 + blocks + TAKE,), jnp.int32),
         ],
         scratch_shapes=[
@@ -244,11 +244,11 @@
         return unused
 
     lax.fori_loop(0, turns, fetch, 0)
-    half = mine_ref.shape[1]
+    half = mine_ref.shape[0] * mine_ref.shape[2]
     total = jnp.zeros((NB, pot_ref.shape[1]), f32)
     for ref, core in ((mine_ref, core_ref[0]), (other_ref, 1 - core_ref[0])):
         scales = jnp.where(core == 0, screening_ref[:, :half], screening_ref[:, half:])
-        screened = ref[...] * scales
+        screened = jnp.concatenate([ref[0], ref[1]], axis=1) * scales
         rows = pot_ref[pl.ds(pl.multiple_of(core * half, half), half), :]
         total += folded(dot(in_two(screened), rows))
     split_ref[...] = in_two(total)
@@ -297,9 +297,10 @@
     mine = exchange(sent, SOURCES)
     mine = mine.reshape(-1, mine.shape[2])
     other = lax.ppermute(mine, "c", [(0, 1), (1, 0)])
-    dens, pot, halves, live = density(group, core, mine, other, slots, eigenpotentials)
-    column = summed(exchange(halves, COLUMN)).astype(bf16)
-    part = summed(exchange(copies(column, 16), PLANE))
+    dens, pot, quarters, live = density(group, core, mine, other, slots, eigenpotentials)
+    column = summed(exchange(quarters, COLUMN)).astype(bf16)
+    wide = exchange(copies(column, 32), WIDE)
+    part = jnp.sum(wide.reshape(2, 2, 8, *column.shape).astype(f32), axis=(0, 2))
     apart = lax.ppermute(part, "c", [(0, 1), (1, 0)])
     terms = direct_terms(core, live, part, apart, scales, pot, dens)
     terms = exchange(terms.reshape(4, -1, NB, BLOCK), GROUP)

time: 97.4 us -> 96.1 us (0.987)
  blocking collectives: 75.1 us -> 73.8 us
    all_to_all x5, blocking collectives: 75.1 us -> 73.8 us  [exchange(): return lax.all_to_all(blocks, axes, 0, 0, tiled=True)]
where the time goes in v4:
time: 96.1 us; the launch traced here: 95.7 us
  blocking collectives  73.8 us (77%)
  Pallas kernels  13 us (14%)
  waiting for transfers between devices  4.5 us (5%)
  starting transfers between devices  3.58 us (4%)
    all_to_all x5, blocking collectives, exchange(): return lax.all_to_all(blocks, axes, 0, 0, tiled=True)  73.8 us
    pallas_call x1, Pallas kernels, density(): pl.pallas_call(density_body, in_specs=[IN_SMEM] * 2 + [IN_VMEM] * 6 + [IN...  8.69 us
    ppermute x3, starting transfers between devices, shards(): slots.append(lax.ppermute(own_slots, GROUP, [(i, i ^ k) for i in range(4)]))  3.49 us
    ppermute x3, waiting for transfers between devices, shards(): slots.append(lax.ppermute(own_slots, GROUP, [(i, i ^ k) for i in range(4)]))  3.3 us
    pallas_call x1, Pallas kernels, direct_terms(): pl.pallas_call(direct_body, in_specs=[IN_SMEM, IN_SMEM] + [IN_VMEM] * 4 +...  3.08 us
  transfers between devices with their start and end apart: 5, of which 4 were waited for; matrix products, arithmetic and copies ran while one was open for 0% of the time, Pallas kernels for 0%

profile of v4, /device:TPU:2, one launch (start us, length us, event | category | flops | bytes accessed | tf_op | source)
XLA Modules:
  0.0 95.7 jit_solution(12287109301372529556)
XLA Ops:
  0.0 0.0 copy-start
  0.0 1.2 %prepare.1 = (bf16[16,16,1024]{2,1,0:T(8,128)(2,1)S(1)}, bf16[8,24,128]{2,1,0:T(8,128)(2,1)S(1)}) custom-call(bf16[16,4096]{1,0:T(8,128)(2,1)} %orbitals_ref.1, bf16[16,1024]{1,0:T(8,128)(2,1)} %trial_ref.1, s32[2,1024]{1,0:T(2,128)} %pair_ref.1), custom_call_target="tpu_custom_call" | custom-call | tf_op jit(solution)/shard_map/prepare/pallas_call | solution.py:100
  1.2 25.1 %all_to_all.25 = bf16[16,16,1024]{2,1,0:T(8,128)(2,1)S(1)} all-to-all(bf16[16,16,1024]{2,1,0:T(8,128)(2,1)S(1)} %get-tuple-element.11), channel_id=1, replica_groups=mesh['yl'=2,'zh'=4,'zl'=2,'c'=2,'yh'=2,'x'=4] {'yl','zh','zl'}, dimensions={0} | all-to-all | bytes 1048576 | tf_op jit(solution)/shard_map/all_to_all | solution.py:30
  26.3 0.0 collective-permute-start
  26.3 2.3 %collective-permute-start.3 = (bf16[8,24,128]{2,1,0:T(8,128)(2,1)S(1)}, bf16[8,24,128]{2,1,0:T(8,128)(2,1)S(1)}, u32[]{:S(2)}, u32[]{:S(2)}) collective-permute-start(bf16[8,24,128]{2,1,0:T(8,128)(2,1)S(1)} %get-tuple-element.12.slots0_ref), channel_id=1, source_target_pairs={{0,144},{16,128},{128,16},{144,0},{1,145},{17,129},{129,17},{145,1... | collective-permute-start | bytes 147464 | tf_op jit(solution)/shard_map/ppermute | solution.py:296
  28.6 0.4 collective-permute-start.2
  29.0 0.8 collective-permute-start.1
  29.8 1.6 %collective-permute-done.3.slots3_ref = bf16[8,24,128]{2,1,0:T(8,128)(2,1)S(1)} collective-permute-done((bf16[8,24,128]{2,1,0:T(8,128)(2,1)S(1)}, bf16[8,24,128]{2,1,0:T(8,128)(2,1)S(1)}, u32[]{:S(2)}, u32[]{:S(2)}) %collective-permute-start.3) | collective-permute-done | bytes 49184 | tf_op jit(solution)/shard_map/ppermute | solution.py:296
  31.3 1.4 %collective-permute-done.2.slots2_ref = bf16[8,24,128]{2,1,0:T(8,128)(2,1)S(1)} collective-permute-done((bf16[8,24,128]{2,1,0:T(8,128)(2,1)S(1)}, bf16[8,24,128]{2,1,0:T(8,128)(2,1)S(1)}, u32[]{:S(2)}, u32[]{:S(2)}) %collective-permute-start.2) | collective-permute-done | bytes 49184 | tf_op jit(solution)/shard_map/ppermute | solution.py:296
  32.7 0.4 collective-permute-done.1.slots1_ref
  33.1 0.0 collective-permute-done.other_ref
  33.1 8.7 %density.1 = (bf16[8,1024,512]{2,1,0:T(8,128)(2,1)}, bf16[1024,1024]{1,0:T(8,128)(2,1)S(1)}, bf16[16,16,256]{2,1,0:T(8,128)(2,1)S(1)}, s32[37]{0:T(128)S(1)}) custom-call(s32[1]{0:T(128)} %bitcast.1.group_ref, s32[1]{0:T(128)} %bitcast.core_ref, bf16[256,1024]{1,0:T(8,128)(2,1)S(1)} %bitcast.14, bf16[256,1024]{1,0:T(8,128)(2,1)S(1)} %collective-permute-done.other_ref, ...), custom_call_target="tpu_custom_call" | custom-call | tf_op jit(solution)/shard_map/density/pallas_call | solution.py:215
  41.8 12.9 %all_to_all.26 = bf16[16,16,256]{2,1,0:T(8,128)(2,1)S(1)} all-to-all(bf16[16,16,256]{2,1,0:T(8,128)(2,1)S(1)} %get-tuple-element.14), channel_id=1, replica_groups=mesh['yl'=2,'zh'=4,'zl'=2,'c'=2,'yh'=2,'x'=4] {'zh','zl','c'}, dimensions={0} | all-to-all | bytes 262144 | tf_op jit(solution)/shard_map/all_to_all | solution.py:30
  54.7 16.1 %all_to_all.27 = bf16[32,16,256]{2,1,0:T(8,128)(2,1)S(1)} all-to-all(bf16[32,16,256]{2,1,0:T(8,128)(2,1)S(1)} %broadcast_in_dim.4), channel_id=1, replica_groups=mesh['yl'=2,'zh'=4,'zl'=2,'c'=2,'yh'=2,'x'=4] {'yl','zl','yh','x'}, dimensions={0} | all-to-all | bytes 524288 | tf_op jit(solution)/shard_map/all_to_all | solution.py:30
  70.8 0.1 collective-permute-start.4
  70.9 1.2 %collective-permute-done.4.other_ref = f32[2,16,256]{2,1,0:T(8,128)S(1)} collective-permute-done((f32[2,16,256]{2,1,0:T(8,128)S(1)}, f32[2,16,256]{2,1,0:T(8,128)S(1)}, u32[]{:S(2)}, u32[]{:S(2)}) %collective-permute-start.4) | collective-permute-done | bytes 32800 | tf_op jit(solution)/shard_map/ppermute | solution.py:304
  72.1 0.0 copy-done
  72.1 3.1 %direct_terms.1 = bf16[32,16,128]{2,1,0:T(8,128)(2,1)S(1)} custom-call(s32[1]{0:T(128)} %bitcast.core_ref, s32[37]{0:T(128)S(1)} %get-tuple-element.13.list_ref, f32[2,16,256]{2,1,0:T(8,128)S(1)} %convert_reduce_fusion.mine_ref, f32[2,16,256]{2,1,0:T(8,128)S(1)} %collective-permute-done.4.other_ref, f32[1,1024]{1,0:T(1,128)S(1)} %bitcast.16, ...), custom_call_target="tpu_custom_call" | custom-call | tf_op jit(solution)/shard_map/direct_terms/pallas_call | solution.py:274
  75.2 7.6 %all_to_all.28 = bf16[4,8,16,128]{3,2,1,0:T(8,128)(2,1)S(1)} all-to-all(bf16[4,8,16,128]{3,2,1,0:T(8,128)(2,1)S(1)} %bitcast.15), channel_id=1, replica_groups=mesh['yl'=2,'zh'=4,'zl'=2,'c'=2,'yh'=2,'x'=4] {'yl','zl'}, dimensions={0} | all-to-all | bytes 262144 | tf_op jit(solution)/shard_map/all_to_all | solution.py:30
  82.9 12.1 %all_to_all.29 = bf16[8,8,16,128]{3,2,1,0:T(8,128)(2,1)S(1)} all-to-all(bf16[8,8,16,128]{3,2,1,0:T(8,128)(2,1)S(1)} %broadcast_in_dim.5), channel_id=1, replica_groups=mesh['yl'=2,'zh'=4,'zl'=2,'c'=2,'yh'=2,'x'=4] {'yh','x'}, dimensions={0} | all-to-all | bytes 524288 | tf_op jit(solution)/shard_map/all_to_all | solution.py:30
  95.1 0.6 copy_bitcast_fusion
  (6 shorter events, 0.2 us)
Async XLA Ops:
  0.0 72.1 %copy-start = (f32[1024]{0:T(1024)S(1)}, f32[1024]{0:T(1024)}, u32[]{:S(2)}) copy-start(f32[1024]{0:T(1024)} %param.7) | copy-start | bytes 12292
  26.3 6.8 %collective-permute-start = (bf16[256,1024]{1,0:T(8,128)(2,1)S(1)}, bf16[256,1024]{1,0:T(8,128)(2,1)S(1)}, u32[]{:S(2)}, u32[]{:S(2)}) collective-permute-start(bf16[256,1024]{1,0:T(8,128)(2,1)S(1)} %bitcast.13), channel_id=1, source_target_pairs={{0,8},{8,0},{1,9},{9,1},{2,10},{10,2},{3,11},{11,3},{4,12},{12,4},... | collective-permute-start | bytes 1572872 | tf_op jit(solution)/shard_map/ppermute | solution.py:299
  26.3 5.1 %collective-permute-start.3 = (bf16[8,24,128]{2,1,0:T(8,128)(2,1)S(1)}, bf16[8,24,128]{2,1,0:T(8,128)(2,1)S(1)}, u32[]{:S(2)}, u32[]{:S(2)}) collective-permute-start(bf16[8,24,128]{2,1,0:T(8,128)(2,1)S(1)} %get-tuple-element.12.slots0_ref), channel_id=1, source_target_pairs={{0,144},{16,128},{128,16},{144,0},{1,145},{17,129},{129,17},{145,1... | collective-permute-start | bytes 147464 | tf_op jit(solution)/shard_map/ppermute | solution.py:296
  28.6 4.1 %collective-permute-start.2 = (bf16[8,24,128]{2,1,0:T(8,128)(2,1)S(1)}, bf16[8,24,128]{2,1,0:T(8,128)(2,1)S(1)}, u32[]{:S(2)}, u32[]{:S(2)}) collective-permute-start(bf16[8,24,128]{2,1,0:T(8,128)(2,1)S(1)} %get-tuple-element.12.slots0_ref), channel_id=1, source_target_pairs={{0,128},{16,144},{128,0},{144,16},{1,129},{17,145},{129,1},{145,17... | collective-permute-start | bytes 147464 | tf_op jit(solution)/shard_map/ppermute | solution.py:296
  29.0 4.1 %collective-permute-start.1 = (bf16[8,24,128]{2,1,0:T(8,128)(2,1)S(1)}, bf16[8,24,128]{2,1,0:T(8,128)(2,1)S(1)}, u32[]{:S(2)}, u32[]{:S(2)}) collective-permute-start(bf16[8,24,128]{2,1,0:T(8,128)(2,1)S(1)} %get-tuple-element.12.slots0_ref), channel_id=1, source_target_pairs={{0,16},{16,0},{128,144},{144,128},{1,17},{17,1},{129,145},{145,129... | collective-permute-start | bytes 147464 | tf_op jit(solution)/shard_map/ppermute | solution.py:296
  70.8 1.3 %collective-permute-start.4 = (f32[2,16,256]{2,1,0:T(8,128)S(1)}, f32[2,16,256]{2,1,0:T(8,128)S(1)}, u32[]{:S(2)}, u32[]{:S(2)}) collective-permute-start(f32[2,16,256]{2,1,0:T(8,128)S(1)} %convert_reduce_fusion.mine_ref), channel_id=1, source_target_pairs={{0,8},{8,0},{1,9},{9,1},{2,10},{10,2},{3,11},{11,3},{4,12},{12,4},... | collective-permute-start | bytes 98312 | tf_op jit(solution)/shard_map/ppermute | solution.py:304

commit v5 on v4

--- a/solution.py
+++ b/solution.py
@@ -193,8 +193,7 @@
     fieldt = fieldt_ref[...]
     upper = fieldt.astype(bf16)
     lower = (fieldt - upper.astype(f32)).astype(bf16)
-    projt = dot(pot_ref[...], upper) + dot(pot_ref[...], lower)
-    proj = projt.T.astype(bf16)
+    proj = folded(dot(pot_ref[...], jnp.concatenate([upper, lower], axis=1)).T).astype(bf16)
     width = quarters_ref.shape[2]
     for to in range(16):
         quarter = (to % 2) * 2 + (to // 2) % 2
@@ -235,7 +234,24 @@
     )(group, core, *vmem(mine, other, *slots), *hbm(eigenpotentials))
 
 
-def direct_body(core_ref, list_ref, mine_ref, other_ref, screening_ref, pot_ref, kept_ref, out_ref, split_ref, dens_ref, sems):
+def direct_body(
+    group_ref,
+    core_ref,
+    list_ref,
+    mine_ref,
+    other_ref,
+    screening_ref,
+    pot_ref,
+    kept_ref,
+    out0_ref,
+    out1_ref,
+    out2_ref,
+    out3_ref,
+    terms_ref,
+    split_ref,
+    dens_ref,
+    sems,
+):
     count = list_ref[0]
     turns = (count + TAKE - 1) // TAKE
 
@@ -244,6 +260,7 @@
         return unused
 
     lax.fori_loop(0, turns, fetch, 0)
+    terms_ref[...] = jnp.zeros_like(terms_ref)
     half = mine_ref.shape[0] * mine_ref.shape[2]
     total = jnp.zeros((NB, pot_ref.shape[1]), f32)
     for ref, core in ((mine_ref, core_ref[0]), (other_ref, 1 - core_ref[0])):
@@ -252,7 +269,8 @@
         rows = pot_ref[pl.ds(pl.multiple_of(core * half, half), half), :]
         total += folded(dot(in_two(screened), rows))
     split_ref[...] = in_two(total)
-    out_ref[...] = jnp.zeros_like(out_ref)
+    each = out0_ref.shape[0]
+    own = group_ref[0] * each
 
     def step(turn, unused):
         pltpu.make_async_copy(kept_ref.at[turn], dens_ref.at[turn], sems.at[turn]).wait()
@@ -262,28 +280,31 @@
 
             @pl.when(at < count)
             def _():
-                out_ref[list_ref[1 + at]] = terms[:, k * BLOCK : (k + 1) * BLOCK]
+                terms_ref[list_ref[1 + at] ^ own] = terms[:, k * BLOCK : (k + 1) * BLOCK]
 
         return unused
 
     lax.fori_loop(0, turns, step, 0)
-
-
-def direct_terms(core, live, mine, other, screening, pot, dens):
+    for k, ref in enumerate((out0_ref, out1_ref, out2_ref, out3_ref)):
+        ref[...] = terms_ref[k * each : (k + 1) * each]
+
+
+def direct_terms(group, core, live, mine, other, screening, pot, dens):
     blocks = dens.shape[0] * TAKE
     return pl.pallas_call(
         direct_body,
-        in_specs=[IN_SMEM, IN_SMEM] + [IN_VMEM] * 4 + [IN_HBM],
-        out_specs=IN_VMEM,
-        out_shape=pltpu.VMEM((blocks, NB, BLOCK), bf16),
+        in_specs=[IN_SMEM] * 3 + [IN_VMEM] * 4 + [IN_HBM],
+        out_specs=[IN_VMEM] * 4,
+        out_shape=[pltpu.VMEM((blocks // 4, NB, BLOCK), bf16)] * 4,
         scratch_shapes=[
+            pltpu.VMEM((blocks, NB, BLOCK), bf16),
             pltpu.VMEM((2 * NB, pot.shape[1]), bf16),
             pltpu.VMEM(dens.shape, bf16),
             pltpu.SemaphoreType.DMA((dens.shape[0],)),
         ],
         compiler_params=pltpu.CompilerParams(vmem_limit_bytes=LIMIT),
         name="direct_terms",
-    )(core, live, *vmem(mine, other, screening, pot), *hbm(dens))
+    )(group, core, live, *vmem(mine, other, screening, pot), *hbm(dens))
 
 
 def shards(orbitals, eigenpotentials, screening, trial_vectors, pair_index):
@@ -302,9 +323,11 @@
     wide = exchange(copies(column, 32), WIDE)
     part = jnp.sum(wide.reshape(2, 2, 8, *column.shape).astype(f32), axis=(0, 2))
     apart = lax.ppermute(part, "c", [(0, 1), (1, 0)])
-    terms = direct_terms(core, live, part, apart, scales, pot, dens)
-    terms = exchange(terms.reshape(4, -1, NB, BLOCK), GROUP)
-    owner = summed(terms).astype(bf16)
+    terms = direct_terms(group, core, live, part, apart, scales, pot, dens)
+    owner = terms[0].astype(f32)
+    for k in range(1, 4):
+        owner += lax.ppermute(terms[k], GROUP, [(i, i ^ k) for i in range(4)]).astype(f32)
+    owner = owner.astype(bf16)
     direct = summed(exchange(copies(owner, 8), SLAB))
     return direct.transpose(1, 0, 2).reshape(NB, -1)
 

time: 96.1 us -> 95 us (0.989)
  blocking collectives: 73.8 us -> 66.8 us
  starting transfers between devices: 3.58 us -> 7.16 us
  waiting for transfers between devices: 4.5 us -> 7.3 us
    all_to_all x5 -> x4, blocking collectives: 73.8 us -> 66.8 us  [exchange(): return lax.all_to_all(blocks, axes, 0, 0, tiled=True)]
    ppermute x0 -> x3, starting transfers between devices: none -> 3.58 us  [shards(): lax.ppermute(terms[k], GROUP, [(i, i ^ k) for i in range(4)]).astype(f32)]
    ppermute x0 -> x3, waiting for transfers between devices: none -> 2.8 us  [shards(): lax.ppermute(terms[k], GROUP, [(i, i ^ k) for i in range(4)]).astype(f32)]
  transfers between devices with their start and end apart: 5 -> 8, of which waited for: 4 -> 7; matrix products, arithmetic and copies ran while one was open for 0% -> 0% of each run, Pallas kernels for 0% -> 0%
where the time goes in v5:
time: 95 us; the launch traced here: 94.7 us
  blocking collectives  66.8 us (70%)
  Pallas kernels  12.5 us (13%)
  waiting for transfers between devices  7.3 us (8%)
  starting transfers between devices  7.16 us (8%)
    all_to_all x4, blocking collectives, exchange(): return lax.all_to_all(blocks, axes, 0, 0, tiled=True)  66.8 us
    pallas_call x1, Pallas kernels, density(): pl.pallas_call(density_body, in_specs=[IN_SMEM] * 2 + [IN_VMEM] * 6 + [IN...  8.23 us
    ppermute x3, starting transfers between devices, shards(): lax.ppermute(terms[k], GROUP, [(i, i ^ k) for i in range(4)]).astype(f32)  3.58 us
    ppermute x3, starting transfers between devices, shards(): slots.append(lax.ppermute(own_slots, GROUP, [(i, i ^ k) for i in range(4)]))  3.49 us
    ppermute x3, waiting for transfers between devices, shards(): slots.append(lax.ppermute(own_slots, GROUP, [(i, i ^ k) for i in range(4)]))  3.3 us
    pallas_call x1, Pallas kernels, direct_terms(): pl.pallas_call(direct_body, in_specs=[IN_SMEM] * 3 + [IN_VMEM] * 4 + [IN_...  3.09 us
    ppermute x3, waiting for transfers between devices, shards(): lax.ppermute(terms[k], GROUP, [(i, i ^ k) for i in range(4)]).astype(f32)  2.8 us
  transfers between devices with their start and end apart: 8, of which 7 were waited for; matrix products, arithmetic and copies ran while one was open for 0% of the time, Pallas kernels for 0%

profile of v5, /device:TPU:2, one launch (start us, length us, event | category | flops | bytes accessed | tf_op | source)
XLA Modules:
  0.0 94.7 jit_solution(7943053243149289801)
XLA Ops:
  0.0 0.0 copy-start
  0.0 1.2 %prepare.1 = (bf16[16,16,1024]{2,1,0:T(8,128)(2,1)S(1)}, bf16[8,24,128]{2,1,0:T(8,128)(2,1)S(1)}) custom-call(bf16[16,4096]{1,0:T(8,128)(2,1)} %orbitals_ref.1, bf16[16,1024]{1,0:T(8,128)(2,1)} %trial_ref.1, s32[2,1024]{1,0:T(2,128)} %pair_ref.1), custom_call_target="tpu_custom_call" | custom-call | tf_op jit(solution)/shard_map/prepare/pallas_call | solution.py:100
  1.2 25.1 %all_to_all.20 = bf16[16,16,1024]{2,1,0:T(8,128)(2,1)S(1)} all-to-all(bf16[16,16,1024]{2,1,0:T(8,128)(2,1)S(1)} %get-tuple-element.15), channel_id=1, replica_groups=mesh['yl'=2,'zh'=4,'zl'=2,'c'=2,'yh'=2,'x'=4] {'yl','zh','zl'}, dimensions={0} | all-to-all | bytes 1048576 | tf_op jit(solution)/shard_map/all_to_all | solution.py:30
  26.3 0.0 collective-permute-start
  26.3 2.3 %collective-permute-start.3 = (bf16[8,24,128]{2,1,0:T(8,128)(2,1)S(1)}, bf16[8,24,128]{2,1,0:T(8,128)(2,1)S(1)}, u32[]{:S(2)}, u32[]{:S(2)}) collective-permute-start(bf16[8,24,128]{2,1,0:T(8,128)(2,1)S(1)} %get-tuple-element.16.slots0_ref), channel_id=1, source_target_pairs={{0,144},{16,128},{128,16},{144,0},{1,145},{17,129},{129,17},{145,1... | collective-permute-start | bytes 147464 | tf_op jit(solution)/shard_map/ppermute | solution.py:317
  28.6 0.4 collective-permute-start.2
  29.0 0.8 collective-permute-start.1
  29.8 1.6 %collective-permute-done.3.slots3_ref = bf16[8,24,128]{2,1,0:T(8,128)(2,1)S(1)} collective-permute-done((bf16[8,24,128]{2,1,0:T(8,128)(2,1)S(1)}, bf16[8,24,128]{2,1,0:T(8,128)(2,1)S(1)}, u32[]{:S(2)}, u32[]{:S(2)}) %collective-permute-start.3) | collective-permute-done | bytes 49184 | tf_op jit(solution)/shard_map/ppermute | solution.py:317
  31.3 1.4 %collective-permute-done.2.slots2_ref = bf16[8,24,128]{2,1,0:T(8,128)(2,1)S(1)} collective-permute-done((bf16[8,24,128]{2,1,0:T(8,128)(2,1)S(1)}, bf16[8,24,128]{2,1,0:T(8,128)(2,1)S(1)}, u32[]{:S(2)}, u32[]{:S(2)}) %collective-permute-start.2) | collective-permute-done | bytes 49184 | tf_op jit(solution)/shard_map/ppermute | solution.py:317
  32.7 0.4 collective-permute-done.1.slots1_ref
  33.1 0.0 collective-permute-done.other_ref
  33.1 8.2 %density.1 = (bf16[8,1024,512]{2,1,0:T(8,128)(2,1)}, bf16[1024,1024]{1,0:T(8,128)(2,1)S(1)}, bf16[16,16,256]{2,1,0:T(8,128)(2,1)S(1)}, s32[37]{0:T(128)S(1)}) custom-call(s32[1]{0:T(128)} %bitcast.group_ref, s32[1]{0:T(128)} %bitcast.1.core_ref, bf16[256,1024]{1,0:T(8,128)(2,1)S(1)} %bitcast.13, bf16[256,1024]{1,0:T(8,128)(2,1)S(1)} %collective-permute-done.other_ref, ...), custom_call_target="tpu_custom_call" | custom-call | tf_op jit(solution)/shard_map/density/pallas_call | solution.py:214
  41.3 12.9 %all_to_all.21 = bf16[16,16,256]{2,1,0:T(8,128)(2,1)S(1)} all-to-all(bf16[16,16,256]{2,1,0:T(8,128)(2,1)S(1)} %get-tuple-element.18), channel_id=1, replica_groups=mesh['yl'=2,'zh'=4,'zl'=2,'c'=2,'yh'=2,'x'=4] {'zh','zl','c'}, dimensions={0} | all-to-all | bytes 262144 | tf_op jit(solution)/shard_map/all_to_all | solution.py:30
  54.3 16.1 %all_to_all.22 = bf16[32,16,256]{2,1,0:T(8,128)(2,1)S(1)} all-to-all(bf16[32,16,256]{2,1,0:T(8,128)(2,1)S(1)} %broadcast_in_dim.4), channel_id=1, replica_groups=mesh['yl'=2,'zh'=4,'zl'=2,'c'=2,'yh'=2,'x'=4] {'yl','zl','yh','x'}, dimensions={0} | all-to-all | bytes 524288 | tf_op jit(solution)/shard_map/all_to_all | solution.py:30
  70.4 0.1 collective-permute-start.4
  70.5 1.2 %collective-permute-done.4.other_ref = f32[2,16,256]{2,1,0:T(8,128)S(1)} collective-permute-done((f32[2,16,256]{2,1,0:T(8,128)S(1)}, f32[2,16,256]{2,1,0:T(8,128)S(1)}, u32[]{:S(2)}, u32[]{:S(2)}) %collective-permute-start.4) | collective-permute-done | bytes 32800 | tf_op jit(solution)/shard_map/ppermute | solution.py:325
  71.7 0.0 copy-done
  71.7 3.1 %direct_terms.1 = (bf16[8,16,128]{2,1,0:T(8,128)(2,1)S(1)}, bf16[8,16,128]{2,1,0:T(8,128)(2,1)S(1)}, bf16[8,16,128]{2,1,0:T(8,128)(2,1)S(1)}, bf16[8,16,128]{2,1,0:T(8,128)(2,1)S(1)}) custom-call(s32[1]{0:T(128)} %bitcast.group_ref, s32[1]{0:T(128)} %bitcast.1.core_ref, s32[37]{0:T(128)S(1)} %get-tuple-element.17.list_ref, ...), custom_call_target="tpu_custom_call" | custom-call | tf_op jit(solution)/shard_map/direct_terms/pallas_call | solution.py:294
  74.8 0.8 collective-permute-start.5
  75.6 0.7 collective-permute-start.6
  76.4 2.0 %collective-permute-start.7 = (bf16[8,16,128]{2,1,0:T(8,128)(2,1)S(1)}, bf16[8,16,128]{2,1,0:T(8,128)(2,1)S(1)}, u32[]{:S(2)}, u32[]{:S(2)}) collective-permute-start(bf16[8,16,128]{2,1,0:T(8,128)(2,1)S(1)} %get-tuple-element.24), channel_id=1, source_target_pairs={{0,144},{16,128},{128,16},{144,0},{1,145},{17,129},{129,17},{145,1... | collective-permute-start | bytes 98312 | tf_op jit(solution)/shard_map/ppermute | solution.py:329
  78.4 0.4 collective-permute-done.5
  78.8 0.7 collective-permute-done.6
  79.5 1.6 %collective-permute-done.7 = bf16[8,16,128]{2,1,0:T(8,128)(2,1)S(1)} collective-permute-done((bf16[8,16,128]{2,1,0:T(8,128)(2,1)S(1)}, bf16[8,16,128]{2,1,0:T(8,128)(2,1)S(1)}, u32[]{:S(2)}, u32[]{:S(2)}) %collective-permute-start.7) | collective-permute-done | bytes 32800 | tf_op jit(solution)/shard_map/ppermute | solution.py:329
  81.2 12.7 %all_to_all.23 = bf16[8,8,16,128]{3,2,1,0:T(8,128)(2,1)S(1)} all-to-all(bf16[8,8,16,128]{3,2,1,0:T(8,128)(2,1)S(1)} %broadcast_in_dim.5), channel_id=1, replica_groups=mesh['yl'=2,'zh'=4,'zl'=2,'c'=2,'yh'=2,'x'=4] {'yh','x'}, dimensions={0} | all-to-all | bytes 524288 | tf_op jit(solution)/shard_map/all_to_all | solution.py:30
  94.0 0.6 copy_bitcast_fusion
  (6 shorter events, 0.2 us)
Async XLA Ops:
  0.0 71.7 %copy-start = (f32[1024]{0:T(1024)S(1)}, f32[1024]{0:T(1024)}, u32[]{:S(2)}) copy-start(f32[1024]{0:T(1024)} %param.7) | copy-start | bytes 12292
  26.3 6.8 %collective-permute-start = (bf16[256,1024]{1,0:T(8,128)(2,1)S(1)}, bf16[256,1024]{1,0:T(8,128)(2,1)S(1)}, u32[]{:S(2)}, u32[]{:S(2)}) collective-permute-start(bf16[256,1024]{1,0:T(8,128)(2,1)S(1)} %bitcast.12), channel_id=1, source_target_pairs={{0,8},{8,0},{1,9},{9,1},{2,10},{10,2},{3,11},{11,3},{4,12},{12,4},... | collective-permute-start | bytes 1572872 | tf_op jit(solution)/shard_map/ppermute | solution.py:320
  26.3 5.1 %collective-permute-start.3 = (bf16[8,24,128]{2,1,0:T(8,128)(2,1)S(1)}, bf16[8,24,128]{2,1,0:T(8,128)(2,1)S(1)}, u32[]{:S(2)}, u32[]{:S(2)}) collective-permute-start(bf16[8,24,128]{2,1,0:T(8,128)(2,1)S(1)} %get-tuple-element.16.slots0_ref), channel_id=1, source_target_pairs={{0,144},{16,128},{128,16},{144,0},{1,145},{17,129},{129,17},{145,1... | collective-permute-start | bytes 147464 | tf_op jit(solution)/shard_map/ppermute | solution.py:317
  28.6 4.1 %collective-permute-start.2 = (bf16[8,24,128]{2,1,0:T(8,128)(2,1)S(1)}, bf16[8,24,128]{2,1,0:T(8,128)(2,1)S(1)}, u32[]{:S(2)}, u32[]{:S(2)}) collective-permute-start(bf16[8,24,128]{2,1,0:T(8,128)(2,1)S(1)} %get-tuple-element.16.slots0_ref), channel_id=1, source_target_pairs={{0,128},{16,144},{128,0},{144,16},{1,129},{17,145},{129,1},{145,17... | collective-permute-start | bytes 147464 | tf_op jit(solution)/shard_map/ppermute | solution.py:317
  29.0 4.1 %collective-permute-start.1 = (bf16[8,24,128]{2,1,0:T(8,128)(2,1)S(1)}, bf16[8,24,128]{2,1,0:T(8,128)(2,1)S(1)}, u32[]{:S(2)}, u32[]{:S(2)}) collective-permute-start(bf16[8,24,128]{2,1,0:T(8,128)(2,1)S(1)} %get-tuple-element.16.slots0_ref), channel_id=1, source_target_pairs={{0,16},{16,0},{128,144},{144,128},{1,17},{17,1},{129,145},{145,129... | collective-permute-start | bytes 147464 | tf_op jit(solution)/shard_map/ppermute | solution.py:317
  70.4 1.3 %collective-permute-start.4 = (f32[2,16,256]{2,1,0:T(8,128)S(1)}, f32[2,16,256]{2,1,0:T(8,128)S(1)}, u32[]{:S(2)}, u32[]{:S(2)}) collective-permute-start(f32[2,16,256]{2,1,0:T(8,128)S(1)} %convert_reduce_fusion.mine_ref), channel_id=1, source_target_pairs={{0,8},{8,0},{1,9},{9,1},{2,10},{10,2},{3,11},{11,3},{4,12},{12,4},... | collective-permute-start | bytes 98312 | tf_op jit(solution)/shard_map/ppermute | solution.py:325
  74.8 4.0 %collective-permute-start.5 = (bf16[8,16,128]{2,1,0:T(8,128)(2,1)S(1)}, bf16[8,16,128]{2,1,0:T(8,128)(2,1)S(1)}, u32[]{:S(2)}, u32[]{:S(2)}) collective-permute-start(bf16[8,16,128]{2,1,0:T(8,128)(2,1)S(1)} %get-tuple-element.22), channel_id=1, source_target_pairs={{0,16},{16,0},{128,144},{144,128},{1,17},{17,1},{129,145},{145,129... | collective-permute-start | bytes 98312 | tf_op jit(solution)/shard_map/ppermute | solution.py:329
  75.6 3.9 %collective-permute-start.6 = (bf16[8,16,128]{2,1,0:T(8,128)(2,1)S(1)}, bf16[8,16,128]{2,1,0:T(8,128)(2,1)S(1)}, u32[]{:S(2)}, u32[]{:S(2)}) collective-permute-start(bf16[8,16,128]{2,1,0:T(8,128)(2,1)S(1)} %get-tuple-element.23), channel_id=1, source_target_pairs={{0,128},{16,144},{128,0},{144,16},{1,129},{17,145},{129,1},{145,17... | collective-permute-start | bytes 98312 | tf_op jit(solution)/shard_map/ppermute | solution.py:329
  76.4 4.8 %collective-permute-start.7 = (bf16[8,16,128]{2,1,0:T(8,128)(2,1)S(1)}, bf16[8,16,128]{2,1,0:T(8,128)(2,1)S(1)}, u32[]{:S(2)}, u32[]{:S(2)}) collective-permute-start(bf16[8,16,128]{2,1,0:T(8,128)(2,1)S(1)} %get-tuple-element.24), channel_id=1, source_target_pairs={{0,144},{16,128},{128,16},{144,0},{1,145},{17,129},{129,17},{145,1... | collective-permute-start | bytes 98312 | tf_op jit(solution)/shard_map/ppermute | solution.py:329

commit v6 on v5

--- a/solution.py
+++ b/solution.py
@@ -12,11 +12,11 @@
 SLAB = ("yh", "x")
 GROUP = ("yl", "zl")
 SOURCES = ("yl", "zh", "zl")
-COLUMN = ("zh", "zl", "c")
-WIDE = ("yl", "zl", "yh", "x")
+FAR = ("zh", "yh", "x")
 
 NB = 16
 BLOCK = 128
+EIGHTH = 128
 ROWS = 24
 TAKE = 4
 
@@ -28,6 +28,14 @@
 
 def exchange(blocks, axes):
     return lax.all_to_all(blocks, axes, 0, 0, tiled=True)
+
+
+def swapped(value):
+    return lax.ppermute(value, "c", [(0, 1), (1, 0)])
+
+
+def passed(value, k):
+    return lax.ppermute(value, GROUP, [(i, i ^ k) for i in range(4)])
 
 
 def summed(blocks):
@@ -128,11 +136,13 @@
     all_pot_ref,
     kept_ref,
     pot_ref,
-    quarters_ref,
+    keep_ref,
+    give_ref,
     list_ref,
     slots_ref,
     phit_ref,
     fieldt_ref,
+    pieces_ref,
     dens_ref,
     sem,
     sems,
@@ -194,10 +204,12 @@
     upper = fieldt.astype(bf16)
     lower = (fieldt - upper.astype(f32)).astype(bf16)
     proj = folded(dot(pot_ref[...], jnp.concatenate([upper, lower], axis=1)).T).astype(bf16)
-    width = quarters_ref.shape[2]
-    for to in range(16):
-        quarter = (to % 2) * 2 + (to // 2) % 2
-        quarters_ref[to] = proj[:, quarter * width : (quarter + 1) * width]
+    for piece in range(8):
+        pieces_ref[piece] = proj[:, piece * EIGHTH : (piece + 1) * EIGHTH]
+    core = core_ref[0]
+    for k in range(4):
+        keep_ref[k] = pieces_ref[core * 4 + (group ^ k)]
+        give_ref[k] = pieces_ref[(1 - core) * 4 + (group ^ k)]
 
     def kept(turn, unused):
         pltpu.make_async_copy(dens_ref.at[turn], kept_ref.at[turn], sems.at[turn]).wait()
@@ -214,17 +226,19 @@
     return pl.pallas_call(
         density_body,
         in_specs=[IN_SMEM] * 2 + [IN_VMEM] * 6 + [IN_HBM],
-        out_specs=[IN_HBM, IN_VMEM, IN_VMEM, IN_SMEM],
+        out_specs=[IN_HBM, IN_VMEM, IN_VMEM, IN_VMEM, IN_SMEM],
         out_shape=[
             pltpu.HBM((turns, points, TAKE * BLOCK), bf16),
             pltpu.VMEM((neig, points), bf16),
-            pltpu.VMEM((16, NB, neig // 4), bf16),
+            pltpu.VMEM((4, NB, EIGHTH), bf16),
+            pltpu.VMEM((4, NB, EIGHTH), bf16),
             jax.ShapeDtypeStruct((1 + blocks + TAKE,), jnp.int32),
         ],
         scratch_shapes=[
             pltpu.VMEM((blocks, ROWS, BLOCK), bf16),
             pltpu.VMEM((points, 2 * half), bf16),
             pltpu.VMEM((points, NB), f32),
+            pltpu.VMEM((8, NB, EIGHTH), bf16),
             pltpu.VMEM((turns, points, TAKE * BLOCK), bf16),
             pltpu.SemaphoreType.DMA(()),
             pltpu.SemaphoreType.DMA((turns,)),
@@ -238,8 +252,10 @@
     group_ref,
     core_ref,
     list_ref,
-    mine_ref,
-    other_ref,
+    both0_ref,
+    both1_ref,
+    both2_ref,
+    both3_ref,
     screening_ref,
     pot_ref,
     kept_ref,
@@ -247,6 +263,7 @@
     out1_ref,
     out2_ref,
     out3_ref,
+    pieces_ref,
     terms_ref,
     split_ref,
     dens_ref,
@@ -261,14 +278,13 @@
 
     lax.fori_loop(0, turns, fetch, 0)
     terms_ref[...] = jnp.zeros_like(terms_ref)
-    half = mine_ref.shape[0] * mine_ref.shape[2]
-    total = jnp.zeros((NB, pot_ref.shape[1]), f32)
-    for ref, core in ((mine_ref, core_ref[0]), (other_ref, 1 - core_ref[0])):
-        scales = jnp.where(core == 0, screening_ref[:, :half], screening_ref[:, half:])
-        screened = jnp.concatenate([ref[0], ref[1]], axis=1) * scales
-        rows = pot_ref[pl.ds(pl.multiple_of(core * half, half), half), :]
-        total += folded(dot(in_two(screened), rows))
-    split_ref[...] = in_two(total)
+    core = core_ref[0]
+    for k, ref in enumerate((both0_ref, both1_ref, both2_ref, both3_ref)):
+        pieces_ref[core * 4 + (group_ref[0] ^ k)] = ref[0]
+        pieces_ref[(1 - core) * 4 + (group_ref[0] ^ k)] = ref[1]
+    projected = jnp.concatenate([pieces_ref[piece] for piece in range(8)], axis=1)
+    screened = projected * screening_ref[...]
+    split_ref[...] = in_two(folded(dot(in_two(screened), pot_ref[...])))
     each = out0_ref.shape[0]
     own = group_ref[0] * each
 
@@ -289,14 +305,15 @@
         ref[...] = terms_ref[k * each : (k + 1) * each]
 
 
-def direct_terms(group, core, live, mine, other, screening, pot, dens):
+def direct_terms(group, core, live, both, screening, pot, dens):
     blocks = dens.shape[0] * TAKE
     return pl.pallas_call(
         direct_body,
-        in_specs=[IN_SMEM] * 3 + [IN_VMEM] * 4 + [IN_HBM],
+        in_specs=[IN_SMEM] * 3 + [IN_VMEM] * 6 + [IN_HBM],
         out_specs=[IN_VMEM] * 4,
         out_shape=[pltpu.VMEM((blocks // 4, NB, BLOCK), bf16)] * 4,
         scratch_shapes=[
+            pltpu.VMEM((8, NB, EIGHTH), f32),
             pltpu.VMEM((blocks, NB, BLOCK), bf16),
             pltpu.VMEM((2 * NB, pot.shape[1]), bf16),
             pltpu.VMEM(dens.shape, bf16),
@@ -304,7 +321,7 @@
         ],
         compiler_params=pltpu.CompilerParams(vmem_limit_bytes=LIMIT),
         name="direct_terms",
-    )(group, core, live, *vmem(mine, other, screening, pot), *hbm(dens))
+    )(group, core, live, *vmem(*both, screening, pot), *hbm(dens))
 
 
 def shards(orbitals, eigenpotentials, screening, trial_vectors, pair_index):
@@ -314,19 +331,22 @@
     sent, own_slots = prepare(orbitals, trial_vectors, pair_index)
     slots = [own_slots]
     for k in range(1, 4):
-        slots.append(lax.ppermute(own_slots, GROUP, [(i, i ^ k) for i in range(4)]))
+        slots.append(passed(own_slots, k))
     mine = exchange(sent, SOURCES)
     mine = mine.reshape(-1, mine.shape[2])
-    other = lax.ppermute(mine, "c", [(0, 1), (1, 0)])
-    dens, pot, quarters, live = density(group, core, mine, other, slots, eigenpotentials)
-    column = summed(exchange(quarters, COLUMN)).astype(bf16)
-    wide = exchange(copies(column, 32), WIDE)
-    part = jnp.sum(wide.reshape(2, 2, 8, *column.shape).astype(f32), axis=(0, 2))
-    apart = lax.ppermute(part, "c", [(0, 1), (1, 0)])
-    terms = direct_terms(group, core, live, part, apart, scales, pot, dens)
+    other = swapped(mine)
+    dens, pot, keep, give, live = density(group, core, mine, other, slots, eigenpotentials)
+    half = (keep.astype(f32) + swapped(give).astype(f32)).astype(bf16)
+    eighth = half[0].astype(f32)
+    for k in range(1, 4):
+        eighth += passed(half[k], k).astype(f32)
+    whole = summed(exchange(copies(eighth.astype(bf16), 32), FAR))
+    pair = jnp.stack([whole, swapped(whole)])
+    both = [pair] + [passed(pair, k) for k in range(1, 4)]
+    terms = direct_terms(group, core, live, both, scales, pot, dens)
     owner = terms[0].astype(f32)
     for k in range(1, 4):
-        owner += lax.ppermute(terms[k], GROUP, [(i, i ^ k) for i in range(4)]).astype(f32)
+        owner += passed(terms[k], k).astype(f32)
     owner = owner.astype(bf16)
     direct = summed(exchange(copies(owner, 8), SLAB))
     return direct.transpose(1, 0, 2).reshape(NB, -1)

time: 95 us -> 100 us (1.053)
  blocking collectives: 66.8 us -> 57.4 us
  starting transfers between devices: 7.16 us -> 14.6 us
  waiting for transfers between devices: 7.3 us -> 14.3 us
    all_to_all x4 -> x3, blocking collectives: 66.8 us -> 57.4 us  [exchange(): return lax.all_to_all(blocks, axes, 0, 0, tiled=True)]
    ppermute x8 -> x15, starting transfers between devices: 7.16 us -> 14.6 us  [the longest x12 14.1 us: passed(): return lax.ppermute(value, GROUP, [(i, i ^ k) for i in range(4)])]
    ppermute x8 -> x15, waiting for transfers between devices: 7.3 us -> 14.3 us  [the longest x12 12.3 us: passed(): return lax.ppermute(value, GROUP, [(i, i ^ k) for i in range(4)])]
  transfers between devices with their start and end apart: 8 -> 15, of which waited for: 7 -> 13; matrix products, arithmetic and copies ran while one was open for 0% -> 0% of each run, Pallas kernels for 0% -> 0%
where the time goes in v6:
time: 100 us; the launch traced here: 99.7 us
  blocking collectives  57.4 us (57%)
  starting transfers between devices  14.6 us (15%)
  waiting for transfers between devices  14.3 us (14%)
  Pallas kernels  12.5 us (12%)
    all_to_all x3, blocking collectives, exchange(): return lax.all_to_all(blocks, axes, 0, 0, tiled=True)  57.4 us
    ppermute x12, starting transfers between devices, passed(): return lax.ppermute(value, GROUP, [(i, i ^ k) for i in range(4)])  14.1 us
    ppermute x12, waiting for transfers between devices, passed(): return lax.ppermute(value, GROUP, [(i, i ^ k) for i in range(4)])  12.3 us
    pallas_call x1, Pallas kernels, density(): pl.pallas_call(density_body, in_specs=[IN_SMEM] * 2 + [IN_VMEM] * 6 + [IN...  8.23 us
    pallas_call x1, Pallas kernels, direct_terms(): pl.pallas_call(direct_body, in_specs=[IN_SMEM] * 3 + [IN_VMEM] * 6 + [IN_...  3.09 us
    ppermute x3, waiting for transfers between devices, swapped(): return lax.ppermute(value, 'c', [(0, 1), (1, 0)])  2.01 us
  transfers between devices with their start and end apart: 15, of which 13 were waited for; matrix products, arithmetic and copies ran while one was open for 0% of the time, Pallas kernels for 0%

profile of v6, /device:TPU:2, one launch (start us, length us, event | category | flops | bytes accessed | tf_op | source)
XLA Modules:
  0.0 99.7 jit_solution(7842891285465164737)
XLA Ops:
  0.0 0.0 copy-start
  0.0 1.2 %prepare.1 = (bf16[16,16,1024]{2,1,0:T(8,128)(2,1)S(1)}, bf16[8,24,128]{2,1,0:T(8,128)(2,1)S(1)}) custom-call(bf16[16,4096]{1,0:T(8,128)(2,1)} %orbitals_ref.1, bf16[16,1024]{1,0:T(8,128)(2,1)} %trial_ref.1, s32[2,1024]{1,0:T(2,128)} %pair_ref.1), custom_call_target="tpu_custom_call" | custom-call | tf_op jit(solution)/shard_map/prepare/pallas_call | solution.py:108
  1.2 25.1 %all_to_all.15 = bf16[16,16,1024]{2,1,0:T(8,128)(2,1)S(1)} all-to-all(bf16[16,16,1024]{2,1,0:T(8,128)(2,1)S(1)} %get-tuple-element.16), channel_id=1, replica_groups=mesh['yl'=2,'zh'=4,'zl'=2,'c'=2,'yh'=2,'x'=4] {'yl','zh','zl'}, dimensions={0} | all-to-all | bytes 1048576 | tf_op jit(solution)/shard_map/all_to_all | solution.py:30
  26.3 0.0 collective-permute-start
  26.3 2.3 %collective-permute-start.3 = (bf16[8,24,128]{2,1,0:T(8,128)(2,1)S(1)}, bf16[8,24,128]{2,1,0:T(8,128)(2,1)S(1)}, u32[]{:S(2)}, u32[]{:S(2)}) collective-permute-start(bf16[8,24,128]{2,1,0:T(8,128)(2,1)S(1)} %get-tuple-element.17.slots0_ref), channel_id=1, source_target_pairs={{0,144},{16,128},{128,16},{144,0},{1,145},{17,129},{129,17},{145,1... | collective-permute-start | bytes 147464 | tf_op jit(solution)/shard_map/ppermute | solution.py:38
  28.6 0.4 collective-permute-start.2
  29.0 0.8 collective-permute-start.1
  29.8 1.6 %collective-permute-done.3.slots3_ref = bf16[8,24,128]{2,1,0:T(8,128)(2,1)S(1)} collective-permute-done((bf16[8,24,128]{2,1,0:T(8,128)(2,1)S(1)}, bf16[8,24,128]{2,1,0:T(8,128)(2,1)S(1)}, u32[]{:S(2)}, u32[]{:S(2)}) %collective-permute-start.3) | collective-permute-done | bytes 49184 | tf_op jit(solution)/shard_map/ppermute | solution.py:38
  31.3 1.4 %collective-permute-done.2.slots2_ref = bf16[8,24,128]{2,1,0:T(8,128)(2,1)S(1)} collective-permute-done((bf16[8,24,128]{2,1,0:T(8,128)(2,1)S(1)}, bf16[8,24,128]{2,1,0:T(8,128)(2,1)S(1)}, u32[]{:S(2)}, u32[]{:S(2)}) %collective-permute-start.2) | collective-permute-done | bytes 49184 | tf_op jit(solution)/shard_map/ppermute | solution.py:38
  32.7 0.4 collective-permute-done.1.slots1_ref
  33.1 0.0 collective-permute-done.other_ref
  33.1 8.2 %density.1 = (bf16[8,1024,512]{2,1,0:T(8,128)(2,1)}, bf16[1024,1024]{1,0:T(8,128)(2,1)S(1)}, bf16[4,16,128]{2,1,0:T(8,128)(2,1)S(1)}, bf16[4,16,128]{2,1,0:T(8,128)(2,1)S(1)}, s32[37]{0:T(128)S(1)}) custom-call(s32[1]{0:T(128)} %bitcast.group_ref, s32[1]{0:T(128)} %bitcast.1.core_ref, bf16[256,1024]{1,0:T(8,128)(2,1)S(1)} %bitcast.24, ...), custom_call_target="tpu_custom_call" | custom-call | tf_op jit(solution)/shard_map/density/pallas_call | solution.py:226
  41.3 0.4 collective-permute-start.4
  41.7 0.8 collective-permute-done.4
  42.6 1.6 %collective-permute-start.5 = (bf16[16,128]{1,0:T(8,128)(2,1)S(1)}, bf16[16,128]{1,0:T(8,128)(2,1)S(1)}, u32[]{:S(2)}, u32[]{:S(2)}) collective-permute-start(bf16[16,128]{1,0:T(8,128)(2,1)S(1)} %get-tuple-element.27), channel_id=1, source_target_pairs={{0,16},{16,0},{128,144},{144,128},{1,17},{17,1},{129,145},{145,129... | collective-permute-start | bytes 12296 | tf_op jit(solution)/shard_map/ppermute | solution.py:38
  44.2 1.6 %collective-permute-start.7 = (bf16[16,128]{1,0:T(8,128)(2,1)S(1)}, bf16[16,128]{1,0:T(8,128)(2,1)S(1)}, u32[]{:S(2)}, u32[]{:S(2)}) collective-permute-start(bf16[16,128]{1,0:T(8,128)(2,1)S(1)} %get-tuple-element.28), channel_id=1, source_target_pairs={{0,144},{16,128},{128,16},{144,0},{1,145},{17,129},{129,17},{145,1... | collective-permute-start | bytes 12296 | tf_op jit(solution)/shard_map/ppermute | solution.py:38
  45.8 0.4 collective-permute-start.6
  46.2 0.1 collective-permute-done.5
  46.3 2.4 %collective-permute-done.7 = bf16[16,128]{1,0:T(8,128)(2,1)S(1)} collective-permute-done((bf16[16,128]{1,0:T(8,128)(2,1)S(1)}, bf16[16,128]{1,0:T(8,128)(2,1)S(1)}, u32[]{:S(2)}, u32[]{:S(2)}) %collective-permute-start.7) | collective-permute-done | bytes 4128 | tf_op jit(solution)/shard_map/ppermute | solution.py:38
  48.7 0.7 collective-permute-done.6
  49.4 20.3 %all_to_all.16 = bf16[32,16,128]{2,1,0:T(8,128)(2,1)S(1)} all-to-all(bf16[32,16,128]{2,1,0:T(8,128)(2,1)S(1)} %broadcast_in_dim.4), channel_id=1, replica_groups=mesh['yl'=2,'zh'=4,'zl'=2,'c'=2,'yh'=2,'x'=4] {'zh','yh','x'}, dimensions={0} | all-to-all | bytes 262144 | tf_op jit(solution)/shard_map/all_to_all | solution.py:30
  69.8 0.1 collective-permute-start.8
  69.9 1.2 %collective-permute-done.8 = f32[16,128]{1,0:T(8,128)S(1)} collective-permute-done((f32[16,128]{1,0:T(8,128)S(1)}, f32[16,128]{1,0:T(8,128)S(1)}, u32[]{:S(2)}, u32[]{:S(2)}) %collective-permute-start.8) | collective-permute-done | bytes 8224 | tf_op jit(solution)/shard_map/ppermute | solution.py:34
  71.1 0.4 collective-permute-start.11
  71.5 1.8 %collective-permute-start.10 = (f32[2,16,128]{2,1,0:T(8,128)S(1)}, f32[2,16,128]{2,1,0:T(8,128)S(1)}, u32[]{:S(2)}, u32[]{:S(2)}) collective-permute-start(f32[2,16,128]{2,1,0:T(8,128)S(1)} %pad_maximum_fusion.both0_ref), channel_id=1, source_target_pairs={{0,128},{16,144},{128,0},{144,16},{1,129},{17,145},{129,1},{145,17... | collective-permute-start | bytes 49160 | tf_op jit(solution)/shard_map/ppermute | solution.py:38
  73.3 1.3 %collective-permute-start.9 = (f32[2,16,128]{2,1,0:T(8,128)S(1)}, f32[2,16,128]{2,1,0:T(8,128)S(1)}, u32[]{:S(2)}, u32[]{:S(2)}) collective-permute-start(f32[2,16,128]{2,1,0:T(8,128)S(1)} %pad_maximum_fusion.both0_ref), channel_id=1, source_target_pairs={{0,16},{16,0},{128,144},{144,128},{1,17},{17,1},{129,145},{145,129... | collective-permute-start | bytes 49160 | tf_op jit(solution)/shard_map/ppermute | solution.py:38
  74.5 1.1 %collective-permute-done.11.both3_ref = f32[2,16,128]{2,1,0:T(8,128)S(1)} collective-permute-done((f32[2,16,128]{2,1,0:T(8,128)S(1)}, f32[2,16,128]{2,1,0:T(8,128)S(1)}, u32[]{:S(2)}, u32[]{:S(2)}) %collective-permute-start.11) | collective-permute-done | bytes 16416 | tf_op jit(solution)/shard_map/ppermute | solution.py:38
  75.7 0.0 collective-permute-done.10.both2_ref
  75.7 1.3 %collective-permute-done.9.both1_ref = f32[2,16,128]{2,1,0:T(8,128)S(1)} collective-permute-done((f32[2,16,128]{2,1,0:T(8,128)S(1)}, f32[2,16,128]{2,1,0:T(8,128)S(1)}, u32[]{:S(2)}, u32[]{:S(2)}) %collective-permute-start.9) | collective-permute-done | bytes 16416 | tf_op jit(solution)/shard_map/ppermute | solution.py:38
  77.0 0.0 copy-done
  77.0 3.1 %direct_terms.1 = (bf16[8,16,128]{2,1,0:T(8,128)(2,1)S(1)}, bf16[8,16,128]{2,1,0:T(8,128)(2,1)S(1)}, bf16[8,16,128]{2,1,0:T(8,128)(2,1)S(1)}, bf16[8,16,128]{2,1,0:T(8,128)(2,1)S(1)}) custom-call(s32[1]{0:T(128)} %bitcast.group_ref, s32[1]{0:T(128)} %bitcast.1.core_ref, s32[37]{0:T(128)S(1)} %get-tuple-element.18.list_ref, ...), custom_call_target="tpu_custom_call" | custom-call | tf_op jit(solution)/shard_map/direct_terms/pallas_call | solution.py:310
  80.1 1.3 %collective-permute-start.12 = (bf16[8,16,128]{2,1,0:T(8,128)(2,1)S(1)}, bf16[8,16,128]{2,1,0:T(8,128)(2,1)S(1)}, u32[]{:S(2)}, u32[]{:S(2)}) collective-permute-start(bf16[8,16,128]{2,1,0:T(8,128)(2,1)S(1)} %get-tuple-element.24), channel_id=1, source_target_pairs={{0,16},{16,0},{128,144},{144,128},{1,17},{17,1},{129,145},{145,129... | collective-permute-start | bytes 98312 | tf_op jit(solution)/shard_map/ppermute | solution.py:38
  81.5 0.7 collective-permute-start.13
  82.2 1.5 %collective-permute-start.14 = (bf16[8,16,128]{2,1,0:T(8,128)(2,1)S(1)}, bf16[8,16,128]{2,1,0:T(8,128)(2,1)S(1)}, u32[]{:S(2)}, u32[]{:S(2)}) collective-permute-start(bf16[8,16,128]{2,1,0:T(8,128)(2,1)S(1)} %get-tuple-element.26), channel_id=1, source_target_pairs={{0,144},{16,128},{128,16},{144,0},{1,145},{17,129},{129,17},{145,1... | collective-permute-start | bytes 98312 | tf_op jit(solution)/shard_map/ppermute | solution.py:38
  83.7 0.5 collective-permute-done.12
  84.2 1.2 %collective-permute-done.13 = bf16[8,16,128]{2,1,0:T(8,128)(2,1)S(1)} collective-permute-done((bf16[8,16,128]{2,1,0:T(8,128)(2,1)S(1)}, bf16[8,16,128]{2,1,0:T(8,128)(2,1)S(1)}, u32[]{:S(2)}, u32[]{:S(2)}) %collective-permute-start.13) | collective-permute-done | bytes 32800 | tf_op jit(solution)/shard_map/ppermute | solution.py:38
  85.4 1.6 %collective-permute-done.14 = bf16[8,16,128]{2,1,0:T(8,128)(2,1)S(1)} collective-permute-done((bf16[8,16,128]{2,1,0:T(8,128)(2,1)S(1)}, bf16[8,16,128]{2,1,0:T(8,128)(2,1)S(1)}, u32[]{:S(2)}, u32[]{:S(2)}) %collective-permute-start.14) | collective-permute-done | bytes 32800 | tf_op jit(solution)/shard_map/ppermute | solution.py:38
  87.1 12.0 %all_to_all.17 = bf16[8,8,16,128]{3,2,1,0:T(8,128)(2,1)S(1)} all-to-all(bf16[8,8,16,128]{3,2,1,0:T(8,128)(2,1)S(1)} %broadcast_in_dim.5), channel_id=1, replica_groups=mesh['yl'=2,'zh'=4,'zl'=2,'c'=2,'yh'=2,'x'=4] {'yh','x'}, dimensions={0} | all-to-all | bytes 524288 | tf_op jit(solution)/shard_map/all_to_all | solution.py:30
  99.1 0.6 copy_bitcast_fusion
  (9 shorter events, 0.2 us)
Async XLA Ops:
  0.0 77.0 %copy-start = (f32[1024]{0:T(1024)S(1)}, f32[1024]{0:T(1024)}, u32[]{:S(2)}) copy-start(f32[1024]{0:T(1024)} %param.7) | copy-start | bytes 12292
  26.3 6.8 %collective-permute-start = (bf16[256,1024]{1,0:T(8,128)(2,1)S(1)}, bf16[256,1024]{1,0:T(8,128)(2,1)S(1)}, u32[]{:S(2)}, u32[]{:S(2)}) collective-permute-start(bf16[256,1024]{1,0:T(8,128)(2,1)S(1)} %bitcast.23), channel_id=1, source_target_pairs={{0,8},{8,0},{1,9},{9,1},{2,10},{10,2},{3,11},{11,3},{4,12},{12,4},... | collective-permute-start | bytes 1572872 | tf_op jit(solution)/shard_map/ppermute | solution.py:34
  26.3 5.1 %collective-permute-start.3 = (bf16[8,24,128]{2,1,0:T(8,128)(2,1)S(1)}, bf16[8,24,128]{2,1,0:T(8,128)(2,1)S(1)}, u32[]{:S(2)}, u32[]{:S(2)}) collective-permute-start(bf16[8,24,128]{2,1,0:T(8,128)(2,1)S(1)} %get-tuple-element.17.slots0_ref), channel_id=1, source_target_pairs={{0,144},{16,128},{128,16},{144,0},{1,145},{17,129},{129,17},{145,1... | collective-permute-start | bytes 147464 | tf_op jit(solution)/shard_map/ppermute | solution.py:38
  28.6 4.1 %collective-permute-start.2 = (bf16[8,24,128]{2,1,0:T(8,128)(2,1)S(1)}, bf16[8,24,128]{2,1,0:T(8,128)(2,1)S(1)}, u32[]{:S(2)}, u32[]{:S(2)}) collective-permute-start(bf16[8,24,128]{2,1,0:T(8,128)(2,1)S(1)} %get-tuple-element.17.slots0_ref), channel_id=1, source_target_pairs={{0,128},{16,144},{128,0},{144,16},{1,129},{17,145},{129,1},{145,17... | collective-permute-start | bytes 147464 | tf_op jit(solution)/shard_map/ppermute | solution.py:38
  29.0 4.1 %collective-permute-start.1 = (bf16[8,24,128]{2,1,0:T(8,128)(2,1)S(1)}, bf16[8,24,128]{2,1,0:T(8,128)(2,1)S(1)}, u32[]{:S(2)}, u32[]{:S(2)}) collective-permute-start(bf16[8,24,128]{2,1,0:T(8,128)(2,1)S(1)} %get-tuple-element.17.slots0_ref), channel_id=1, source_target_pairs={{0,16},{16,0},{128,144},{144,128},{1,17},{17,1},{129,145},{145,129... | collective-permute-start | bytes 147464 | tf_op jit(solution)/shard_map/ppermute | solution.py:38
  41.3 1.3 %collective-permute-start.4 = (bf16[4,16,128]{2,1,0:T(8,128)(2,1)S(1)}, bf16[4,16,128]{2,1,0:T(8,128)(2,1)S(1)}, u32[]{:S(2)}, u32[]{:S(2)}) collective-permute-start(bf16[4,16,128]{2,1,0:T(8,128)(2,1)S(1)} %get-tuple-element.20), channel_id=1, source_target_pairs={{0,8},{8,0},{1,9},{9,1},{2,10},{10,2},{3,11},{11,3},{4,12},{12,4},... | collective-permute-start | bytes 49160 | tf_op jit(solution)/shard_map/ppermute | solution.py:34
  42.6 3.7 %collective-permute-start.5 = (bf16[16,128]{1,0:T(8,128)(2,1)S(1)}, bf16[16,128]{1,0:T(8,128)(2,1)S(1)}, u32[]{:S(2)}, u32[]{:S(2)}) collective-permute-start(bf16[16,128]{1,0:T(8,128)(2,1)S(1)} %get-tuple-element.27), channel_id=1, source_target_pairs={{0,16},{16,0},{128,144},{144,128},{1,17},{17,1},{129,145},{145,129... | collective-permute-start | bytes 12296 | tf_op jit(solution)/shard_map/ppermute | solution.py:38
  44.2 4.5 %collective-permute-start.7 = (bf16[16,128]{1,0:T(8,128)(2,1)S(1)}, bf16[16,128]{1,0:T(8,128)(2,1)S(1)}, u32[]{:S(2)}, u32[]{:S(2)}) collective-permute-start(bf16[16,128]{1,0:T(8,128)(2,1)S(1)} %get-tuple-element.28), channel_id=1, source_target_pairs={{0,144},{16,128},{128,16},{144,0},{1,145},{17,129},{129,17},{145,1... | collective-permute-start | bytes 12296 | tf_op jit(solution)/shard_map/ppermute | solution.py:38
  45.8 3.6 %collective-permute-start.6 = (bf16[16,128]{1,0:T(8,128)(2,1)S(1)}, bf16[16,128]{1,0:T(8,128)(2,1)S(1)}, u32[]{:S(2)}, u32[]{:S(2)}) collective-permute-start(bf16[16,128]{1,0:T(8,128)(2,1)S(1)} %get-tuple-element.29), channel_id=1, source_target_pairs={{0,128},{16,144},{128,0},{144,16},{1,129},{17,145},{129,1},{145,17... | collective-permute-start | bytes 12296 | tf_op jit(solution)/shard_map/ppermute | solution.py:38
  69.8 1.3 %collective-permute-start.8 = (f32[16,128]{1,0:T(8,128)S(1)}, f32[16,128]{1,0:T(8,128)S(1)}, u32[]{:S(2)}, u32[]{:S(2)}) collective-permute-start(f32[16,128]{1,0:T(8,128)S(1)} %convert_reduce_fusion.1), channel_id=1, source_target_pairs={{0,8},{8,0},{1,9},{9,1},{2,10},{10,2},{3,11},{11,3},{4,12},{12,4},... | collective-permute-start | bytes 24584 | tf_op jit(solution)/shard_map/ppermute | solution.py:34
  71.1 4.6 %collective-permute-start.11 = (f32[2,16,128]{2,1,0:T(8,128)S(1)}, f32[2,16,128]{2,1,0:T(8,128)S(1)}, u32[]{:S(2)}, u32[]{:S(2)}) collective-permute-start(f32[2,16,128]{2,1,0:T(8,128)S(1)} %pad_maximum_fusion.both0_ref), channel_id=1, source_target_pairs={{0,144},{16,128},{128,16},{144,0},{1,145},{17,129},{129,17},{145,1... | collective-permute-start | bytes 49160 | tf_op jit(solution)/shard_map/ppermute | solution.py:38
  71.5 4.2 %collective-permute-start.10 = (f32[2,16,128]{2,1,0:T(8,128)S(1)}, f32[2,16,128]{2,1,0:T(8,128)S(1)}, u32[]{:S(2)}, u32[]{:S(2)}) collective-permute-start(f32[2,16,128]{2,1,0:T(8,128)S(1)} %pad_maximum_fusion.both0_ref), channel_id=1, source_target_pairs={{0,128},{16,144},{128,0},{144,16},{1,129},{17,145},{129,1},{145,17... | collective-permute-start | bytes 49160 | tf_op jit(solution)/shard_map/ppermute | solution.py:38
  73.3 3.7 %collective-permute-start.9 = (f32[2,16,128]{2,1,0:T(8,128)S(1)}, f32[2,16,128]{2,1,0:T(8,128)S(1)}, u32[]{:S(2)}, u32[]{:S(2)}) collective-permute-start(f32[2,16,128]{2,1,0:T(8,128)S(1)} %pad_maximum_fusion.both0_ref), channel_id=1, source_target_pairs={{0,16},{16,0},{128,144},{144,128},{1,17},{17,1},{129,145},{145,129... | collective-permute-start | bytes 49160 | tf_op jit(solution)/shard_map/ppermute | solution.py:38
  80.1 4.1 %collective-permute-start.12 = (bf16[8,16,128]{2,1,0:T(8,128)(2,1)S(1)}, bf16[8,16,128]{2,1,0:T(8,128)(2,1)S(1)}, u32[]{:S(2)}, u32[]{:S(2)}) collective-permute-start(bf16[8,16,128]{2,1,0:T(8,128)(2,1)S(1)} %get-tuple-element.24), channel_id=1, source_target_pairs={{0,16},{16,0},{128,144},{144,128},{1,17},{17,1},{129,145},{145,129... | collective-permute-start | bytes 98312 | tf_op jit(solution)/shard_map/ppermute | solution.py:38
  81.5 3.9 %collective-permute-start.13 = (bf16[8,16,128]{2,1,0:T(8,128)(2,1)S(1)}, bf16[8,16,128]{2,1,0:T(8,128)(2,1)S(1)}, u32[]{:S(2)}, u32[]{:S(2)}) collective-permute-start(bf16[8,16,128]{2,1,0:T(8,128)(2,1)S(1)} %get-tuple-element.25), channel_id=1, source_target_pairs={{0,128},{16,144},{128,0},{144,16},{1,129},{17,145},{129,1},{145,17... | collective-permute-start | bytes 98312 | tf_op jit(solution)/shard_map/ppermute | solution.py:38
  82.2 4.8 %collective-permute-start.14 = (bf16[8,16,128]{2,1,0:T(8,128)(2,1)S(1)}, bf16[8,16,128]{2,1,0:T(8,128)(2,1)S(1)}, u32[]{:S(2)}, u32[]{:S(2)}) collective-permute-start(bf16[8,16,128]{2,1,0:T(8,128)(2,1)S(1)} %get-tuple-element.26), channel_id=1, source_target_pairs={{0,144},{16,128},{128,16},{144,0},{1,145},{17,129},{129,17},{145,1... | collective-permute-start | bytes 98312 | tf_op jit(solution)/shard_map/ppermute | solution.py:38

commit v7 on v5

--- a/solution.py
+++ b/solution.py
@@ -12,7 +12,7 @@
 SLAB = ("yh", "x")
 GROUP = ("yl", "zl")
 SOURCES = ("yl", "zh", "zl")
-COLUMN = ("zh", "zl", "c")
+COLUMN = ("zh", "zl")
 WIDE = ("yl", "zl", "yh", "x")
 
 NB = 16
@@ -128,11 +128,13 @@
     all_pot_ref,
     kept_ref,
     pot_ref,
-    quarters_ref,
+    keep_ref,
+    give_ref,
     list_ref,
     slots_ref,
     phit_ref,
     fieldt_ref,
+    pieces_ref,
     dens_ref,
     sem,
     sems,
@@ -194,10 +196,12 @@
     upper = fieldt.astype(bf16)
     lower = (fieldt - upper.astype(f32)).astype(bf16)
     proj = folded(dot(pot_ref[...], jnp.concatenate([upper, lower], axis=1)).T).astype(bf16)
-    width = quarters_ref.shape[2]
-    for to in range(16):
-        quarter = (to % 2) * 2 + (to // 2) % 2
-        quarters_ref[to] = proj[:, quarter * width : (quarter + 1) * width]
+    width = keep_ref.shape[2]
+    for piece in range(4):
+        pieces_ref[piece] = proj[:, piece * width : (piece + 1) * width]
+    core = core_ref[0]
+    keep_ref[...] = pieces_ref[pl.ds(core * 2, 2)]
+    give_ref[...] = pieces_ref[pl.ds((1 - core) * 2, 2)]
 
     def kept(turn, unused):
         pltpu.make_async_copy(dens_ref.at[turn], kept_ref.at[turn], sems.at[turn]).wait()
@@ -214,17 +218,19 @@
     return pl.pallas_call(
         density_body,
         in_specs=[IN_SMEM] * 2 + [IN_VMEM] * 6 + [IN_HBM],
-        out_specs=[IN_HBM, IN_VMEM, IN_VMEM, IN_SMEM],
+        out_specs=[IN_HBM, IN_VMEM, IN_VMEM, IN_VMEM, IN_SMEM],
         out_shape=[
             pltpu.HBM((turns, points, TAKE * BLOCK), bf16),
             pltpu.VMEM((neig, points), bf16),
-            pltpu.VMEM((16, NB, neig // 4), bf16),
+            pltpu.VMEM((2, NB, neig // 4), bf16),
+            pltpu.VMEM((2, NB, neig // 4), bf16),
             jax.ShapeDtypeStruct((1 + blocks + TAKE,), jnp.int32),
         ],
         scratch_shapes=[
             pltpu.VMEM((blocks, ROWS, BLOCK), bf16),
             pltpu.VMEM((points, 2 * half), bf16),
             pltpu.VMEM((points, NB), f32),
+            pltpu.VMEM((4, NB, neig // 4), bf16),
             pltpu.VMEM((turns, points, TAKE * BLOCK), bf16),
             pltpu.SemaphoreType.DMA(()),
             pltpu.SemaphoreType.DMA((turns,)),
@@ -318,8 +324,10 @@
     mine = exchange(sent, SOURCES)
     mine = mine.reshape(-1, mine.shape[2])
     other = lax.ppermute(mine, "c", [(0, 1), (1, 0)])
-    dens, pot, quarters, live = density(group, core, mine, other, slots, eigenpotentials)
-    column = summed(exchange(quarters, COLUMN)).astype(bf16)
+    dens, pot, keep, give, live = density(group, core, mine, other, slots, eigenpotentials)
+    given = lax.ppermute(give, "c", [(0, 1), (1, 0)])
+    half = (keep.astype(f32) + given.astype(f32)).astype(bf16)
+    column = summed(exchange(copies(half, 4).reshape(8, *half.shape[1:]), COLUMN)).astype(bf16)
     wide = exchange(copies(column, 32), WIDE)
     part = jnp.sum(wide.reshape(2, 2, 8, *column.shape).astype(f32), axis=(0, 2))
     apart = lax.ppermute(part, "c", [(0, 1), (1, 0)])

time: 95 us -> 95.1 us (level)
  blocking collectives: 66.8 us -> 65.6 us
    all_to_all x4, blocking collectives: 66.8 us -> 65.6 us  [exchange(): return lax.all_to_all(blocks, axes, 0, 0, tiled=True)]
  transfers between devices with their start and end apart: 8 -> 9, of which waited for: 7 -> 8; matrix products, arithmetic and copies ran while one was open for 0% -> 0% of each run, Pallas kernels for 0% -> 0%
where the time goes in v7:
time: 95.1 us; the launch traced here: 94.8 us
  blocking collectives  65.6 us (69%)
  Pallas kernels  12.5 us (13%)
  waiting for transfers between devices  8.14 us (9%)
  starting transfers between devices  7.6 us (8%)
    all_to_all x4, blocking collectives, exchange(): return lax.all_to_all(blocks, axes, 0, 0, tiled=True)  65.6 us
    pallas_call x1, Pallas kernels, density(): pl.pallas_call(density_body, in_specs=[IN_SMEM] * 2 + [IN_VMEM] * 6 + [IN...  8.24 us
    ppermute x3, starting transfers between devices, shards(): lax.ppermute(terms[k], GROUP, [(i, i ^ k) for i in range(4)]).astype(f32)  3.58 us
    ppermute x3, starting transfers between devices, shards(): slots.append(lax.ppermute(own_slots, GROUP, [(i, i ^ k) for i in range(4)]))  3.49 us
    ppermute x3, waiting for transfers between devices, shards(): slots.append(lax.ppermute(own_slots, GROUP, [(i, i ^ k) for i in range(4)]))  3.3 us
    pallas_call x1, Pallas kernels, direct_terms(): pl.pallas_call(direct_body, in_specs=[IN_SMEM] * 3 + [IN_VMEM] * 4 + [IN_...  3.09 us
    ppermute x3, waiting for transfers between devices, shards(): lax.ppermute(terms[k], GROUP, [(i, i ^ k) for i in range(4)]).astype(f32)  2.8 us
  transfers between devices with their start and end apart: 9, of which 8 were waited for; matrix products, arithmetic and copies ran while one was open for 0% of the time, Pallas kernels for 0%

profile of v7, /device:TPU:2, one launch (start us, length us, event | category | flops | bytes accessed | tf_op | source)
XLA Modules:
  0.0 94.8 jit_solution(6774008926167681548)
XLA Ops:
  0.0 0.0 copy-start
  0.0 1.2 %prepare.1 = (bf16[16,16,1024]{2,1,0:T(8,128)(2,1)S(1)}, bf16[8,24,128]{2,1,0:T(8,128)(2,1)S(1)}) custom-call(bf16[16,4096]{1,0:T(8,128)(2,1)} %orbitals_ref.1, bf16[16,1024]{1,0:T(8,128)(2,1)} %trial_ref.1, s32[2,1024]{1,0:T(2,128)} %pair_ref.1), custom_call_target="tpu_custom_call" | custom-call | tf_op jit(solution)/shard_map/prepare/pallas_call | solution.py:100
  1.2 25.1 %all_to_all.20 = bf16[16,16,1024]{2,1,0:T(8,128)(2,1)S(1)} all-to-all(bf16[16,16,1024]{2,1,0:T(8,128)(2,1)S(1)} %get-tuple-element.16), channel_id=1, replica_groups=mesh['yl'=2,'zh'=4,'zl'=2,'c'=2,'yh'=2,'x'=4] {'yl','zh','zl'}, dimensions={0} | all-to-all | bytes 1048576 | tf_op jit(solution)/shard_map/all_to_all | solution.py:30
  26.3 0.0 collective-permute-start
  26.3 2.3 %collective-permute-start.3 = (bf16[8,24,128]{2,1,0:T(8,128)(2,1)S(1)}, bf16[8,24,128]{2,1,0:T(8,128)(2,1)S(1)}, u32[]{:S(2)}, u32[]{:S(2)}) collective-permute-start(bf16[8,24,128]{2,1,0:T(8,128)(2,1)S(1)} %get-tuple-element.17.slots0_ref), channel_id=1, source_target_pairs={{0,144},{16,128},{128,16},{144,0},{1,145},{17,129},{129,17},{145,1... | collective-permute-start | bytes 147464 | tf_op jit(solution)/shard_map/ppermute | solution.py:323
  28.6 0.4 collective-permute-start.2
  29.0 0.8 collective-permute-start.1
  29.8 1.6 %collective-permute-done.3.slots3_ref = bf16[8,24,128]{2,1,0:T(8,128)(2,1)S(1)} collective-permute-done((bf16[8,24,128]{2,1,0:T(8,128)(2,1)S(1)}, bf16[8,24,128]{2,1,0:T(8,128)(2,1)S(1)}, u32[]{:S(2)}, u32[]{:S(2)}) %collective-permute-start.3) | collective-permute-done | bytes 49184 | tf_op jit(solution)/shard_map/ppermute | solution.py:323
  31.3 1.4 %collective-permute-done.2.slots2_ref = bf16[8,24,128]{2,1,0:T(8,128)(2,1)S(1)} collective-permute-done((bf16[8,24,128]{2,1,0:T(8,128)(2,1)S(1)}, bf16[8,24,128]{2,1,0:T(8,128)(2,1)S(1)}, u32[]{:S(2)}, u32[]{:S(2)}) %collective-permute-start.2) | collective-permute-done | bytes 49184 | tf_op jit(solution)/shard_map/ppermute | solution.py:323
  32.7 0.4 collective-permute-done.1.slots1_ref
  33.1 0.0 collective-permute-done.other_ref
  33.1 8.2 %density.1 = (bf16[8,1024,512]{2,1,0:T(8,128)(2,1)}, bf16[1024,1024]{1,0:T(8,128)(2,1)S(1)}, bf16[2,16,256]{2,1,0:T(8,128)(2,1)S(1)}, bf16[2,16,256]{2,1,0:T(8,128)(2,1)S(1)}, s32[37]{0:T(128)S(1)}) custom-call(s32[1]{0:T(128)} %bitcast.group_ref, s32[1]{0:T(128)} %bitcast.1.core_ref, bf16[256,1024]{1,0:T(8,128)(2,1)S(1)} %bitcast.14, ...), custom_call_target="tpu_custom_call" | custom-call | tf_op jit(solution)/shard_map/density/pallas_call | solution.py:218
  41.3 0.4 collective-permute-start.4
  41.8 0.8 collective-permute-done.4
  42.6 12.5 %all_to_all.21 = bf16[8,16,256]{2,1,0:T(8,128)(2,1)S(1)} all-to-all(bf16[8,16,256]{2,1,0:T(8,128)(2,1)S(1)} %bitcast.17), channel_id=1, replica_groups=mesh['yl'=2,'zh'=4,'zl'=2,'c'=2,'yh'=2,'x'=4] {'zh','zl'}, dimensions={0} | all-to-all | bytes 131072 | tf_op jit(solution)/shard_map/all_to_all | solution.py:30
  55.2 15.3 %all_to_all.22 = bf16[32,16,256]{2,1,0:T(8,128)(2,1)S(1)} all-to-all(bf16[32,16,256]{2,1,0:T(8,128)(2,1)S(1)} %broadcast_in_dim.7), channel_id=1, replica_groups=mesh['yl'=2,'zh'=4,'zl'=2,'c'=2,'yh'=2,'x'=4] {'yl','zl','yh','x'}, dimensions={0} | all-to-all | bytes 524288 | tf_op jit(solution)/shard_map/all_to_all | solution.py:30
  70.5 0.1 collective-permute-start.5
  70.6 1.2 %collective-permute-done.5.other_ref = f32[2,16,256]{2,1,0:T(8,128)S(1)} collective-permute-done((f32[2,16,256]{2,1,0:T(8,128)S(1)}, f32[2,16,256]{2,1,0:T(8,128)S(1)}, u32[]{:S(2)}, u32[]{:S(2)}) %collective-permute-start.5) | collective-permute-done | bytes 32800 | tf_op jit(solution)/shard_map/ppermute | solution.py:333
  71.8 0.0 copy-done
  71.8 3.1 %direct_terms.1 = (bf16[8,16,128]{2,1,0:T(8,128)(2,1)S(1)}, bf16[8,16,128]{2,1,0:T(8,128)(2,1)S(1)}, bf16[8,16,128]{2,1,0:T(8,128)(2,1)S(1)}, bf16[8,16,128]{2,1,0:T(8,128)(2,1)S(1)}) custom-call(s32[1]{0:T(128)} %bitcast.group_ref, s32[1]{0:T(128)} %bitcast.1.core_ref, s32[37]{0:T(128)S(1)} %get-tuple-element.18.list_ref, ...), custom_call_target="tpu_custom_call" | custom-call | tf_op jit(solution)/shard_map/direct_terms/pallas_call | solution.py:300
  74.9 0.8 collective-permute-start.6
  75.7 0.7 collective-permute-start.7
  76.5 2.0 %collective-permute-start.8 = (bf16[8,16,128]{2,1,0:T(8,128)(2,1)S(1)}, bf16[8,16,128]{2,1,0:T(8,128)(2,1)S(1)}, u32[]{:S(2)}, u32[]{:S(2)}) collective-permute-start(bf16[8,16,128]{2,1,0:T(8,128)(2,1)S(1)} %get-tuple-element.26), channel_id=1, source_target_pairs={{0,144},{16,128},{128,16},{144,0},{1,145},{17,129},{129,17},{145,1... | collective-permute-start | bytes 98312 | tf_op jit(solution)/shard_map/ppermute | solution.py:337
  78.5 0.4 collective-permute-done.6
  78.9 0.7 collective-permute-done.7
  79.6 1.6 %collective-permute-done.8 = bf16[8,16,128]{2,1,0:T(8,128)(2,1)S(1)} collective-permute-done((bf16[8,16,128]{2,1,0:T(8,128)(2,1)S(1)}, bf16[8,16,128]{2,1,0:T(8,128)(2,1)S(1)}, u32[]{:S(2)}, u32[]{:S(2)}) %collective-permute-start.8) | collective-permute-done | bytes 32800 | tf_op jit(solution)/shard_map/ppermute | solution.py:337
  81.3 12.7 %all_to_all.23 = bf16[8,8,16,128]{3,2,1,0:T(8,128)(2,1)S(1)} all-to-all(bf16[8,8,16,128]{3,2,1,0:T(8,128)(2,1)S(1)} %broadcast_in_dim.8), channel_id=1, replica_groups=mesh['yl'=2,'zh'=4,'zl'=2,'c'=2,'yh'=2,'x'=4] {'yh','x'}, dimensions={0} | all-to-all | bytes 524288 | tf_op jit(solution)/shard_map/all_to_all | solution.py:30
  94.1 0.6 copy_bitcast_fusion
  (8 shorter events, 0.2 us)
Async XLA Ops:
  0.0 71.8 %copy-start = (f32[1024]{0:T(1024)S(1)}, f32[1024]{0:T(1024)}, u32[]{:S(2)}) copy-start(f32[1024]{0:T(1024)} %param.7) | copy-start | bytes 12292
  26.3 6.8 %collective-permute-start = (bf16[256,1024]{1,0:T(8,128)(2,1)S(1)}, bf16[256,1024]{1,0:T(8,128)(2,1)S(1)}, u32[]{:S(2)}, u32[]{:S(2)}) collective-permute-start(bf16[256,1024]{1,0:T(8,128)(2,1)S(1)} %bitcast.13), channel_id=1, source_target_pairs={{0,8},{8,0},{1,9},{9,1},{2,10},{10,2},{3,11},{11,3},{4,12},{12,4},... | collective-permute-start | bytes 1572872 | tf_op jit(solution)/shard_map/ppermute | solution.py:326
  26.3 5.1 %collective-permute-start.3 = (bf16[8,24,128]{2,1,0:T(8,128)(2,1)S(1)}, bf16[8,24,128]{2,1,0:T(8,128)(2,1)S(1)}, u32[]{:S(2)}, u32[]{:S(2)}) collective-permute-start(bf16[8,24,128]{2,1,0:T(8,128)(2,1)S(1)} %get-tuple-element.17.slots0_ref), channel_id=1, source_target_pairs={{0,144},{16,128},{128,16},{144,0},{1,145},{17,129},{129,17},{145,1... | collective-permute-start | bytes 147464 | tf_op jit(solution)/shard_map/ppermute | solution.py:323
  28.6 4.1 %collective-permute-start.2 = (bf16[8,24,128]{2,1,0:T(8,128)(2,1)S(1)}, bf16[8,24,128]{2,1,0:T(8,128)(2,1)S(1)}, u32[]{:S(2)}, u32[]{:S(2)}) collective-permute-start(bf16[8,24,128]{2,1,0:T(8,128)(2,1)S(1)} %get-tuple-element.17.slots0_ref), channel_id=1, source_target_pairs={{0,128},{16,144},{128,0},{144,16},{1,129},{17,145},{129,1},{145,17... | collective-permute-start | bytes 147464 | tf_op jit(solution)/shard_map/ppermute | solution.py:323
  29.0 4.1 %collective-permute-start.1 = (bf16[8,24,128]{2,1,0:T(8,128)(2,1)S(1)}, bf16[8,24,128]{2,1,0:T(8,128)(2,1)S(1)}, u32[]{:S(2)}, u32[]{:S(2)}) collective-permute-start(bf16[8,24,128]{2,1,0:T(8,128)(2,1)S(1)} %get-tuple-element.17.slots0_ref), channel_id=1, source_target_pairs={{0,16},{16,0},{128,144},{144,128},{1,17},{17,1},{129,145},{145,129... | collective-permute-start | bytes 147464 | tf_op jit(solution)/shard_map/ppermute | solution.py:323
  41.3 1.3 %collective-permute-start.4 = (bf16[2,16,256]{2,1,0:T(8,128)(2,1)S(1)}, bf16[2,16,256]{2,1,0:T(8,128)(2,1)S(1)}, u32[]{:S(2)}, u32[]{:S(2)}) collective-permute-start(bf16[2,16,256]{2,1,0:T(8,128)(2,1)S(1)} %get-tuple-element.20), channel_id=1, source_target_pairs={{0,8},{8,0},{1,9},{9,1},{2,10},{10,2},{3,11},{11,3},{4,12},{12,4},... | collective-permute-start | bytes 49160 | tf_op jit(solution)/shard_map/ppermute | solution.py:328
  70.5 1.3 %collective-permute-start.5 = (f32[2,16,256]{2,1,0:T(8,128)S(1)}, f32[2,16,256]{2,1,0:T(8,128)S(1)}, u32[]{:S(2)}, u32[]{:S(2)}) collective-permute-start(f32[2,16,256]{2,1,0:T(8,128)S(1)} %convert_reduce_fusion.mine_ref), channel_id=1, source_target_pairs={{0,8},{8,0},{1,9},{9,1},{2,10},{10,2},{3,11},{11,3},{4,12},{12,4},... | collective-permute-start | bytes 98312 | tf_op jit(solution)/shard_map/ppermute | solution.py:333
  74.9 4.0 %collective-permute-start.6 = (bf16[8,16,128]{2,1,0:T(8,128)(2,1)S(1)}, bf16[8,16,128]{2,1,0:T(8,128)(2,1)S(1)}, u32[]{:S(2)}, u32[]{:S(2)}) collective-permute-start(bf16[8,16,128]{2,1,0:T(8,128)(2,1)S(1)} %get-tuple-element.24), channel_id=1, source_target_pairs={{0,16},{16,0},{128,144},{144,128},{1,17},{17,1},{129,145},{145,129... | collective-permute-start | bytes 98312 | tf_op jit(solution)/shard_map/ppermute | solution.py:337
  75.7 3.9 %collective-permute-start.7 = (bf16[8,16,128]{2,1,0:T(8,128)(2,1)S(1)}, bf16[8,16,128]{2,1,0:T(8,128)(2,1)S(1)}, u32[]{:S(2)}, u32[]{:S(2)}) collective-permute-start(bf16[8,16,128]{2,1,0:T(8,128)(2,1)S(1)} %get-tuple-element.25), channel_id=1, source_target_pairs={{0,128},{16,144},{128,0},{144,16},{1,129},{17,145},{129,1},{145,17... | collective-permute-start | bytes 98312 | tf_op jit(solution)/shard_map/ppermute | solution.py:337
  76.5 4.8 %collective-permute-start.8 = (bf16[8,16,128]{2,1,0:T(8,128)(2,1)S(1)}, bf16[8,16,128]{2,1,0:T(8,128)(2,1)S(1)}, u32[]{:S(2)}, u32[]{:S(2)}) collective-permute-start(bf16[8,16,128]{2,1,0:T(8,128)(2,1)S(1)} %get-tuple-element.26), channel_id=1, source_target_pairs={{0,144},{16,128},{128,16},{144,0},{1,145},{17,129},{129,17},{145,1... | collective-permute-start | bytes 98312 | tf_op jit(solution)/shard_map/ppermute | solution.py:337

commit v8 on v5

--- a/solution.py
+++ b/solution.py
@@ -132,7 +132,7 @@
     list_ref,
     slots_ref,
     phit_ref,
-    fieldt_ref,
+    field_ref,
     dens_ref,
     sem,
     sems,
@@ -152,7 +152,7 @@
             phit_ref[:, core * half : (core + 1) * half] = mine_ref[...].T
             phit_ref[:, (1 - core) * half : (2 - core) * half] = other_ref[...].T
 
-    fieldt_ref[...] = jnp.zeros_like(fieldt_ref)
+    field_ref[...] = jnp.zeros_like(field_ref)
     blocks = slots_ref.shape[0]
     count = jnp.int32(0)
     for block in range(blocks):
@@ -184,13 +184,13 @@
         dens = (picked(0) * picked(1)).astype(bf16)
         dens_ref[turn] = dens
         pltpu.make_async_copy(dens_ref.at[turn], kept_ref.at[turn], sems.at[turn]).start()
-        fieldt_ref[...] += dot(dens, trial, NT)
+        field_ref[...] += dot(trial, dens, NT)
         return unused
 
     turns = (count + TAKE - 1) // TAKE
     lax.fori_loop(0, turns, step, 0)
     fetch.wait()
-    fieldt = fieldt_ref[...]
+    fieldt = field_ref[...].T
     upper = fieldt.astype(bf16)
     lower = (fieldt - upper.astype(f32)).astype(bf16)
     proj = folded(dot(pot_ref[...], jnp.concatenate([upper, lower], axis=1)).T).astype(bf16)
@@ -224,7 +224,7 @@
         scratch_shapes=[
             pltpu.VMEM((blocks, ROWS, BLOCK), bf16),
             pltpu.VMEM((points, 2 * half), bf16),
-            pltpu.VMEM((points, NB), f32),
+            pltpu.VMEM((NB, points), f32),
             pltpu.VMEM((turns, points, TAKE * BLOCK), bf16),
             pltpu.SemaphoreType.DMA(()),
             pltpu.SemaphoreType.DMA((turns,)),

time: 95 us -> 94.8 us (level)
  no operation moved by 1% of the time
where the time goes in v8:
time: 94.8 us; the launch traced here: 94.5 us
  blocking collectives  66.8 us (70%)
  Pallas kernels  12.3 us (13%)
  waiting for transfers between devices  7.3 us (8%)
  starting transfers between devices  7.16 us (8%)
    all_to_all x4, blocking collectives, exchange(): return lax.all_to_all(blocks, axes, 0, 0, tiled=True)  66.8 us
    pallas_call x1, Pallas kernels, density(): pl.pallas_call(density_body, in_specs=[IN_SMEM] * 2 + [IN_VMEM] * 6 + [IN...  8.04 us
    ppermute x3, starting transfers between devices, shards(): lax.ppermute(terms[k], GROUP, [(i, i ^ k) for i in range(4)]).astype(f32)  3.58 us
    ppermute x3, starting transfers between devices, shards(): slots.append(lax.ppermute(own_slots, GROUP, [(i, i ^ k) for i in range(4)]))  3.49 us
    ppermute x3, waiting for transfers between devices, shards(): slots.append(lax.ppermute(own_slots, GROUP, [(i, i ^ k) for i in range(4)]))  3.3 us
    pallas_call x1, Pallas kernels, direct_terms(): pl.pallas_call(direct_body, in_specs=[IN_SMEM] * 3 + [IN_VMEM] * 4 + [IN_...  3.09 us
    ppermute x3, waiting for transfers between devices, shards(): lax.ppermute(terms[k], GROUP, [(i, i ^ k) for i in range(4)]).astype(f32)  2.8 us
  transfers between devices with their start and end apart: 8, of which 7 were waited for; matrix products, arithmetic and copies ran while one was open for 0% of the time, Pallas kernels for 0%

profile of v8, /device:TPU:2, one launch (start us, length us, event | category | flops | bytes accessed | tf_op | source)
XLA Modules:
  0.0 94.5 jit_solution(14990481009616196284)
XLA Ops:
  0.0 0.0 copy-start
  0.0 1.2 %prepare.1 = (bf16[16,16,1024]{2,1,0:T(8,128)(2,1)S(1)}, bf16[8,24,128]{2,1,0:T(8,128)(2,1)S(1)}) custom-call(bf16[16,4096]{1,0:T(8,128)(2,1)} %orbitals_ref.1, bf16[16,1024]{1,0:T(8,128)(2,1)} %trial_ref.1, s32[2,1024]{1,0:T(2,128)} %pair_ref.1), custom_call_target="tpu_custom_call" | custom-call | tf_op jit(solution)/shard_map/prepare/pallas_call | solution.py:100
  1.2 25.1 %all_to_all.20 = bf16[16,16,1024]{2,1,0:T(8,128)(2,1)S(1)} all-to-all(bf16[16,16,1024]{2,1,0:T(8,128)(2,1)S(1)} %get-tuple-element.15), channel_id=1, replica_groups=mesh['yl'=2,'zh'=4,'zl'=2,'c'=2,'yh'=2,'x'=4] {'yl','zh','zl'}, dimensions={0} | all-to-all | bytes 1048576 | tf_op jit(solution)/shard_map/all_to_all | solution.py:30
  26.3 0.0 collective-permute-start
  26.3 2.3 %collective-permute-start.3 = (bf16[8,24,128]{2,1,0:T(8,128)(2,1)S(1)}, bf16[8,24,128]{2,1,0:T(8,128)(2,1)S(1)}, u32[]{:S(2)}, u32[]{:S(2)}) collective-permute-start(bf16[8,24,128]{2,1,0:T(8,128)(2,1)S(1)} %get-tuple-element.16.slots0_ref), channel_id=1, source_target_pairs={{0,144},{16,128},{128,16},{144,0},{1,145},{17,129},{129,17},{145,1... | collective-permute-start | bytes 147464 | tf_op jit(solution)/shard_map/ppermute | solution.py:317
  28.6 0.4 collective-permute-start.2
  29.0 0.8 collective-permute-start.1
  29.8 1.6 %collective-permute-done.3.slots3_ref = bf16[8,24,128]{2,1,0:T(8,128)(2,1)S(1)} collective-permute-done((bf16[8,24,128]{2,1,0:T(8,128)(2,1)S(1)}, bf16[8,24,128]{2,1,0:T(8,128)(2,1)S(1)}, u32[]{:S(2)}, u32[]{:S(2)}) %collective-permute-start.3) | collective-permute-done | bytes 49184 | tf_op jit(solution)/shard_map/ppermute | solution.py:317
  31.3 1.4 %collective-permute-done.2.slots2_ref = bf16[8,24,128]{2,1,0:T(8,128)(2,1)S(1)} collective-permute-done((bf16[8,24,128]{2,1,0:T(8,128)(2,1)S(1)}, bf16[8,24,128]{2,1,0:T(8,128)(2,1)S(1)}, u32[]{:S(2)}, u32[]{:S(2)}) %collective-permute-start.2) | collective-permute-done | bytes 49184 | tf_op jit(solution)/shard_map/ppermute | solution.py:317
  32.7 0.4 collective-permute-done.1.slots1_ref
  33.1 0.0 collective-permute-done.other_ref
  33.1 8.0 %density.1 = (bf16[8,1024,512]{2,1,0:T(8,128)(2,1)}, bf16[1024,1024]{1,0:T(8,128)(2,1)S(1)}, bf16[16,16,256]{2,1,0:T(8,128)(2,1)S(1)}, s32[37]{0:T(128)S(1)}) custom-call(s32[1]{0:T(128)} %bitcast.group_ref, s32[1]{0:T(128)} %bitcast.1.core_ref, bf16[256,1024]{1,0:T(8,128)(2,1)S(1)} %bitcast.13, bf16[256,1024]{1,0:T(8,128)(2,1)S(1)} %collective-permute-done.other_ref, ...), custom_call_target="tpu_custom_call" | custom-call | tf_op jit(solution)/shard_map/density/pallas_call | solution.py:214
  41.1 12.9 %all_to_all.21 = bf16[16,16,256]{2,1,0:T(8,128)(2,1)S(1)} all-to-all(bf16[16,16,256]{2,1,0:T(8,128)(2,1)S(1)} %get-tuple-element.18), channel_id=1, replica_groups=mesh['yl'=2,'zh'=4,'zl'=2,'c'=2,'yh'=2,'x'=4] {'zh','zl','c'}, dimensions={0} | all-to-all | bytes 262144 | tf_op jit(solution)/shard_map/all_to_all | solution.py:30
  54.1 16.1 %all_to_all.22 = bf16[32,16,256]{2,1,0:T(8,128)(2,1)S(1)} all-to-all(bf16[32,16,256]{2,1,0:T(8,128)(2,1)S(1)} %broadcast_in_dim.4), channel_id=1, replica_groups=mesh['yl'=2,'zh'=4,'zl'=2,'c'=2,'yh'=2,'x'=4] {'yl','zl','yh','x'}, dimensions={0} | all-to-all | bytes 524288 | tf_op jit(solution)/shard_map/all_to_all | solution.py:30
  70.2 0.1 collective-permute-start.4
  70.3 1.2 %collective-permute-done.4.other_ref = f32[2,16,256]{2,1,0:T(8,128)S(1)} collective-permute-done((f32[2,16,256]{2,1,0:T(8,128)S(1)}, f32[2,16,256]{2,1,0:T(8,128)S(1)}, u32[]{:S(2)}, u32[]{:S(2)}) %collective-permute-start.4) | collective-permute-done | bytes 32800 | tf_op jit(solution)/shard_map/ppermute | solution.py:325
  71.5 0.0 copy-done
  71.5 3.1 %direct_terms.1 = (bf16[8,16,128]{2,1,0:T(8,128)(2,1)S(1)}, bf16[8,16,128]{2,1,0:T(8,128)(2,1)S(1)}, bf16[8,16,128]{2,1,0:T(8,128)(2,1)S(1)}, bf16[8,16,128]{2,1,0:T(8,128)(2,1)S(1)}) custom-call(s32[1]{0:T(128)} %bitcast.group_ref, s32[1]{0:T(128)} %bitcast.1.core_ref, s32[37]{0:T(128)S(1)} %get-tuple-element.17.list_ref, ...), custom_call_target="tpu_custom_call" | custom-call | tf_op jit(solution)/shard_map/direct_terms/pallas_call | solution.py:294
  74.6 0.8 collective-permute-start.5
  75.4 0.7 collective-permute-start.6
  76.2 2.0 %collective-permute-start.7 = (bf16[8,16,128]{2,1,0:T(8,128)(2,1)S(1)}, bf16[8,16,128]{2,1,0:T(8,128)(2,1)S(1)}, u32[]{:S(2)}, u32[]{:S(2)}) collective-permute-start(bf16[8,16,128]{2,1,0:T(8,128)(2,1)S(1)} %get-tuple-element.24), channel_id=1, source_target_pairs={{0,144},{16,128},{128,16},{144,0},{1,145},{17,129},{129,17},{145,1... | collective-permute-start | bytes 98312 | tf_op jit(solution)/shard_map/ppermute | solution.py:329
  78.2 0.4 collective-permute-done.5
  78.6 0.7 collective-permute-done.6
  79.3 1.6 %collective-permute-done.7 = bf16[8,16,128]{2,1,0:T(8,128)(2,1)S(1)} collective-permute-done((bf16[8,16,128]{2,1,0:T(8,128)(2,1)S(1)}, bf16[8,16,128]{2,1,0:T(8,128)(2,1)S(1)}, u32[]{:S(2)}, u32[]{:S(2)}) %collective-permute-start.7) | collective-permute-done | bytes 32800 | tf_op jit(solution)/shard_map/ppermute | solution.py:329
  81.1 12.7 %all_to_all.23 = bf16[8,8,16,128]{3,2,1,0:T(8,128)(2,1)S(1)} all-to-all(bf16[8,8,16,128]{3,2,1,0:T(8,128)(2,1)S(1)} %broadcast_in_dim.5), channel_id=1, replica_groups=mesh['yl'=2,'zh'=4,'zl'=2,'c'=2,'yh'=2,'x'=4] {'yh','x'}, dimensions={0} | all-to-all | bytes 524288 | tf_op jit(solution)/shard_map/all_to_all | solution.py:30
  93.8 0.6 copy_bitcast_fusion
  (6 shorter events, 0.2 us)
Async XLA Ops:
  0.0 71.5 %copy-start = (f32[1024]{0:T(1024)S(1)}, f32[1024]{0:T(1024)}, u32[]{:S(2)}) copy-start(f32[1024]{0:T(1024)} %param.7) | copy-start | bytes 12292
  26.3 6.8 %collective-permute-start = (bf16[256,1024]{1,0:T(8,128)(2,1)S(1)}, bf16[256,1024]{1,0:T(8,128)(2,1)S(1)}, u32[]{:S(2)}, u32[]{:S(2)}) collective-permute-start(bf16[256,1024]{1,0:T(8,128)(2,1)S(1)} %bitcast.12), channel_id=1, source_target_pairs={{0,8},{8,0},{1,9},{9,1},{2,10},{10,2},{3,11},{11,3},{4,12},{12,4},... | collective-permute-start | bytes 1572872 | tf_op jit(solution)/shard_map/ppermute | solution.py:320
  26.3 5.1 %collective-permute-start.3 = (bf16[8,24,128]{2,1,0:T(8,128)(2,1)S(1)}, bf16[8,24,128]{2,1,0:T(8,128)(2,1)S(1)}, u32[]{:S(2)}, u32[]{:S(2)}) collective-permute-start(bf16[8,24,128]{2,1,0:T(8,128)(2,1)S(1)} %get-tuple-element.16.slots0_ref), channel_id=1, source_target_pairs={{0,144},{16,128},{128,16},{144,0},{1,145},{17,129},{129,17},{145,1... | collective-permute-start | bytes 147464 | tf_op jit(solution)/shard_map/ppermute | solution.py:317
  28.6 4.1 %collective-permute-start.2 = (bf16[8,24,128]{2,1,0:T(8,128)(2,1)S(1)}, bf16[8,24,128]{2,1,0:T(8,128)(2,1)S(1)}, u32[]{:S(2)}, u32[]{:S(2)}) collective-permute-start(bf16[8,24,128]{2,1,0:T(8,128)(2,1)S(1)} %get-tuple-element.16.slots0_ref), channel_id=1, source_target_pairs={{0,128},{16,144},{128,0},{144,16},{1,129},{17,145},{129,1},{145,17... | collective-permute-start | bytes 147464 | tf_op jit(solution)/shard_map/ppermute | solution.py:317
  29.0 4.1 %collective-permute-start.1 = (bf16[8,24,128]{2,1,0:T(8,128)(2,1)S(1)}, bf16[8,24,128]{2,1,0:T(8,128)(2,1)S(1)}, u32[]{:S(2)}, u32[]{:S(2)}) collective-permute-start(bf16[8,24,128]{2,1,0:T(8,128)(2,1)S(1)} %get-tuple-element.16.slots0_ref), channel_id=1, source_target_pairs={{0,16},{16,0},{128,144},{144,128},{1,17},{17,1},{129,145},{145,129... | collective-permute-start | bytes 147464 | tf_op jit(solution)/shard_map/ppermute | solution.py:317
  70.2 1.3 %collective-permute-start.4 = (f32[2,16,256]{2,1,0:T(8,128)S(1)}, f32[2,16,256]{2,1,0:T(8,128)S(1)}, u32[]{:S(2)}, u32[]{:S(2)}) collective-permute-start(f32[2,16,256]{2,1,0:T(8,128)S(1)} %convert_reduce_fusion.mine_ref), channel_id=1, source_target_pairs={{0,8},{8,0},{1,9},{9,1},{2,10},{10,2},{3,11},{11,3},{4,12},{12,4},... | collective-permute-start | bytes 98312 | tf_op jit(solution)/shard_map/ppermute | solution.py:325
  74.6 4.0 %collective-permute-start.5 = (bf16[8,16,128]{2,1,0:T(8,128)(2,1)S(1)}, bf16[8,16,128]{2,1,0:T(8,128)(2,1)S(1)}, u32[]{:S(2)}, u32[]{:S(2)}) collective-permute-start(bf16[8,16,128]{2,1,0:T(8,128)(2,1)S(1)} %get-tuple-element.22), channel_id=1, source_target_pairs={{0,16},{16,0},{128,144},{144,128},{1,17},{17,1},{129,145},{145,129... | collective-permute-start | bytes 98312 | tf_op jit(solution)/shard_map/ppermute | solution.py:329
  75.4 3.9 %collective-permute-start.6 = (bf16[8,16,128]{2,1,0:T(8,128)(2,1)S(1)}, bf16[8,16,128]{2,1,0:T(8,128)(2,1)S(1)}, u32[]{:S(2)}, u32[]{:S(2)}) collective-permute-start(bf16[8,16,128]{2,1,0:T(8,128)(2,1)S(1)} %get-tuple-element.23), channel_id=1, source_target_pairs={{0,128},{16,144},{128,0},{144,16},{1,129},{17,145},{129,1},{145,17... | collective-permute-start | bytes 98312 | tf_op jit(solution)/shard_map/ppermute | solution.py:329
  76.2 4.8 %collective-permute-start.7 = (bf16[8,16,128]{2,1,0:T(8,128)(2,1)S(1)}, bf16[8,16,128]{2,1,0:T(8,128)(2,1)S(1)}, u32[]{:S(2)}, u32[]{:S(2)}) collective-permute-start(bf16[8,16,128]{2,1,0:T(8,128)(2,1)S(1)} %get-tuple-element.24), channel_id=1, source_target_pairs={{0,144},{16,128},{128,16},{144,0},{1,145},{17,129},{129,17},{145,1... | collective-permute-start | bytes 98312 | tf_op jit(solution)/shard_map/ppermute | solution.py:329

commit v9 on v8

--- a/solution.py
+++ b/solution.py
@@ -18,7 +18,7 @@
 NB = 16
 BLOCK = 128
 ROWS = 24
-TAKE = 4
+TAKE = 2
 
 f32 = jnp.float32
 bf16 = jnp.bfloat16
@@ -163,7 +163,8 @@
     for extra in range(TAKE):
         list_ref[1 + count + extra] = jnp.int32(0)
 
-    rows = lax.broadcasted_iota(jnp.int32, (half, TAKE * BLOCK), 0).astype(f32)
+    rows = lax.broadcasted_iota(jnp.int32, (half, TAKE * BLOCK), 0).astype(f32).astype(bf16)
+    one, none = jnp.ones((), bf16), jnp.zeros((), bf16)
 
     def step(turn, unused):
         pieces, trials = [], []
@@ -173,15 +174,15 @@
             where = slots_ref[block, NB:ROWS, :].astype(f32)
             pieces.append(jnp.where(at < count, where, -1.0))
             trials.append(slots_ref[block, :NB, :])
-        where = jnp.concatenate(pieces, axis=1)
+        where = jnp.concatenate(pieces, axis=1).astype(bf16)
         trial = jnp.concatenate(trials, axis=1)
 
         def picked(row):
-            even_core = (rows == where[row : row + 1]).astype(bf16)
-            odd_core = (rows == where[row + 2 : row + 3]).astype(bf16)
+            even_core = jnp.where(rows == where[row : row + 1], one, none)
+            odd_core = jnp.where(rows == where[row + 2 : row + 3], one, none)
             return dot(phit_ref[...], jnp.concatenate([even_core, odd_core], axis=0))
 
-        dens = (picked(0) * picked(1)).astype(bf16)
+        dens = picked(0).astype(bf16) * picked(1).astype(bf16)
         dens_ref[turn] = dens
         pltpu.make_async_copy(dens_ref.at[turn], kept_ref.at[turn], sems.at[turn]).start()
         field_ref[...] += dot(trial, dens, NT)

time: 94.8 us -> 95.1 us (level)
  Pallas kernels: 12.3 us -> 13.5 us
where the time goes in v9:
time: 95.1 us; the launch traced here: 94.8 us
  blocking collectives  65.9 us (69%)
  Pallas kernels  13.5 us (14%)
  waiting for transfers between devices  7.3 us (8%)
  starting transfers between devices  7.16 us (8%)
    all_to_all x4, blocking collectives, exchange(): return lax.all_to_all(blocks, axes, 0, 0, tiled=True)  65.9 us
    pallas_call x1, Pallas kernels, density(): pl.pallas_call(density_body, in_specs=[IN_SMEM] * 2 + [IN_VMEM] * 6 + [IN...  8.94 us
    ppermute x3, starting transfers between devices, shards(): lax.ppermute(terms[k], GROUP, [(i, i ^ k) for i in range(4)]).astype(f32)  3.58 us
    ppermute x3, starting transfers between devices, shards(): slots.append(lax.ppermute(own_slots, GROUP, [(i, i ^ k) for i in range(4)]))  3.49 us
    pallas_call x1, Pallas kernels, direct_terms(): pl.pallas_call(direct_body, in_specs=[IN_SMEM] * 3 + [IN_VMEM] * 4 + [IN_...  3.36 us
    ppermute x3, waiting for transfers between devices, shards(): slots.append(lax.ppermute(own_slots, GROUP, [(i, i ^ k) for i in range(4)]))  3.3 us
    ppermute x3, waiting for transfers between devices, shards(): lax.ppermute(terms[k], GROUP, [(i, i ^ k) for i in range(4)]).astype(f32)  2.8 us
  transfers between devices with their start and end apart: 8, of which 7 were waited for; matrix products, arithmetic and copies ran while one was open for 0% of the time, Pallas kernels for 0%

profile of v9, /device:TPU:2, one launch (start us, length us, event | category | flops | bytes accessed | tf_op | source)
XLA Modules:
  0.0 94.8 jit_solution(10250632689648988301)
XLA Ops:
  0.0 0.0 copy-start
  0.0 1.2 %prepare.1 = (bf16[16,16,1024]{2,1,0:T(8,128)(2,1)S(1)}, bf16[8,24,128]{2,1,0:T(8,128)(2,1)S(1)}) custom-call(bf16[16,4096]{1,0:T(8,128)(2,1)} %orbitals_ref.1, bf16[16,1024]{1,0:T(8,128)(2,1)} %trial_ref.1, s32[2,1024]{1,0:T(2,128)} %pair_ref.1), custom_call_target="tpu_custom_call" | custom-call | tf_op jit(solution)/shard_map/prepare/pallas_call | solution.py:100
  1.2 25.1 %all_to_all.20 = bf16[16,16,1024]{2,1,0:T(8,128)(2,1)S(1)} all-to-all(bf16[16,16,1024]{2,1,0:T(8,128)(2,1)S(1)} %get-tuple-element.15), channel_id=1, replica_groups=mesh['yl'=2,'zh'=4,'zl'=2,'c'=2,'yh'=2,'x'=4] {'yl','zh','zl'}, dimensions={0} | all-to-all | bytes 1048576 | tf_op jit(solution)/shard_map/all_to_all | solution.py:30
  26.3 0.0 collective-permute-start
  26.3 2.3 %collective-permute-start.3 = (bf16[8,24,128]{2,1,0:T(8,128)(2,1)S(1)}, bf16[8,24,128]{2,1,0:T(8,128)(2,1)S(1)}, u32[]{:S(2)}, u32[]{:S(2)}) collective-permute-start(bf16[8,24,128]{2,1,0:T(8,128)(2,1)S(1)} %get-tuple-element.16.slots0_ref), channel_id=1, source_target_pairs={{0,144},{16,128},{128,16},{144,0},{1,145},{17,129},{129,17},{145,1... | collective-permute-start | bytes 147464 | tf_op jit(solution)/shard_map/ppermute | solution.py:318
  28.6 0.4 collective-permute-start.2
  29.0 0.8 collective-permute-start.1
  29.8 1.6 %collective-permute-done.3.slots3_ref = bf16[8,24,128]{2,1,0:T(8,128)(2,1)S(1)} collective-permute-done((bf16[8,24,128]{2,1,0:T(8,128)(2,1)S(1)}, bf16[8,24,128]{2,1,0:T(8,128)(2,1)S(1)}, u32[]{:S(2)}, u32[]{:S(2)}) %collective-permute-start.3) | collective-permute-done | bytes 49184 | tf_op jit(solution)/shard_map/ppermute | solution.py:318
  31.3 1.4 %collective-permute-done.2.slots2_ref = bf16[8,24,128]{2,1,0:T(8,128)(2,1)S(1)} collective-permute-done((bf16[8,24,128]{2,1,0:T(8,128)(2,1)S(1)}, bf16[8,24,128]{2,1,0:T(8,128)(2,1)S(1)}, u32[]{:S(2)}, u32[]{:S(2)}) %collective-permute-start.2) | collective-permute-done | bytes 49184 | tf_op jit(solution)/shard_map/ppermute | solution.py:318
  32.7 0.4 collective-permute-done.1.slots1_ref
  33.1 0.0 collective-permute-done.other_ref
  33.1 8.9 %density.1 = (bf16[16,1024,256]{2,1,0:T(8,128)(2,1)}, bf16[1024,1024]{1,0:T(8,128)(2,1)S(1)}, bf16[16,16,256]{2,1,0:T(8,128)(2,1)S(1)}, s32[35]{0:T(128)S(1)}) custom-call(s32[1]{0:T(128)} %bitcast.group_ref, s32[1]{0:T(128)} %bitcast.1.core_ref, bf16[256,1024]{1,0:T(8,128)(2,1)S(1)} %bitcast.13, bf16[256,1024]{1,0:T(8,128)(2,1)S(1)} %collective-permute-done.other_ref, ...), custom_call_target="tpu_custom_call" | custom-call | tf_op jit(solution)/shard_map/density/pallas_call | solution.py:215
  42.0 12.1 %all_to_all.21 = bf16[16,16,256]{2,1,0:T(8,128)(2,1)S(1)} all-to-all(bf16[16,16,256]{2,1,0:T(8,128)(2,1)S(1)} %get-tuple-element.18), channel_id=1, replica_groups=mesh['yl'=2,'zh'=4,'zl'=2,'c'=2,'yh'=2,'x'=4] {'zh','zl','c'}, dimensions={0} | all-to-all | bytes 262144 | tf_op jit(solution)/shard_map/all_to_all | solution.py:30
  54.1 16.1 %all_to_all.22 = bf16[32,16,256]{2,1,0:T(8,128)(2,1)S(1)} all-to-all(bf16[32,16,256]{2,1,0:T(8,128)(2,1)S(1)} %broadcast_in_dim.4), channel_id=1, replica_groups=mesh['yl'=2,'zh'=4,'zl'=2,'c'=2,'yh'=2,'x'=4] {'yl','zl','yh','x'}, dimensions={0} | all-to-all | bytes 524288 | tf_op jit(solution)/shard_map/all_to_all | solution.py:30
  70.2 0.1 collective-permute-start.4
  70.3 1.2 %collective-permute-done.4.other_ref = f32[2,16,256]{2,1,0:T(8,128)S(1)} collective-permute-done((f32[2,16,256]{2,1,0:T(8,128)S(1)}, f32[2,16,256]{2,1,0:T(8,128)S(1)}, u32[]{:S(2)}, u32[]{:S(2)}) %collective-permute-start.4) | collective-permute-done | bytes 32800 | tf_op jit(solution)/shard_map/ppermute | solution.py:326
  71.5 0.0 copy-done
  71.5 3.4 %direct_terms.1 = (bf16[8,16,128]{2,1,0:T(8,128)(2,1)S(1)}, bf16[8,16,128]{2,1,0:T(8,128)(2,1)S(1)}, bf16[8,16,128]{2,1,0:T(8,128)(2,1)S(1)}, bf16[8,16,128]{2,1,0:T(8,128)(2,1)S(1)}) custom-call(s32[1]{0:T(128)} %bitcast.group_ref, s32[1]{0:T(128)} %bitcast.1.core_ref, s32[35]{0:T(128)S(1)} %get-tuple-element.17.list_ref, ...), custom_call_target="tpu_custom_call" | custom-call | tf_op jit(solution)/shard_map/direct_terms/pallas_call | solution.py:295
  74.9 0.8 collective-permute-start.5
  75.7 0.7 collective-permute-start.6
  76.5 2.0 %collective-permute-start.7 = (bf16[8,16,128]{2,1,0:T(8,128)(2,1)S(1)}, bf16[8,16,128]{2,1,0:T(8,128)(2,1)S(1)}, u32[]{:S(2)}, u32[]{:S(2)}) collective-permute-start(bf16[8,16,128]{2,1,0:T(8,128)(2,1)S(1)} %get-tuple-element.24), channel_id=1, source_target_pairs={{0,144},{16,128},{128,16},{144,0},{1,145},{17,129},{129,17},{145,1... | collective-permute-start | bytes 98312 | tf_op jit(solution)/shard_map/ppermute | solution.py:330
  78.5 0.4 collective-permute-done.5
  78.9 0.7 collective-permute-done.6
  79.6 1.6 %collective-permute-done.7 = bf16[8,16,128]{2,1,0:T(8,128)(2,1)S(1)} collective-permute-done((bf16[8,16,128]{2,1,0:T(8,128)(2,1)S(1)}, bf16[8,16,128]{2,1,0:T(8,128)(2,1)S(1)}, u32[]{:S(2)}, u32[]{:S(2)}) %collective-permute-start.7) | collective-permute-done | bytes 32800 | tf_op jit(solution)/shard_map/ppermute | solution.py:330
  81.4 12.7 %all_to_all.23 = bf16[8,8,16,128]{3,2,1,0:T(8,128)(2,1)S(1)} all-to-all(bf16[8,8,16,128]{3,2,1,0:T(8,128)(2,1)S(1)} %broadcast_in_dim.5), channel_id=1, replica_groups=mesh['yl'=2,'zh'=4,'zl'=2,'c'=2,'yh'=2,'x'=4] {'yh','x'}, dimensions={0} | all-to-all | bytes 524288 | tf_op jit(solution)/shard_map/all_to_all | solution.py:30
  94.1 0.6 copy_bitcast_fusion
  (6 shorter events, 0.2 us)
Async XLA Ops:
  0.0 71.5 %copy-start = (f32[1024]{0:T(1024)S(1)}, f32[1024]{0:T(1024)}, u32[]{:S(2)}) copy-start(f32[1024]{0:T(1024)} %param.7) | copy-start | bytes 12292
  26.3 6.8 %collective-permute-start = (bf16[256,1024]{1,0:T(8,128)(2,1)S(1)}, bf16[256,1024]{1,0:T(8,128)(2,1)S(1)}, u32[]{:S(2)}, u32[]{:S(2)}) collective-permute-start(bf16[256,1024]{1,0:T(8,128)(2,1)S(1)} %bitcast.12), channel_id=1, source_target_pairs={{0,8},{8,0},{1,9},{9,1},{2,10},{10,2},{3,11},{11,3},{4,12},{12,4},... | collective-permute-start | bytes 1572872 | tf_op jit(solution)/shard_map/ppermute | solution.py:321
  26.3 5.1 %collective-permute-start.3 = (bf16[8,24,128]{2,1,0:T(8,128)(2,1)S(1)}, bf16[8,24,128]{2,1,0:T(8,128)(2,1)S(1)}, u32[]{:S(2)}, u32[]{:S(2)}) collective-permute-start(bf16[8,24,128]{2,1,0:T(8,128)(2,1)S(1)} %get-tuple-element.16.slots0_ref), channel_id=1, source_target_pairs={{0,144},{16,128},{128,16},{144,0},{1,145},{17,129},{129,17},{145,1... | collective-permute-start | bytes 147464 | tf_op jit(solution)/shard_map/ppermute | solution.py:318
  28.6 4.1 %collective-permute-start.2 = (bf16[8,24,128]{2,1,0:T(8,128)(2,1)S(1)}, bf16[8,24,128]{2,1,0:T(8,128)(2,1)S(1)}, u32[]{:S(2)}, u32[]{:S(2)}) collective-permute-start(bf16[8,24,128]{2,1,0:T(8,128)(2,1)S(1)} %get-tuple-element.16.slots0_ref), channel_id=1, source_target_pairs={{0,128},{16,144},{128,0},{144,16},{1,129},{17,145},{129,1},{145,17... | collective-permute-start | bytes 147464 | tf_op jit(solution)/shard_map/ppermute | solution.py:318
  29.0 4.1 %collective-permute-start.1 = (bf16[8,24,128]{2,1,0:T(8,128)(2,1)S(1)}, bf16[8,24,128]{2,1,0:T(8,128)(2,1)S(1)}, u32[]{:S(2)}, u32[]{:S(2)}) collective-permute-start(bf16[8,24,128]{2,1,0:T(8,128)(2,1)S(1)} %get-tuple-element.16.slots0_ref), channel_id=1, source_target_pairs={{0,16},{16,0},{128,144},{144,128},{1,17},{17,1},{129,145},{145,129... | collective-permute-start | bytes 147464 | tf_op jit(solution)/shard_map/ppermute | solution.py:318
  70.2 1.3 %collective-permute-start.4 = (f32[2,16,256]{2,1,0:T(8,128)S(1)}, f32[2,16,256]{2,1,0:T(8,128)S(1)}, u32[]{:S(2)}, u32[]{:S(2)}) collective-permute-start(f32[2,16,256]{2,1,0:T(8,128)S(1)} %convert_reduce_fusion.mine_ref), channel_id=1, source_target_pairs={{0,8},{8,0},{1,9},{9,1},{2,10},{10,2},{3,11},{11,3},{4,12},{12,4},... | collective-permute-start | bytes 98312 | tf_op jit(solution)/shard_map/ppermute | solution.py:326
  74.9 4.0 %collective-permute-start.5 = (bf16[8,16,128]{2,1,0:T(8,128)(2,1)S(1)}, bf16[8,16,128]{2,1,0:T(8,128)(2,1)S(1)}, u32[]{:S(2)}, u32[]{:S(2)}) collective-permute-start(bf16[8,16,128]{2,1,0:T(8,128)(2,1)S(1)} %get-tuple-element.22), channel_id=1, source_target_pairs={{0,16},{16,0},{128,144},{144,128},{1,17},{17,1},{129,145},{145,129... | collective-permute-start | bytes 98312 | tf_op jit(solution)/shard_map/ppermute | solution.py:330
  75.7 3.9 %collective-permute-start.6 = (bf16[8,16,128]{2,1,0:T(8,128)(2,1)S(1)}, bf16[8,16,128]{2,1,0:T(8,128)(2,1)S(1)}, u32[]{:S(2)}, u32[]{:S(2)}) collective-permute-start(bf16[8,16,128]{2,1,0:T(8,128)(2,1)S(1)} %get-tuple-element.23), channel_id=1, source_target_pairs={{0,128},{16,144},{128,0},{144,16},{1,129},{17,145},{129,1},{145,17... | collective-permute-start | bytes 98312 | tf_op jit(solution)/shard_map/ppermute | solution.py:330
  76.5 4.8 %collective-permute-start.7 = (bf16[8,16,128]{2,1,0:T(8,128)(2,1)S(1)}, bf16[8,16,128]{2,1,0:T(8,128)(2,1)S(1)}, u32[]{:S(2)}, u32[]{:S(2)}) collective-permute-start(bf16[8,16,128]{2,1,0:T(8,128)(2,1)S(1)} %get-tuple-element.24), channel_id=1, source_target_pairs={{0,144},{16,128},{128,16},{144,0},{1,145},{17,129},{129,17},{145,1... | collective-permute-start | bytes 98312 | tf_op jit(solution)/shard_map/ppermute | solution.py:330
